TPU v7x, 128 devices: a whole 4x4x4 slice. The times are simulated.
128 devices in a mesh: row: 8 (over z, core), col: 16 (over x, y).
Axes of the slice: x: 4, y: 4, z: 4, core: 2. Of those that a mesh axis runs over, the one named last changes fastest.
Arguments:
- adjacency: int32 [65536, 4096], P('col', 'row'), may hold values from -2147483648 to 2147483647, as said below
- frontier: bfloat16 [131072, 128], P(('row', 'col')), may hold values from 0 to 1, as said below
- visited: int32 [4, 65536], P(None, ('col', 'row')), may hold values from -2147483648 to 2147483647, as said below
Outputs:
- path_counts: float32 [65536, 128], P(('col', 'row'))
- reached_bits: int32 [4, 65536], P(None, ('col', 'row'))
Inputs may be any that keep to these rules, and one draw needn't show every extreme that they name: Bit k of adjacency[d, w] is the edge from source vertex 32 w + k to destination d; degrees and edge densities differ between vertices and between blocks of 128 by 128 vertices. `frontier`: values are zero or between 0.1 and 1. Bit k of visited[w, d] tells whether destination d was reached from root 32 w + k.
All inputs are finite; a program needn't handle non-finite values.
Results may differ from a plain program's by a relative error of at most 0.0003.
Values may be sent and summed in bfloat16 or wider, within the bound.
No kernel may reach another device: no remote copies, remote signals or barrier semaphores. Data moves between devices by JAX's collectives and lax.ppermute only.
A program may use at most 64 MiB of HBM per device.

v0:
```python
import functools
import math

import jax
import jax.numpy as jnp
from jax import lax
from jax.sharding import PartitionSpec as P


def cut_along(value, dim, devices):
    lengths = value.shape
    tiles = value.reshape(*lengths[:dim], devices, lengths[dim] // devices, *lengths[dim + 1 :])
    return jnp.moveaxis(tiles, dim, 0)


def sent_and_summed(value, axis, dim):
    devices = lax.axis_size(axis)
    tiles = lax.all_to_all(cut_along(value, dim, devices), axis, 0, 0, tiled=True)
    return jnp.sum(tiles, axis=0)


def expand_bits(packed):
    shift_table = jnp.arange(32, dtype=jnp.int32)
    bit_table = jnp.bitwise_and(jnp.right_shift(packed[:, :, None], shift_table), 1)
    return bit_table.reshape(packed.shape[0], packed.shape[1] * 32).astype(jnp.bfloat16)


def tile_product(packed, vectors):
    row_total = packed.shape[0]
    src_width = vectors.shape[0]
    row_len = math.gcd(row_total, 1024)
    block_len = math.gcd(src_width, 4096)
    block_count = src_width // block_len
    row_blocks = packed.reshape(row_total // row_len, row_len, packed.shape[1])

    def one_rows(packed_rows):
        initial = jnp.zeros((row_len, vectors.shape[1]), jnp.float32)

        def add_block(turn_index, total):
            offset = turn_index * block_len
            packed_cols = lax.dynamic_slice_in_dim(packed_rows, offset // 32, block_len // 32, 1)
            vector_rows = lax.dynamic_slice_in_dim(vectors, offset, block_len, 0)
            return total + jnp.dot(
                expand_bits(packed_cols), vector_rows, preferred_element_type=jnp.float32
            )

        return lax.fori_loop(0, block_count, add_block, initial)

    return lax.map(one_rows, row_blocks).reshape(row_total, vectors.shape[1])


def finish(reached, visited):
    row_count = reached.shape[0]
    word_count = visited.shape[0]
    shift_table = jnp.arange(32, dtype=jnp.int32)
    seen_bits = jnp.bitwise_and(jnp.right_shift(visited[:, :, None], shift_table), 1)
    seen_bits = jnp.transpose(seen_bits, (1, 0, 2)).reshape(row_count, word_count * 32)
    path_counts = jnp.where(seen_bits == 1, jnp.float32(0.0), reached)
    fresh = jnp.logical_and(seen_bits == 0, reached > 0).astype(jnp.int32)
    fresh = fresh.reshape(row_count, word_count, 32)
    added = functools.reduce(
        jnp.bitwise_or, [jnp.left_shift(fresh[:, :, position], position) for position in range(32)]
    )
    reached_bits = jnp.bitwise_or(visited, jnp.transpose(added))
    return (path_counts, reached_bits)


def shards(adjacency, frontier, visited):
    partial_sum = tile_product(adjacency, lax.all_gather(frontier, "col", axis=0, tiled=True))
    reached = sent_and_summed(partial_sum, "row", 0)
    return finish(reached, visited)


def solution(mesh):
    placed = (P("col", "row"), P(("row", "col"), None), P(None, ("col", "row")))
    return jax.shard_map(
        shards,
        mesh=mesh,
        in_specs=placed,
        out_specs=(P(("col", "row"), None), P(None, ("col", "row"))),
        check_vma=False,
    )
```

profile of v0, /device:TPU:1, one launch (start us, length us, event | category | flops | bytes accessed | tf_op | source)
XLA Modules:
  0.0 300.3 jit_solution(9416377873293730131)
XLA Ops:
  7.9 56.5 %all-gather.2.cloned.1.call-done = bf16[16384,128]{1,0:T(8,128)(2,1)} async-done(((bf16[1024,128]{1,0:T(8,128)(2,1)}), bf16[16384,128]{1,0:T(8,128)(2,1)}) %all-gather.2.cloned.1.call-update) | async-done | bytes 4194320 | tf_op jit(solution)/shard_map/all_gather | solution.py:69
  64.5 195.4 %while.36 = (s32[]{:T(128)}, f32[4,1024,128]{2,1,0:T(8,128)}, s32[4,1024,512]{2,1,0:T(8,128)}, bf16[16384,128]{1,0:T(8,128)(2,1)}, s32[]{:T(128)}, /*index=5*/s3...) while((s32[]{:T(128)}, f32[4,1024,128]{2,1,0:T(8,128)}, ...), condition=%wide.region_3.4_spmd, body=%wide.region_0.3_spmd.sunk | while | flops 1086586880 | bytes 29951060 | solution.py:49
  69.5 43.0 %while.37 = (s32[]{:T(128)}, f32[1024,128]{1,0:T(8,128)S(1)}, s32[1024,512]{0,1:T(8,128)S(1)}, bf16[16384,128]{1,0:T(8,128)(2,1)}, s32[]{:T(128)}, /*index=5*/s3...) while((s32[]{:T(128)}, f32[1024,128]{1,0:T(8,128)S(1)}, ...), condition=%wide.region_2.2_spmd.clone, body=%wide.region_1.1_spmd.clone.sunk | while | flops 1086586880 | bytes 20513124 | solution.py:47
  74.1 6.1 %convolution_add_fusion.2 = f32[1024,128]{1,0:T(8,128)S(1)} fusion(bf16[1024,4096]{0,1:T(8,128)(2,1)} %fusion.63, bf16[16384,128]{1,0:T(8,128)(2,1)} %get-tuple-element.344, s32[]{:T(128)S(6)} %select_n.46, f32[1024,128]{1,0:T(8,128)S(1)} %get-tuple-element.330, pred[]{:T(512)S(6)} %compare.13), kind=kOutput, calls=%fused_computation.3.clone.1 | convolution fusion | flops 1074003968 | bytes 10485765 | tf_op jit(solution)/shard_map/while/body/eval_jaxpr/while/body/eval_jaxpr/dot_general | solution.py:43
  84.9 6.1 %convolution_add_fusion.2 = f32[1024,128]{1,0:T(8,128)S(1)} fusion(bf16[1024,4096]{0,1:T(8,128)(2,1)} %fusion.63, bf16[16384,128]{1,0:T(8,128)(2,1)} %get-tuple-element.344, s32[]{:T(128)S(6)} %select_n.46, f32[1024,128]{1,0:T(8,128)S(1)} %get-tuple-element.330, pred[]{:T(512)S(6)} %compare.13), kind=kOutput, calls=%fused_computation.3.clone.1 | convolution fusion | flops 1074003968 | bytes 10485765 | tf_op jit(solution)/shard_map/while/body/eval_jaxpr/while/body/eval_jaxpr/dot_general | solution.py:43
  95.6 6.1 %convolution_add_fusion.2 = f32[1024,128]{1,0:T(8,128)S(1)} fusion(bf16[1024,4096]{0,1:T(8,128)(2,1)} %fusion.63, bf16[16384,128]{1,0:T(8,128)(2,1)} %get-tuple-element.344, s32[]{:T(128)S(6)} %select_n.46, f32[1024,128]{1,0:T(8,128)S(1)} %get-tuple-element.330, pred[]{:T(512)S(6)} %compare.13), kind=kOutput, calls=%fused_computation.3.clone.1 | convolution fusion | flops 1074003968 | bytes 10485765 | tf_op jit(solution)/shard_map/while/body/eval_jaxpr/while/body/eval_jaxpr/dot_general | solution.py:43
  106.4 6.1 %convolution_add_fusion.2 = f32[1024,128]{1,0:T(8,128)S(1)} fusion(bf16[1024,4096]{0,1:T(8,128)(2,1)} %fusion.63, bf16[16384,128]{1,0:T(8,128)(2,1)} %get-tuple-element.344, s32[]{:T(128)S(6)} %select_n.46, f32[1024,128]{1,0:T(8,128)S(1)} %get-tuple-element.330, pred[]{:T(512)S(6)} %compare.13), kind=kOutput, calls=%fused_computation.3.clone.1 | convolution fusion | flops 1074003968 | bytes 10485765 | tf_op jit(solution)/shard_map/while/body/eval_jaxpr/while/body/eval_jaxpr/dot_general | solution.py:43
  118.4 43.0 %while.37 = (s32[]{:T(128)}, f32[1024,128]{1,0:T(8,128)S(1)}, s32[1024,512]{0,1:T(8,128)S(1)}, bf16[16384,128]{1,0:T(8,128)(2,1)}, s32[]{:T(128)}, /*index=5*/s3...) while((s32[]{:T(128)}, f32[1024,128]{1,0:T(8,128)S(1)}, ...), condition=%wide.region_2.2_spmd.clone, body=%wide.region_1.1_spmd.clone.sunk | while | flops 1086586880 | bytes 20513124 | solution.py:47
  123.0 6.1 %convolution_add_fusion.2 = f32[1024,128]{1,0:T(8,128)S(1)} fusion(bf16[1024,4096]{0,1:T(8,128)(2,1)} %fusion.63, bf16[16384,128]{1,0:T(8,128)(2,1)} %get-tuple-element.344, s32[]{:T(128)S(6)} %select_n.46, f32[1024,128]{1,0:T(8,128)S(1)} %get-tuple-element.330, pred[]{:T(512)S(6)} %compare.13), kind=kOutput, calls=%fused_computation.3.clone.1 | convolution fusion | flops 1074003968 | bytes 10485765 | tf_op jit(solution)/shard_map/while/body/eval_jaxpr/while/body/eval_jaxpr/dot_general | solution.py:43
  133.8 6.1 %convolution_add_fusion.2 = f32[1024,128]{1,0:T(8,128)S(1)} fusion(bf16[1024,4096]{0,1:T(8,128)(2,1)} %fusion.63, bf16[16384,128]{1,0:T(8,128)(2,1)} %get-tuple-element.344, s32[]{:T(128)S(6)} %select_n.46, f32[1024,128]{1,0:T(8,128)S(1)} %get-tuple-element.330, pred[]{:T(512)S(6)} %compare.13), kind=kOutput, calls=%fused_computation.3.clone.1 | convolution fusion | flops 1074003968 | bytes 10485765 | tf_op jit(solution)/shard_map/while/body/eval_jaxpr/while/body/eval_jaxpr/dot_general | solution.py:43
  144.5 6.1 %convolution_add_fusion.2 = f32[1024,128]{1,0:T(8,128)S(1)} fusion(bf16[1024,4096]{0,1:T(8,128)(2,1)} %fusion.63, bf16[16384,128]{1,0:T(8,128)(2,1)} %get-tuple-element.344, s32[]{:T(128)S(6)} %select_n.46, f32[1024,128]{1,0:T(8,128)S(1)} %get-tuple-element.330, pred[]{:T(512)S(6)} %compare.13), kind=kOutput, calls=%fused_computation.3.clone.1 | convolution fusion | flops 1074003968 | bytes 10485765 | tf_op jit(solution)/shard_map/while/body/eval_jaxpr/while/body/eval_jaxpr/dot_general | solution.py:43
  155.2 6.1 %convolution_add_fusion.2 = f32[1024,128]{1,0:T(8,128)S(1)} fusion(bf16[1024,4096]{0,1:T(8,128)(2,1)} %fusion.63, bf16[16384,128]{1,0:T(8,128)(2,1)} %get-tuple-element.344, s32[]{:T(128)S(6)} %select_n.46, f32[1024,128]{1,0:T(8,128)S(1)} %get-tuple-element.330, pred[]{:T(512)S(6)} %compare.13), kind=kOutput, calls=%fused_computation.3.clone.1 | convolution fusion | flops 1074003968 | bytes 10485765 | tf_op jit(solution)/shard_map/while/body/eval_jaxpr/while/body/eval_jaxpr/dot_general | solution.py:43
  167.2 43.0 %while.37 = (s32[]{:T(128)}, f32[1024,128]{1,0:T(8,128)S(1)}, s32[1024,512]{0,1:T(8,128)S(1)}, bf16[16384,128]{1,0:T(8,128)(2,1)}, s32[]{:T(128)}, /*index=5*/s3...) while((s32[]{:T(128)}, f32[1024,128]{1,0:T(8,128)S(1)}, ...), condition=%wide.region_2.2_spmd.clone, body=%wide.region_1.1_spmd.clone.sunk | while | flops 1086586880 | bytes 20513124 | solution.py:47
  171.9 6.1 %convolution_add_fusion.2 = f32[1024,128]{1,0:T(8,128)S(1)} fusion(bf16[1024,4096]{0,1:T(8,128)(2,1)} %fusion.63, bf16[16384,128]{1,0:T(8,128)(2,1)} %get-tuple-element.344, s32[]{:T(128)S(6)} %select_n.46, f32[1024,128]{1,0:T(8,128)S(1)} %get-tuple-element.330, pred[]{:T(512)S(6)} %compare.13), kind=kOutput, calls=%fused_computation.3.clone.1 | convolution fusion | flops 1074003968 | bytes 10485765 | tf_op jit(solution)/shard_map/while/body/eval_jaxpr/while/body/eval_jaxpr/dot_general | solution.py:43
  182.6 6.1 %convolution_add_fusion.2 = f32[1024,128]{1,0:T(8,128)S(1)} fusion(bf16[1024,4096]{0,1:T(8,128)(2,1)} %fusion.63, bf16[16384,128]{1,0:T(8,128)(2,1)} %get-tuple-element.344, s32[]{:T(128)S(6)} %select_n.46, f32[1024,128]{1,0:T(8,128)S(1)} %get-tuple-element.330, pred[]{:T(512)S(6)} %compare.13), kind=kOutput, calls=%fused_computation.3.clone.1 | convolution fusion | flops 1074003968 | bytes 10485765 | tf_op jit(solution)/shard_map/while/body/eval_jaxpr/while/body/eval_jaxpr/dot_general | solution.py:43
  193.4 6.1 %convolution_add_fusion.2 = f32[1024,128]{1,0:T(8,128)S(1)} fusion(bf16[1024,4096]{0,1:T(8,128)(2,1)} %fusion.63, bf16[16384,128]{1,0:T(8,128)(2,1)} %get-tuple-element.344, s32[]{:T(128)S(6)} %select_n.46, f32[1024,128]{1,0:T(8,128)S(1)} %get-tuple-element.330, pred[]{:T(512)S(6)} %compare.13), kind=kOutput, calls=%fused_computation.3.clone.1 | convolution fusion | flops 1074003968 | bytes 10485765 | tf_op jit(solution)/shard_map/while/body/eval_jaxpr/while/body/eval_jaxpr/dot_general | solution.py:43
  204.1 6.1 %convolution_add_fusion.2 = f32[1024,128]{1,0:T(8,128)S(1)} fusion(bf16[1024,4096]{0,1:T(8,128)(2,1)} %fusion.63, bf16[16384,128]{1,0:T(8,128)(2,1)} %get-tuple-element.344, s32[]{:T(128)S(6)} %select_n.46, f32[1024,128]{1,0:T(8,128)S(1)} %get-tuple-element.330, pred[]{:T(512)S(6)} %compare.13), kind=kOutput, calls=%fused_computation.3.clone.1 | convolution fusion | flops 1074003968 | bytes 10485765 | tf_op jit(solution)/shard_map/while/body/eval_jaxpr/while/body/eval_jaxpr/dot_general | solution.py:43
  216.1 43.0 %while.37 = (s32[]{:T(128)}, f32[1024,128]{1,0:T(8,128)S(1)}, s32[1024,512]{0,1:T(8,128)S(1)}, bf16[16384,128]{1,0:T(8,128)(2,1)}, s32[]{:T(128)}, /*index=5*/s3...) while((s32[]{:T(128)}, f32[1024,128]{1,0:T(8,128)S(1)}, ...), condition=%wide.region_2.2_spmd.clone, body=%wide.region_1.1_spmd.clone.sunk | while | flops 1086586880 | bytes 20513124 | solution.py:47
  220.7 6.1 %convolution_add_fusion.2 = f32[1024,128]{1,0:T(8,128)S(1)} fusion(bf16[1024,4096]{0,1:T(8,128)(2,1)} %fusion.63, bf16[16384,128]{1,0:T(8,128)(2,1)} %get-tuple-element.344, s32[]{:T(128)S(6)} %select_n.46, f32[1024,128]{1,0:T(8,128)S(1)} %get-tuple-element.330, pred[]{:T(512)S(6)} %compare.13), kind=kOutput, calls=%fused_computation.3.clone.1 | convolution fusion | flops 1074003968 | bytes 10485765 | tf_op jit(solution)/shard_map/while/body/eval_jaxpr/while/body/eval_jaxpr/dot_general | solution.py:43
  231.5 6.1 %convolution_add_fusion.2 = f32[1024,128]{1,0:T(8,128)S(1)} fusion(bf16[1024,4096]{0,1:T(8,128)(2,1)} %fusion.63, bf16[16384,128]{1,0:T(8,128)(2,1)} %get-tuple-element.344, s32[]{:T(128)S(6)} %select_n.46, f32[1024,128]{1,0:T(8,128)S(1)} %get-tuple-element.330, pred[]{:T(512)S(6)} %compare.13), kind=kOutput, calls=%fused_computation.3.clone.1 | convolution fusion | flops 1074003968 | bytes 10485765 | tf_op jit(solution)/shard_map/while/body/eval_jaxpr/while/body/eval_jaxpr/dot_general | solution.py:43
  242.2 6.1 %convolution_add_fusion.2 = f32[1024,128]{1,0:T(8,128)S(1)} fusion(bf16[1024,4096]{0,1:T(8,128)(2,1)} %fusion.63, bf16[16384,128]{1,0:T(8,128)(2,1)} %get-tuple-element.344, s32[]{:T(128)S(6)} %select_n.46, f32[1024,128]{1,0:T(8,128)S(1)} %get-tuple-element.330, pred[]{:T(512)S(6)} %compare.13), kind=kOutput, calls=%fused_computation.3.clone.1 | convolution fusion | flops 1074003968 | bytes 10485765 | tf_op jit(solution)/shard_map/while/body/eval_jaxpr/while/body/eval_jaxpr/dot_general | solution.py:43
  252.9 6.1 %convolution_add_fusion.2 = f32[1024,128]{1,0:T(8,128)S(1)} fusion(bf16[1024,4096]{0,1:T(8,128)(2,1)} %fusion.63, bf16[16384,128]{1,0:T(8,128)(2,1)} %get-tuple-element.344, s32[]{:T(128)S(6)} %select_n.46, f32[1024,128]{1,0:T(8,128)S(1)} %get-tuple-element.330, pred[]{:T(512)S(6)} %compare.13), kind=kOutput, calls=%fused_computation.3.clone.1 | convolution fusion | flops 1074003968 | bytes 10485765 | tf_op jit(solution)/shard_map/while/body/eval_jaxpr/while/body/eval_jaxpr/dot_general | solution.py:43
  259.9 5.4 %all-to-all-start = ((f32[8,512,128]{2,1,0:T(8,128)}), f32[8,512,128]{2,1,0:T(8,128)S(1)}, u32[]{:S(2)}, u32[]{:S(2)}) async-start(f32[8,512,128]{2,1,0:T(8,128)} %bitcast.129), calls=%async_computation | async-start | bytes 4194304 | tf_op jit(solution)/shard_map/all_to_all | solution.py:18
  265.5 26.0 %all-to-all-done = f32[8,512,128]{2,1,0:T(8,128)S(1)} async-done(((f32[8,512,128]{2,1,0:T(8,128)}), f32[8,512,128]{2,1,0:T(8,128)S(1)}, u32[]{:S(2)}, u32[]{:S(2)}) %all-to-all-start) | async-done | bytes 2097184 | tf_op jit(solution)/shard_map/all_to_all | solution.py:18
  (97 shorter events, 99.7 us)
Async XLA Ops:
  7.2 57.3 %all-gather.2.cloned.1.call-start = ((), (), s32[]{:S(2)}) async-start(), calls=%async_computation.1 | async-start | bytes 4456448 | tf_op jit(solution)/shard_map/all_gather | solution.py:69
  259.9 5.4 %copy-start = (s32[4,512]{1,0:T(4,128)S(1)}, s32[4,512]{1,0:T(4,128)}, u32[]{:S(2)}) copy-start(s32[4,512]{1,0:T(4,128)} %param.9) | copy-start | bytes 24580
  259.9 31.6 %all-to-all-start = ((f32[8,512,128]{2,1,0:T(8,128)}), f32[8,512,128]{2,1,0:T(8,128)S(1)}, u32[]{:S(2)}, u32[]{:S(2)}) async-start(f32[8,512,128]{2,1,0:T(8,128)} %bitcast.129), calls=%async_computation | async-start | bytes 4194304 | tf_op jit(solution)/shard_map/all_to_all | solution.py:18
Sparse Core Ops, SparseCore 0:
  10.1 54.2 all-gather.1
where the time goes:
time: 301 us; the launch traced here: 300 us
  matrix products  97.5 us (32%)
  waiting for transfers between devices  83.2 us (28%)
  other arithmetic  72.7 us (24%)
  local copies, waits for them, and re-layouts  26.2 us (9%)
  between operations  14.1 us (5%)
  starting transfers between devices  5.43 us (2%)
    dot_general x16, matrix products, add_block(): jnp.dot(expand_bits(packed_cols), vector_rows, preferred_element_type=jnp...  97.5 us
    convert_element_type x16, other arithmetic, expand_bits(): bit_table.reshape(packed.shape[0], packed.shape[1] * 32)  71 us
    all_gather x1, waiting for transfers between devices, shards(): lax.all_gather(frontier, 'col', axis=0, tiled=True)  56.5 us
    all_to_all x1, waiting for transfers between devices, sent_and_summed(): lax.all_to_all(cut_along(value, dim, devices), axis, 0, 0, tiled=True)  26 us
    dynamic_slice x8, local copies, waits for them, and re-layouts, tile_product(): return lax.map(one_rows, row_blocks).reshape(row_total, vectors.shape[1])  20.1 us
  transfers between devices with their start and end apart: 2, of which 2 were waited for; matrix products, arithmetic and copies ran while one was open for 0% of the time, Pallas kernels for 0%

commit v1 on v0

v1 whole, which is shorter than its diff:
```python
import functools

import jax
import jax.numpy as jnp
import numpy as np
from jax import lax
from jax.experimental import pallas as pl
from jax.experimental.pallas import tpu as pltpu
from jax.sharding import PartitionSpec as P

SIDE = 4
TILE = 256
CHUNK = 1024
TILES = CHUNK // TILE
BITS = 8

VM = pltpu.VMEM
FULL = pl.BlockSpec(memory_space=VM)
SCAL = pl.BlockSpec(memory_space=pltpu.SMEM)

AXES = ("row", "col")


def place(x, y, z, core):
    return (z * 2 + core) * (SIDE * SIDE) + x * SIDE + y


def pairs(axis, flip=False):
    out = []
    for x in range(SIDE):
        for y in range(SIDE):
            for z in range(SIDE):
                for core in range(2):
                    at = [x, y, z]
                    if axis == "core":
                        out.append((place(*at, core), place(*at, 1 - core)))
                        continue
                    n = "xyz".index(axis)
                    step = 1 if (core == 0) != flip else -1
                    to = list(at)
                    to[n] = (to[n] + step) % SIDE
                    out.append((place(*at, core), place(*to, core)))
    return out


def send(value, axis, flip=False):
    return lax.ppermute(value, AXES, pairs(axis, flip))


def swap(value):
    return lax.ppermute(value, AXES, pairs("core"))


def prep_kernel(f_ref, o_ref, s_ref):
    s_ref[...] = f_ref[...].astype(jnp.float32)
    for j in range(TILES):
        rows = []
        for b in range(BITS):
            scale = 2.0**-b if b < 7 else -(2.0**-7)
            rows.append(s_ref[pl.ds(8 * j + b, 32, stride=32), :] * scale)
        o_ref[j] = jnp.concatenate(rows, 0).T.astype(jnp.bfloat16)


def prep(f):
    return pl.pallas_call(
        prep_kernel,
        out_shape=VM((TILES, 128, TILE), jnp.bfloat16),
        in_specs=[FULL],
        out_specs=FULL,
        scratch_shapes=[pltpu.VMEM((CHUNK, 128), jnp.float32)],
        name="prep",
    )(f)


def split_kernel(a_ref, o_ref):
    k = pl.program_id(0)
    i = pl.program_id(1)
    a = a_ref[...]
    for j in range(4):
        part = (lax.shift_right_logical(a, 8 * j) if j else a).astype(jnp.int8).T
        for h in range(2):
            for c in range(4):
                o_ref[2 * k + h, 16 * i + 4 * c + j] = part[32 * c : 32 * c + 32, 512 * h : 512 * h + 512]


def split(adj):
    d, w = adj.shape
    return pl.pallas_call(
        split_kernel,
        grid=(d // 1024, w // 128),
        in_specs=[pl.BlockSpec((1024, 128), lambda k, i: (k, i))],
        out_specs=FULL,
        out_shape=VM((d // 512, w // 8, 32, 512), jnp.int8),
        compiler_params=pltpu.CompilerParams(vmem_limit_bytes=24 << 20),
        name="split",
    )(adj)


def expand(a_ref, r, tiles, at):
    parts = []
    for t in range(tiles):
        x = a_ref[r, at(t)]
        for b in range(BITS):
            m = 1 << b if b < 7 else -128
            parts.append((x & jnp.int8(m)).astype(jnp.bfloat16))
    return jnp.concatenate(parts, 0)


def mm_kernel(*refs, first, group, picks, whole, acc_in):
    idx_ref, a_ref = refs[0], refs[1]
    refs = refs[2:]
    if acc_in:
        acc_ref, refs = refs[0], refs[1:]
    srcs = sorted({p[0] for p in picks})
    f_refs, rest = refs[: len(srcs)], refs[len(srcs) :]
    outs, scr = rest[:-1], rest[-1]
    for t, (n, k) in enumerate(picks):
        scr[t] = f_refs[n][k]
    steps = len(picks) // group

    def step(i, carry):
        base = i * group if steps > 1 else 0
        f = jnp.concatenate([scr[base + t] for t in range(group)], 1)
        at = lambda t: idx_ref[first + base + t]
        if whole:
            out = outs[0]
            for r in range(8):
                got = jnp.dot(f, expand(a_ref, r, group, at), preferred_element_type=jnp.float32)
                out[r] = out[r] + got
        else:
            for n in range(2):
                r = idx_ref[64 + whole_off[0] + n]
                got = jnp.dot(f, expand(a_ref, r, group, at), preferred_element_type=jnp.float32)
                if steps > 1:
                    outs[n][...] += got
                else:
                    outs[n][...] = got + acc_ref[r]
        return carry

    whole_off = (0,)
    if not isinstance(whole, bool):
        whole_off, whole = (whole,), False
    if whole:
        if acc_in:
            outs[0][...] = acc_ref[...]
        else:
            outs[0][...] = jnp.zeros_like(outs[0])
    elif steps > 1:
        for n in range(2):
            outs[n][...] = acc_ref[idx_ref[64 + whole_off[0] + n]]
    if steps > 1:
        lax.fori_loop(0, steps, step, 0)
    else:
        step(0, 0)


def mm(idx, ab, acc, arrays, picks, first, group, whole=True):
    tiles = len(picks)
    if whole is True:
        out_shape = VM((8, 128, 512), jnp.float32)
        out_specs = FULL
        lanes = 4096
    else:
        out_shape = (VM((128, 512), jnp.float32),) * 2
        out_specs = (FULL, FULL)
        lanes = 1024
    args = [idx, ab] + ([acc] if acc is not None else []) + list(arrays)
    alias = {2: 0} if whole is True and acc is not None else {}
    return pl.pallas_call(
        functools.partial(mm_kernel, first=first, group=group, picks=tuple(picks), whole=whole, acc_in=acc is not None),
        out_shape=out_shape,
        in_specs=[SCAL] + [FULL] * (len(args) - 1),
        out_specs=out_specs,
        scratch_shapes=[pltpu.VMEM((tiles, 128, TILE), jnp.bfloat16)],
        input_output_aliases=alias,
        cost_estimate=pl.CostEstimate(flops=2 * 128 * TILE * tiles * lanes, bytes_accessed=0, transcendentals=0),
        compiler_params=pltpu.CompilerParams(vmem_limit_bytes=32 << 20),
        name="bits_mm",
    )(*args)


def finish_kernel(a_ref, b_ref, c_ref, d_ref, v_ref, p_ref, o_ref):
    reached = a_ref[...] + b_ref[...] + c_ref[...] + d_ref[...]
    shift = lax.broadcasted_iota(jnp.int32, (32, 1), 0)
    rows = []
    words = []
    for w in range(4):
        got = reached[32 * w : 32 * w + 32]
        word = v_ref[w : w + 1]
        unseen = (lax.shift_right_arithmetic(jnp.broadcast_to(word, got.shape), jnp.broadcast_to(shift, got.shape)) & 1) == 0
        rows.append(jnp.where(unseen, got, 0.0))
        fresh = jnp.where(unseen & (got > 0), lax.shift_left(jnp.int32(1), jnp.broadcast_to(shift, got.shape)), 0)
        words.append(word | jnp.sum(fresh, 0, keepdims=True))
    p_ref[...] = jnp.concatenate(rows, 0).T
    o_ref[...] = jnp.concatenate(words, 0)


def finish(parts, visited):
    return pl.pallas_call(
        finish_kernel,
        out_shape=(jax.ShapeDtypeStruct((512, 128), jnp.float32), jax.ShapeDtypeStruct((4, 512), jnp.int32)),
        in_specs=[FULL] * 5,
        out_specs=(FULL, FULL),
        name="finish",
    )(*parts, visited)


O, M, Q, T = (0, 0), (-1, 0), (1, 0), (0, 1)


def shards(adjacency, frontier, visited):
    row, col = lax.axis_index("row"), lax.axis_index("col")
    x, y, z, core = col // SIDE, col % SIDE, row // 2, row % 2
    s = 1 - 2 * core

    lists = []

    def tiles(array, start, dx, dy, js):
        return [(array, start + n, dx, dy, j) for n, j in enumerate(js)]

    H0, H1, ALL = (0, 1), (2, 3), (0, 1, 2, 3)
    ph0 = tiles(0, 0, O, O, ALL)
    ph1 = tiles(0, 0, M, O, ALL) + tiles(1, 4, Q, O, ALL) + tiles(2, 0, O, M, ALL) + tiles(3, 4, O, Q, ALL)
    ph2 = (
        tiles(0, 0, T, O, ALL)
        + tiles(1, 0, O, T, ALL)
        + tiles(2, 0, M, M, H1)
        + tiles(2, 2, M, Q, H1)
        + tiles(3, 0, Q, Q, H1)
        + tiles(3, 2, Q, M, H1)
        + tiles(4, 0, M, M, H0)
        + tiles(4, 2, Q, M, H0)
        + tiles(5, 0, Q, Q, H0)
        + tiles(5, 2, M, Q, H0)
    )
    ph3 = (
        tiles(0, 0, M, T, H1)
        + tiles(1, 0, Q, T, H1)
        + tiles(0, 4, T, M, H1)
        + tiles(0, 6, T, Q, H1)
        + tiles(2, 0, T, M, H0)
        + tiles(3, 0, T, Q, H0)
        + tiles(2, 4, M, T, H0)
        + tiles(2, 6, Q, T, H0)
        + tiles(4, 0, T, T, H1)
        + tiles(5, 0, T, T, H0)
    )
    every = ph0 + ph1 + ph2 + ph3
    tab = np.array([(t[2][0], 2 * t[2][1], t[3][0], 2 * t[3][1], t[4]) for t in every], np.int32).T
    xs = (x + s * tab[0] + tab[1] + 8) % SIDE
    ys = (y + s * tab[2] + tab[3] + 8) % SIDE
    where = (xs * SIDE + ys) * TILES + tab[4]
    zs = (z + np.array([2, 2, 0, 0, 0, 0, 0, 0]) + s * np.array([0, 0, 1, -1, -1, 1, 0, 0]) + 8) % SIDE
    blocks = zs * 2 + (core + np.array([0, 1] * 4)) % 2
    idx = jnp.concatenate([where, blocks]).astype(jnp.int32)
    pick = lambda ph: [(t[0], t[1]) for t in ph]

    ft = prep(frontier)
    mine = jnp.concatenate([ft, swap(ft)], 0)
    dx = send(mine, "x")
    dy = send(mine, "y")
    ab = split(adjacency)
    acc = mm(idx, ab, None, [ft], pick(ph0), 0, 4)
    px, py = swap(dx), swap(dy)
    bx = send(dx[:4], "x")
    by = send(dy[:4], "y")
    cx = send(jnp.concatenate([dy[2:4], py[6:8], dy[6:8], py[2:4]], 0), "x")
    cy = send(jnp.concatenate([dx[0:2], px[4:6], dx[4:6], px[0:2]], 0), "y")
    acc = mm(idx, ab, acc, [dx, px, dy, py], pick(ph1), 4, 4)
    pbx, pby = swap(bx[0:2]), swap(by[2:4])
    pcx, pcy = swap(cx[4:8]), swap(cy[4:8])
    ex = send(jnp.concatenate([by[2:4], pby, cx[:4]], 0), "x")
    ey = send(jnp.concatenate([bx[0:2], pbx, cy[:4]], 0), "y")
    acc = mm(idx, ab, acc, [bx, by, cx, pcx, cy, pcy], pick(ph2), 20, 4)
    pex, pey = swap(ex[2:4]), swap(ey[2:4])
    gx, gy = send(ex[:2], "x"), send(ey[:2], "y")
    last = [ex, pex, ey, pey, gx, gy]
    two = mm(idx, ab, acc, last, pick(ph3), 44, 10, 0)
    near = mm(idx, ab, acc, last, pick(ph3), 44, 10, 2)
    back = mm(idx, ab, acc, last, pick(ph3), 44, 10, 4)
    own = mm(idx, ab, acc, last, pick(ph3), 44, 10, 6)
    got2 = send(two[0] + swap(two[1]), "z")
    got1 = send(near[0] + swap(near[1]) + got2, "z")
    got0 = send(back[0] + swap(back[1]), "z", True)
    return finish([own[0], swap(own[1]), got1, got0], visited)


def solution(mesh):
    placed = (P("col", "row"), P(("row", "col"), None), P(None, ("col", "row")))
    return jax.shard_map(
        shards,
        mesh=mesh,
        in_specs=placed,
        out_specs=(P(("col", "row"), None), P(None, ("col", "row"))),
        check_vma=False,
    )
```

time: 301 us -> 84.5 us (0.28)
  matrix products: 97.5 us -> 0 us
  waiting for transfers between devices: 83.2 us -> 10.4 us
  other arithmetic: 72.7 us -> 1.94 us
  Pallas kernels: 0 us -> 33.7 us
  starting transfers between devices: 5.43 us -> 32.4 us
  local copies, waits for them, and re-layouts: 26.2 us -> 4.86 us
  between operations: 14.1 us -> 0.96 us
    dot_general x16 -> x0, matrix products: 97.5 us -> none  [add_block(): jnp.dot(expand_bits(packed_cols), vector_rows, preferred_element_type=jnp...]
    convert_element_type x17 -> x0, other arithmetic: 71 us -> none  [the longest x16 71 us: expand_bits(): bit_table.reshape(packed.shape[0], packed.shape[1] * 32)]
    all_gather x1 -> x0, waiting for transfers between devices: 56.5 us -> none  [shards(): lax.all_gather(frontier, 'col', axis=0, tiled=True)]
    pallas_call x0 -> x10, Pallas kernels: none -> 33.7 us  [the longest x7 25.8 us: mm(): pl.pallas_call(functools.partial(mm_kernel, first=first, group=group, pic...]
    ppermute x0 -> x26, starting transfers between devices: none -> 32.4 us  [the longest x13 25.8 us: send(): return lax.ppermute(value, AXES, pairs(axis, flip))]
    all_to_all x1 -> x0, waiting for transfers between devices: 26 us -> none  [sent_and_summed(): lax.all_to_all(cut_along(value, dim, devices), axis, 0, 0, tiled=True)]
    dynamic_slice x24 -> x0, local copies, waits for them, and re-layouts: 21 us -> none  [the longest x8 20.1 us: tile_product(): return lax.map(one_rows, row_blocks).reshape(row_total, vectors.shape[1])]
    ppermute x0 -> x26, waiting for transfers between devices: none -> 10.4 us  [the longest x13 8.25 us: send(): return lax.ppermute(value, AXES, pairs(axis, flip))]
  transfers between devices with their start and end apart: 2 -> 26, of which waited for: 2 -> 7; matrix products, arithmetic and copies ran while one was open for 0% -> 3% of each run, Pallas kernels for 0% -> 33%
where the time goes in v1:
time: 84.5 us; the launch traced here: 84.3 us
  Pallas kernels  33.7 us (40%)
  starting transfers between devices  32.4 us (38%)
  waiting for transfers between devices  10.4 us (12%)
  local copies, waits for them, and re-layouts  4.86 us (6%)
  other arithmetic  1.94 us (2%)
  between operations  0.96 us (1%)
    ppermute x13, starting transfers between devices, send(): return lax.ppermute(value, AXES, pairs(axis, flip))  25.8 us
    pallas_call x7, Pallas kernels, mm(): pl.pallas_call(functools.partial(mm_kernel, first=first, group=group, pic...  25.8 us
    ppermute x13, waiting for transfers between devices, send(): return lax.ppermute(value, AXES, pairs(axis, flip))  8.25 us
    ppermute x13, starting transfers between devices, swap(): return lax.ppermute(value, AXES, pairs('core'))  6.54 us
    unnamed x10, local copies, waits for them, and re-layouts  4.63 us
    pallas_call x1, Pallas kernels, split(): pl.pallas_call(split_kernel, grid=(d // 1024, w // 128), in_specs=[pl.Blo...  4.53 us
    ppermute x13, waiting for transfers between devices, swap(): return lax.ppermute(value, AXES, pairs('core'))  2.17 us
    pallas_call x1, Pallas kernels, finish(): pl.pallas_call(finish_kernel, out_shape=(jax.ShapeDtypeStruct((512, 128),...  2.07 us
  transfers between devices with their start and end apart: 26, of which 7 were waited for; matrix products, arithmetic and copies ran while one was open for 3% of the time, Pallas kernels for 33%

profile of v1, /device:TPU:1, one launch (start us, length us, event | category | flops | bytes accessed | tf_op | source)
XLA Modules:
  0.0 84.3 jit_solution(901997539336952597)
XLA Ops:
  2.0 1.5 %collective-permute-start = (bf16[4,128,256]{2,1,0:T(8,128)(2,1)S(1)}, bf16[4,128,256]{2,1,0:T(8,128)(2,1)S(1)}, u32[]{:S(2)}, u32[]{:S(2)}) collective-permute-start(bf16[4,128,256]{2,1,0:T(8,128)(2,1)S(1)} %prep.1.refs_2_), channel_id=1, source_target_pairs={{0,16},{16,0},{32,48},{48,32},{64,80},{80,64},{96,112},{112,96},{1... | collective-permute-start | bytes 786440 | tf_op jit(solution)/shard_map/ppermute | solution.py:51
  4.7 2.9 %collective-permute-start.3 = (bf16[8,128,256]{2,1,0:T(8,128)(2,1)S(1)}, bf16[8,128,256]{2,1,0:T(8,128)(2,1)S(1)}, u32[]{:S(2)}, u32[]{:S(2)}) collective-permute-start(bf16[8,128,256]{2,1,0:T(8,128)(2,1)S(1)} %pad_maximum_fusion), channel_id=1, source_target_pairs={{0,1},{16,19},{32,33},{48,51},{64,65},{80,83},{96,97},{112,115},{1... | collective-permute-start | bytes 1572872 | tf_op jit(solution)/shard_map/ppermute | solution.py:47
  7.6 2.5 %collective-permute-start.1 = (bf16[8,128,256]{2,1,0:T(8,128)(2,1)S(1)}, bf16[8,128,256]{2,1,0:T(8,128)(2,1)S(1)}, u32[]{:S(2)}, u32[]{:S(2)}) collective-permute-start(bf16[8,128,256]{2,1,0:T(8,128)(2,1)S(1)} %pad_maximum_fusion), channel_id=1, source_target_pairs={{0,4},{16,28},{32,36},{48,60},{64,68},{80,92},{96,100},{112,124},{... | collective-permute-start | bytes 1572872 | tf_op jit(solution)/shard_map/ppermute | solution.py:47
  10.8 2.9 %collective-permute-done.3.refs_5_ = bf16[8,128,256]{2,1,0:T(8,128)(2,1)S(1)} collective-permute-done((bf16[8,128,256]{2,1,0:T(8,128)(2,1)S(1)}, bf16[8,128,256]{2,1,0:T(8,128)(2,1)S(1)}, u32[]{:S(2)}, u32[]{:S(2)}) %collective-permute-start.3) | collective-permute-done | bytes 524320 | tf_op jit(solution)/shard_map/ppermute | solution.py:47
  13.7 1.8 %collective-permute-start.4 = (bf16[8,128,256]{2,1,0:T(8,128)(2,1)S(1)}, bf16[8,128,256]{2,1,0:T(8,128)(2,1)S(1)}, u32[]{:S(2)}, u32[]{:S(2)}) collective-permute-start(bf16[8,128,256]{2,1,0:T(8,128)(2,1)S(1)} %collective-permute-done.3.refs_5_), channel_id=1, source_target_pairs={{0,16},{16,0},{32,48},{48,32},{64,80},{80,64},{96,112},{112,96},{1... | collective-permute-start | bytes 1572872 | tf_op jit(solution)/shard_map/ppermute | solution.py:51
  16.2 3.2 %collective-permute-start.5 = (bf16[4,128,256]{2,1,0:T(8,128)(2,1)S(1)}, bf16[4,128,256]{2,1,0:T(8,128)(2,1)S(1)}, u32[]{:S(2)}, u32[]{:S(2)}) collective-permute-start(bf16[4,128,256]{2,1,0:T(8,128)(2,1)S(1)} %slice.82), channel_id=1, source_target_pairs={{0,4},{16,28},{32,36},{48,60},{64,68},{80,92},{96,100},{112,124},{... | collective-permute-start | bytes 786440 | tf_op jit(solution)/shard_map/ppermute | solution.py:47
  20.7 1.5 %collective-permute-start.7 = (bf16[8,128,256]{2,1,0:T(8,128)(2,1)S(1)}, bf16[8,128,256]{2,1,0:T(8,128)(2,1)S(1)}, u32[]{:S(2)}, u32[]{:S(2)}) collective-permute-start(bf16[8,128,256]{2,1,0:T(8,128)(2,1)S(1)} %pad_maximum_fusion.1), channel_id=1, source_target_pairs={{0,4},{16,28},{32,36},{48,60},{64,68},{80,92},{96,100},{112,124},{... | collective-permute-start | bytes 1572872 | tf_op jit(solution)/shard_map/ppermute | solution.py:47
  23.8 3.4 %copy-done = s32[4096,512]{1,0:T(8,128)S(1)} copy-done((s32[4096,512]{1,0:T(8,128)S(1)}, s32[4096,512]{1,0:T(8,128)}, u32[]{:S(2)}) %copy-start) | copy-done | bytes 8388632
  27.1 4.5 %split.1.refs_1_ = s8[8,64,32,512]{3,2,1,0:T(32,128)(4,1)S(1)} custom-call(s32[4096,512]{1,0:T(8,128)S(1)} %copy-done), custom_call_target="tpu_custom_call" | custom-call | tf_op jit(solution)/shard_map/split/pallas_call | solution.py:88
  31.7 1.8 %bits_mm.7.refs_2_ = f32[8,128,512]{2,1,0:T(8,128)S(1)} custom-call(s32[72]{0:T(128)S(1)} %pad_add_fusion.refs_0_, s8[8,64,32,512]{3,2,1,0:T(32,128)(4,1)S(1)} %split.1.refs_1_, bf16[4,128,256]{2,1,0:T(8,128)(2,1)S(1)} %prep.1.refs_2_), custom_call_target="tpu_custom_call" | custom-call | flops 1073741824 | tf_op jit(solution)/shard_map/bits_mm/pallas_call | solution.py:169
  35.0 1.4 %collective-permute-start.12 = (bf16[8,128,256]{2,1,0:T(8,128)(2,1)S(1)}, bf16[8,128,256]{2,1,0:T(8,128)(2,1)S(1)}, u32[]{:S(2)}, u32[]{:S(2)}) collective-permute-start(bf16[8,128,256]{2,1,0:T(8,128)(2,1)S(1)} %pad_maximum_fusion.3), channel_id=1, source_target_pairs={{0,4},{16,28},{32,36},{48,60},{64,68},{80,92},{96,100},{112,124},{... | collective-permute-start | bytes 1572872 | tf_op jit(solution)/shard_map/ppermute | solution.py:47
  36.5 2.1 %collective-permute-start.15 = (bf16[8,128,256]{2,1,0:T(8,128)(2,1)S(1)}, bf16[8,128,256]{2,1,0:T(8,128)(2,1)S(1)}, u32[]{:S(2)}, u32[]{:S(2)}) collective-permute-start(bf16[8,128,256]{2,1,0:T(8,128)(2,1)S(1)} %pad_maximum_fusion.4), channel_id=1, source_target_pairs={{0,1},{16,19},{32,33},{48,51},{64,65},{80,83},{96,97},{112,115},{1... | collective-permute-start | bytes 1572872 | tf_op jit(solution)/shard_map/ppermute | solution.py:47
  38.5 6.0 %bits_mm.8.refs_2_ = f32[8,128,512]{2,1,0:T(8,128)S(1)} custom-call(s32[72]{0:T(128)S(1)} %pad_add_fusion.refs_0_, s8[8,64,32,512]{3,2,1,0:T(32,128)(4,1)S(1)} %split.1.refs_1_, f32[8,128,512]{2,1,0:T(8,128)S(1)} %bits_mm.7.refs_2_, bf16[8,128,256]{2,1,0:T(8,128)(2,1)S(1)} %collective-permute-done.1.refs_3_, ...), custom_call_target="tpu_custom_call", output_to_operand_aliasing={{}: (2, {})} | custom-call | flops 4294967296 | tf_op jit(solution)/shard_map/bits_mm/pallas_call | solution.py:169
  46.4 2.5 %collective-permute-start.17 = (bf16[2,128,256]{2,1,0:T(8,128)(2,1)S(1)}, bf16[2,128,256]{2,1,0:T(8,128)(2,1)S(1)}, u32[]{:S(2)}, u32[]{:S(2)}) collective-permute-start(bf16[2,128,256]{2,1,0:T(8,128)(2,1)S(1)} %get-tuple-element.20), channel_id=1, source_target_pairs={{0,4},{16,28},{32,36},{48,60},{64,68},{80,92},{96,100},{112,124},{... | collective-permute-start | bytes 393224 | tf_op jit(solution)/shard_map/ppermute | solution.py:47
  49.5 8.5 %bits_mm.9.refs_2_ = f32[8,128,512]{2,1,0:T(8,128)S(1)} custom-call(s32[72]{0:T(128)S(1)} %pad_add_fusion.refs_0_, s8[8,64,32,512]{3,2,1,0:T(32,128)(4,1)S(1)} %split.1.refs_1_, f32[8,128,512]{2,1,0:T(8,128)S(1)} %bits_mm.8.refs_2_, bf16[4,128,256]{2,1,0:T(8,128)(2,1)S(1)} %collective-permute-done.5.refs_3_, ...), custom_call_target="tpu_custom_call", output_to_operand_aliasing={{}: (2, {})} | custom-call | flops 6442450944 | tf_op jit(solution)/shard_map/bits_mm/pallas_call | solution.py:169
  58.1 2.4 %bits_mm.12 = (f32[128,512]{1,0:T(8,128)S(1)}, f32[128,512]{1,0:T(8,128)S(1)}) custom-call(s32[72]{0:T(128)S(1)} %pad_add_fusion.refs_0_, s8[8,64,32,512]{3,2,1,0:T(32,128)(4,1)S(1)} %split.1.refs_1_, f32[8,128,512]{2,1,0:T(8,128)S(1)} %bits_mm.9.refs_2_, bf16[8,128,256]{2,1,0:T(8,128)(2,1)S(1)} %collective-permute-done.12.refs_3_, ...), custom_call_target="tpu_custom_call" | custom-call | flops 1342177280 | tf_op jit(solution)/shard_map/bits_mm/pallas_call | solution.py:169
  60.6 2.4 %bits_mm.13 = (f32[128,512]{1,0:T(8,128)S(1)}, f32[128,512]{1,0:T(8,128)S(1)}) custom-call(s32[72]{0:T(128)S(1)} %pad_add_fusion.refs_0_, s8[8,64,32,512]{3,2,1,0:T(32,128)(4,1)S(1)} %split.1.refs_1_, f32[8,128,512]{2,1,0:T(8,128)S(1)} %bits_mm.9.refs_2_, bf16[8,128,256]{2,1,0:T(8,128)(2,1)S(1)} %collective-permute-done.12.refs_3_, ...), custom_call_target="tpu_custom_call" | custom-call | flops 1342177280 | tf_op jit(solution)/shard_map/bits_mm/pallas_call | solution.py:169
  63.5 2.4 %bits_mm.11 = (f32[128,512]{1,0:T(8,128)S(1)}, f32[128,512]{1,0:T(8,128)S(1)}) custom-call(s32[72]{0:T(128)S(1)} %pad_add_fusion.refs_0_, s8[8,64,32,512]{3,2,1,0:T(32,128)(4,1)S(1)} %split.1.refs_1_, f32[8,128,512]{2,1,0:T(8,128)S(1)} %bits_mm.9.refs_2_, bf16[8,128,256]{2,1,0:T(8,128)(2,1)S(1)} %collective-permute-done.12.refs_3_, ...), custom_call_target="tpu_custom_call" | custom-call | flops 1342177280 | tf_op jit(solution)/shard_map/bits_mm/pallas_call | solution.py:169
  66.1 3.8 %collective-permute-start.22 = (f32[128,512]{1,0:T(8,128)S(1)}, f32[128,512]{1,0:T(8,128)S(1)}, u32[]{:S(2)}, u32[]{:S(2)}) collective-permute-start(f32[128,512]{1,0:T(8,128)S(1)} %add.116), channel_id=1, source_target_pairs={{0,32},{16,112},{32,64},{48,16},{64,96},{80,48},{96,0},{112,80},{1... | collective-permute-start | bytes 786440 | tf_op jit(solution)/shard_map/ppermute | solution.py:47
  69.9 2.4 %bits_mm.10 = (f32[128,512]{1,0:T(8,128)S(1)}, f32[128,512]{1,0:T(8,128)S(1)}) custom-call(s32[72]{0:T(128)S(1)} %pad_add_fusion.refs_0_, s8[8,64,32,512]{3,2,1,0:T(32,128)(4,1)S(1)} %split.1.refs_1_, f32[8,128,512]{2,1,0:T(8,128)S(1)} %bits_mm.9.refs_2_, bf16[8,128,256]{2,1,0:T(8,128)(2,1)S(1)} %collective-permute-done.12.refs_3_, ...), custom_call_target="tpu_custom_call" | custom-call | flops 1342177280 | tf_op jit(solution)/shard_map/bits_mm/pallas_call | solution.py:169
  73.3 3.2 %collective-permute-start.23 = (f32[128,512]{1,0:T(8,128)S(1)}, f32[128,512]{1,0:T(8,128)S(1)}, u32[]{:S(2)}, u32[]{:S(2)}) collective-permute-start(f32[128,512]{1,0:T(8,128)S(1)} %add_add_fusion), channel_id=1, source_target_pairs={{0,32},{16,112},{32,64},{48,16},{64,96},{80,48},{96,0},{112,80},{1... | collective-permute-start | bytes 786440 | tf_op jit(solution)/shard_map/ppermute | solution.py:47
  76.4 3.4 %collective-permute-done.25.d_ref = f32[128,512]{1,0:T(8,128)S(1)} collective-permute-done((f32[128,512]{1,0:T(8,128)S(1)}, f32[128,512]{1,0:T(8,128)S(1)}, u32[]{:S(2)}, u32[]{:S(2)}) %collective-permute-start.25) | collective-permute-done | bytes 262176 | tf_op jit(solution)/shard_map/ppermute | solution.py:47
  79.9 1.7 %collective-permute-done.23.c_ref = f32[128,512]{1,0:T(8,128)S(1)} collective-permute-done((f32[128,512]{1,0:T(8,128)S(1)}, f32[128,512]{1,0:T(8,128)S(1)}, u32[]{:S(2)}, u32[]{:S(2)}) %collective-permute-start.23) | collective-permute-done | bytes 262176 | tf_op jit(solution)/shard_map/ppermute | solution.py:47
  82.2 2.1 %finish.1 = (f32[512,128]{1,0:T(8,128)}, s32[4,512]{1,0:T(4,128)}) custom-call(f32[128,512]{1,0:T(8,128)} %copy-done.1, f32[128,512]{1,0:T(8,128)} %copy-done.2, f32[128,512]{1,0:T(8,128)} %copy-done.4, f32[128,512]{1,0:T(8,128)} %copy-done.3, s32[4,512]{1,0:T(4,128)} %v_ref.1), custom_call_target="tpu_custom_call" | custom-call | tf_op jit(solution)/shard_map/finish/pallas_call | solution.py:199
  (71 shorter events, 13.4 us)
Async XLA Ops:
  2.0 2.6 %collective-permute-start = (bf16[4,128,256]{2,1,0:T(8,128)(2,1)S(1)}, bf16[4,128,256]{2,1,0:T(8,128)(2,1)S(1)}, u32[]{:S(2)}, u32[]{:S(2)}) collective-permute-start(bf16[4,128,256]{2,1,0:T(8,128)(2,1)S(1)} %prep.1.refs_2_), channel_id=1, source_target_pairs={{0,16},{16,0},{32,48},{48,32},{64,80},{80,64},{96,112},{112,96},{1... | collective-permute-start | bytes 786440 | tf_op jit(solution)/shard_map/ppermute | solution.py:51
  4.7 9.0 %collective-permute-start.3 = (bf16[8,128,256]{2,1,0:T(8,128)(2,1)S(1)}, bf16[8,128,256]{2,1,0:T(8,128)(2,1)S(1)}, u32[]{:S(2)}, u32[]{:S(2)}) collective-permute-start(bf16[8,128,256]{2,1,0:T(8,128)(2,1)S(1)} %pad_maximum_fusion), channel_id=1, source_target_pairs={{0,1},{16,19},{32,33},{48,51},{64,65},{80,83},{96,97},{112,115},{1... | collective-permute-start | bytes 1572872 | tf_op jit(solution)/shard_map/ppermute | solution.py:47
  7.6 8.6 %collective-permute-start.1 = (bf16[8,128,256]{2,1,0:T(8,128)(2,1)S(1)}, bf16[8,128,256]{2,1,0:T(8,128)(2,1)S(1)}, u32[]{:S(2)}, u32[]{:S(2)}) collective-permute-start(bf16[8,128,256]{2,1,0:T(8,128)(2,1)S(1)} %pad_maximum_fusion), channel_id=1, source_target_pairs={{0,4},{16,28},{32,36},{48,60},{64,68},{80,92},{96,100},{112,124},{... | collective-permute-start | bytes 1572872 | tf_op jit(solution)/shard_map/ppermute | solution.py:47
  13.7 6.9 %collective-permute-start.4 = (bf16[8,128,256]{2,1,0:T(8,128)(2,1)S(1)}, bf16[8,128,256]{2,1,0:T(8,128)(2,1)S(1)}, u32[]{:S(2)}, u32[]{:S(2)}) collective-permute-start(bf16[8,128,256]{2,1,0:T(8,128)(2,1)S(1)} %collective-permute-done.3.refs_5_), channel_id=1, source_target_pairs={{0,16},{16,0},{32,48},{48,32},{64,80},{80,64},{96,112},{112,96},{1... | collective-permute-start | bytes 1572872 | tf_op jit(solution)/shard_map/ppermute | solution.py:51
  16.2 17.4 %collective-permute-start.5 = (bf16[4,128,256]{2,1,0:T(8,128)(2,1)S(1)}, bf16[4,128,256]{2,1,0:T(8,128)(2,1)S(1)}, u32[]{:S(2)}, u32[]{:S(2)}) collective-permute-start(bf16[4,128,256]{2,1,0:T(8,128)(2,1)S(1)} %slice.82), channel_id=1, source_target_pairs={{0,4},{16,28},{32,36},{48,60},{64,68},{80,92},{96,100},{112,124},{... | collective-permute-start | bytes 786440 | tf_op jit(solution)/shard_map/ppermute | solution.py:47
  19.4 14.1 %collective-permute-start.6 = (bf16[4,128,256]{2,1,0:T(8,128)(2,1)S(1)}, bf16[4,128,256]{2,1,0:T(8,128)(2,1)S(1)}, u32[]{:S(2)}, u32[]{:S(2)}) collective-permute-start(bf16[4,128,256]{2,1,0:T(8,128)(2,1)S(1)} %slice.83), channel_id=1, source_target_pairs={{0,1},{16,19},{32,33},{48,51},{64,65},{80,83},{96,97},{112,115},{1... | collective-permute-start | bytes 786440 | tf_op jit(solution)/shard_map/ppermute | solution.py:47
  20.7 13.5 %collective-permute-start.7 = (bf16[8,128,256]{2,1,0:T(8,128)(2,1)S(1)}, bf16[8,128,256]{2,1,0:T(8,128)(2,1)S(1)}, u32[]{:S(2)}, u32[]{:S(2)}) collective-permute-start(bf16[8,128,256]{2,1,0:T(8,128)(2,1)S(1)} %pad_maximum_fusion.1), channel_id=1, source_target_pairs={{0,4},{16,28},{32,36},{48,60},{64,68},{80,92},{96,100},{112,124},{... | collective-permute-start | bytes 1572872 | tf_op jit(solution)/shard_map/ppermute | solution.py:47
  22.5 13.9 %collective-permute-start.9 = (bf16[8,128,256]{2,1,0:T(8,128)(2,1)S(1)}, bf16[8,128,256]{2,1,0:T(8,128)(2,1)S(1)}, u32[]{:S(2)}, u32[]{:S(2)}) collective-permute-start(bf16[8,128,256]{2,1,0:T(8,128)(2,1)S(1)} %pad_maximum_fusion.2), channel_id=1, source_target_pairs={{0,1},{16,19},{32,33},{48,51},{64,65},{80,83},{96,97},{112,115},{1... | collective-permute-start | bytes 1572872 | tf_op jit(solution)/shard_map/ppermute | solution.py:47
  33.6 2.8 %collective-permute-start.14 = (bf16[2,128,256]{2,1,0:T(8,128)(2,1)S(1)}, bf16[2,128,256]{2,1,0:T(8,128)(2,1)S(1)}, u32[]{:S(2)}, u32[]{:S(2)}) collective-permute-start(bf16[2,128,256]{2,1,0:T(8,128)(2,1)S(1)} %slice.97), channel_id=1, source_target_pairs={{0,16},{16,0},{32,48},{48,32},{64,80},{80,64},{96,112},{112,96},{1... | collective-permute-start | bytes 393224 | tf_op jit(solution)/shard_map/ppermute | solution.py:51
  35.0 10.1 %collective-permute-start.12 = (bf16[8,128,256]{2,1,0:T(8,128)(2,1)S(1)}, bf16[8,128,256]{2,1,0:T(8,128)(2,1)S(1)}, u32[]{:S(2)}, u32[]{:S(2)}) collective-permute-start(bf16[8,128,256]{2,1,0:T(8,128)(2,1)S(1)} %pad_maximum_fusion.3), channel_id=1, source_target_pairs={{0,4},{16,28},{32,36},{48,60},{64,68},{80,92},{96,100},{112,124},{... | collective-permute-start | bytes 1572872 | tf_op jit(solution)/shard_map/ppermute | solution.py:47
  36.5 9.2 %collective-permute-start.15 = (bf16[8,128,256]{2,1,0:T(8,128)(2,1)S(1)}, bf16[8,128,256]{2,1,0:T(8,128)(2,1)S(1)}, u32[]{:S(2)}, u32[]{:S(2)}) collective-permute-start(bf16[8,128,256]{2,1,0:T(8,128)(2,1)S(1)} %pad_maximum_fusion.4), channel_id=1, source_target_pairs={{0,1},{16,19},{32,33},{48,51},{64,65},{80,83},{96,97},{112,115},{1... | collective-permute-start | bytes 1572872 | tf_op jit(solution)/shard_map/ppermute | solution.py:47
  44.5 4.3 %collective-permute-start.10 = (bf16[4,128,256]{2,1,0:T(8,128)(2,1)S(1)}, bf16[4,128,256]{2,1,0:T(8,128)(2,1)S(1)}, u32[]{:S(2)}, u32[]{:S(2)}) collective-permute-start(bf16[4,128,256]{2,1,0:T(8,128)(2,1)S(1)} %get-tuple-element.23), channel_id=1, source_target_pairs={{0,16},{16,0},{32,48},{48,32},{64,80},{80,64},{96,112},{112,96},{1... | collective-permute-start | bytes 786440 | tf_op jit(solution)/shard_map/ppermute | solution.py:51
  44.6 4.9 %collective-permute-start.8 = (bf16[4,128,256]{2,1,0:T(8,128)(2,1)S(1)}, bf16[4,128,256]{2,1,0:T(8,128)(2,1)S(1)}, u32[]{:S(2)}, u32[]{:S(2)}) collective-permute-start(bf16[4,128,256]{2,1,0:T(8,128)(2,1)S(1)} %get-tuple-element.25), channel_id=1, source_target_pairs={{0,16},{16,0},{32,48},{48,32},{64,80},{80,64},{96,112},{112,96},{1... | collective-permute-start | bytes 786440 | tf_op jit(solution)/shard_map/ppermute | solution.py:51
  45.1 12.9 %collective-permute-start.13 = (bf16[2,128,256]{2,1,0:T(8,128)(2,1)S(1)}, bf16[2,128,256]{2,1,0:T(8,128)(2,1)S(1)}, u32[]{:S(2)}, u32[]{:S(2)}) collective-permute-start(bf16[2,128,256]{2,1,0:T(8,128)(2,1)S(1)} %get-tuple-element.21), channel_id=1, source_target_pairs={{0,16},{16,0},{32,48},{48,32},{64,80},{80,64},{96,112},{112,96},{1... | collective-permute-start | bytes 393224 | tf_op jit(solution)/shard_map/ppermute | solution.py:51
  45.7 12.3 %collective-permute-start.16 = (bf16[2,128,256]{2,1,0:T(8,128)(2,1)S(1)}, bf16[2,128,256]{2,1,0:T(8,128)(2,1)S(1)}, u32[]{:S(2)}, u32[]{:S(2)}) collective-permute-start(bf16[2,128,256]{2,1,0:T(8,128)(2,1)S(1)} %get-tuple-element.19), channel_id=1, source_target_pairs={{0,16},{16,0},{32,48},{48,32},{64,80},{80,64},{96,112},{112,96},{1... | collective-permute-start | bytes 393224 | tf_op jit(solution)/shard_map/ppermute | solution.py:51
  46.4 11.7 %collective-permute-start.17 = (bf16[2,128,256]{2,1,0:T(8,128)(2,1)S(1)}, bf16[2,128,256]{2,1,0:T(8,128)(2,1)S(1)}, u32[]{:S(2)}, u32[]{:S(2)}) collective-permute-start(bf16[2,128,256]{2,1,0:T(8,128)(2,1)S(1)} %get-tuple-element.20), channel_id=1, source_target_pairs={{0,4},{16,28},{32,36},{48,60},{64,68},{80,92},{96,100},{112,124},{... | collective-permute-start | bytes 393224 | tf_op jit(solution)/shard_map/ppermute | solution.py:47
  48.9 9.2 %collective-permute-start.18 = (bf16[2,128,256]{2,1,0:T(8,128)(2,1)S(1)}, bf16[2,128,256]{2,1,0:T(8,128)(2,1)S(1)}, u32[]{:S(2)}, u32[]{:S(2)}) collective-permute-start(bf16[2,128,256]{2,1,0:T(8,128)(2,1)S(1)} %get-tuple-element.18), channel_id=1, source_target_pairs={{0,1},{16,19},{32,33},{48,51},{64,65},{80,83},{96,97},{112,115},{1... | collective-permute-start | bytes 393224 | tf_op jit(solution)/shard_map/ppermute | solution.py:47
  60.5 5.5 %collective-permute-start.21 = (f32[128,512]{1,0:T(8,128)S(1)}, f32[128,512]{1,0:T(8,128)S(1)}, u32[]{:S(2)}, u32[]{:S(2)}) collective-permute-start(f32[128,512]{1,0:T(8,128)S(1)} %get-tuple-element.15), channel_id=1, source_target_pairs={{0,16},{16,0},{32,48},{48,32},{64,80},{80,64},{96,112},{112,96},{1... | collective-permute-start | bytes 786440 | tf_op jit(solution)/shard_map/ppermute | solution.py:51
  62.9 9.4 %collective-permute-start.24 = (f32[128,512]{1,0:T(8,128)S(1)}, f32[128,512]{1,0:T(8,128)S(1)}, u32[]{:S(2)}, u32[]{:S(2)}) collective-permute-start(f32[128,512]{1,0:T(8,128)S(1)} %get-tuple-element.17), channel_id=1, source_target_pairs={{0,16},{16,0},{32,48},{48,32},{64,80},{80,64},{96,112},{112,96},{1... | collective-permute-start | bytes 786440 | tf_op jit(solution)/shard_map/ppermute | solution.py:51
  65.9 7.1 %collective-permute-start.20 = (f32[128,512]{1,0:T(8,128)S(1)}, f32[128,512]{1,0:T(8,128)S(1)}, u32[]{:S(2)}, u32[]{:S(2)}) collective-permute-start(f32[128,512]{1,0:T(8,128)S(1)} %get-tuple-element.13), channel_id=1, source_target_pairs={{0,16},{16,0},{32,48},{48,32},{64,80},{80,64},{96,112},{112,96},{1... | collective-permute-start | bytes 786440 | tf_op jit(solution)/shard_map/ppermute | solution.py:51
  66.1 7.1 %collective-permute-start.22 = (f32[128,512]{1,0:T(8,128)S(1)}, f32[128,512]{1,0:T(8,128)S(1)}, u32[]{:S(2)}, u32[]{:S(2)}) collective-permute-start(f32[128,512]{1,0:T(8,128)S(1)} %add.116), channel_id=1, source_target_pairs={{0,32},{16,112},{32,64},{48,16},{64,96},{80,48},{96,0},{112,80},{1... | collective-permute-start | bytes 786440 | tf_op jit(solution)/shard_map/ppermute | solution.py:47
  72.3 4.2 %collective-permute-start.19 = (f32[128,512]{1,0:T(8,128)S(1)}, f32[128,512]{1,0:T(8,128)S(1)}, u32[]{:S(2)}, u32[]{:S(2)}) collective-permute-start(f32[128,512]{1,0:T(8,128)S(1)} %get-tuple-element.11), channel_id=1, source_target_pairs={{0,16},{16,0},{32,48},{48,32},{64,80},{80,64},{96,112},{112,96},{1... | collective-permute-start | bytes 786440 | tf_op jit(solution)/shard_map/ppermute | solution.py:51
  73.0 6.9 %collective-permute-start.25 = (f32[128,512]{1,0:T(8,128)S(1)}, f32[128,512]{1,0:T(8,128)S(1)}, u32[]{:S(2)}, u32[]{:S(2)}) collective-permute-start(f32[128,512]{1,0:T(8,128)S(1)} %add.118), channel_id=1, source_target_pairs={{0,96},{16,48},{32,0},{48,80},{64,32},{80,112},{96,64},{112,16},{1... | collective-permute-start | bytes 786440 | tf_op jit(solution)/shard_map/ppermute | solution.py:47
  73.3 8.3 %collective-permute-start.23 = (f32[128,512]{1,0:T(8,128)S(1)}, f32[128,512]{1,0:T(8,128)S(1)}, u32[]{:S(2)}, u32[]{:S(2)}) collective-permute-start(f32[128,512]{1,0:T(8,128)S(1)} %add_add_fusion), channel_id=1, source_target_pairs={{0,32},{16,112},{32,64},{48,16},{64,96},{80,48},{96,0},{112,80},{1... | collective-permute-start | bytes 786440 | tf_op jit(solution)/shard_map/ppermute | solution.py:47
  (7 other events, 14.9 us)

commit v2 on v1

v2 whole, which is shorter than its diff:
```python
import functools

import jax
import jax.numpy as jnp
from jax import lax
from jax.experimental import pallas as pl
from jax.experimental.pallas import tpu as pltpu
from jax.sharding import PartitionSpec as P

SIDE = 4
TILE = 256
CHUNK = 1024
TILES = CHUNK // TILE
BITS = 8

VM = pltpu.VMEM
FULL = pl.BlockSpec(memory_space=VM)

AXES = ("row", "col")


def place(x, y, z, core):
    return (z * 2 + core) * (SIDE * SIDE) + x * SIDE + y


def pairs(axis, flip=False):
    out = []
    for x in range(SIDE):
        for y in range(SIDE):
            for z in range(SIDE):
                for core in range(2):
                    at = [x, y, z]
                    if axis == "core":
                        out.append((place(*at, core), place(*at, 1 - core)))
                        continue
                    n = "xyz".index(axis)
                    step = 1 if (core == 0) != flip else -1
                    to = list(at)
                    to[n] = (to[n] + step) % SIDE
                    out.append((place(*at, core), place(*to, core)))
    return out


def send(value, axis, flip=False):
    return lax.ppermute(value, AXES, pairs(axis, flip))


def swap(value):
    return lax.ppermute(value, AXES, pairs("core"))


def prep_kernel(f_ref, o_ref, s_ref):
    s_ref[...] = f_ref[...].astype(jnp.float32)
    for j in range(TILES):
        rows = []
        for b in range(BITS):
            scale = 2.0**-b if b < 7 else -(2.0**-7)
            rows.append(s_ref[pl.ds(8 * j + b, 32, stride=32), :] * scale)
        o_ref[j] = jnp.concatenate(rows, 0).T.astype(jnp.bfloat16)


def prep(f):
    return pl.pallas_call(
        prep_kernel,
        out_shape=VM((TILES, 128, TILE), jnp.bfloat16),
        in_specs=[FULL],
        out_specs=FULL,
        scratch_shapes=[pltpu.VMEM((CHUNK, 128), jnp.float32)],
        name="prep",
    )(f)


def split_kernel(a_ref, v_ref, o_ref, w_ref):
    r = pl.program_id(0)
    for i in range(a_ref.shape[1] // 128):
        a = a_ref[:, 128 * i : 128 * i + 128]
        for j in range(4):
            part = (lax.shift_right_logical(a, 8 * j) if j else a).astype(jnp.int8).T
            for c in range(4):
                o_ref[r, 16 * i + 4 * c + j] = part[32 * c : 32 * c + 32]
    w_ref[...] = v_ref[...]


def split(adj, visited):
    d, w = adj.shape
    return pl.pallas_call(
        split_kernel,
        grid=(d // 512,),
        in_specs=[pl.BlockSpec((512, w), lambda k: (k, 0)), FULL],
        out_specs=(FULL, FULL),
        out_shape=(VM((d // 512, w // 8, 32, 512), jnp.int8), VM(visited.shape, jnp.int32)),
        compiler_params=pltpu.CompilerParams(vmem_limit_bytes=24 << 20),
        name="split",
    )(pltpu.with_memory_space_constraint(adj, pltpu.HBM), visited)


def here():
    row, col = lax.axis_index("row"), lax.axis_index("col")
    core = row & 1
    return col >> 2, col & 3, row >> 1, core, 1 - 2 * core


def expand(a_ref, r, where):
    parts = []
    for at in where:
        x = a_ref[r, at]
        for b in range(BITS):
            m = 1 << b if b < 7 else -128
            parts.append((x & jnp.int8(m)).astype(jnp.bfloat16))
    return jnp.concatenate(parts, 0)


def mm_kernel(*refs, tiles, arrays, group, blocks, start):
    a_ref, refs = refs[0], refs[1:]
    if not start:
        acc_ref, refs = refs[0], refs[1:]
    f_refs, outs = refs[:arrays], refs[arrays:]
    x, y, z, core, s = here()
    home = {}
    for t in tiles:
        if t[2:4] not in home:
            (a, b), (c, d) = t[2:4]
            home[t[2:4]] = (((x + a * s + 2 * b) & 3) * SIDE + ((y + c * s + 2 * d) & 3)) * TILES
    where = [home[t[2:4]] + t[4] for t in tiles]

    if blocks is not None:
        f = jnp.concatenate([f_refs[t[0]][t[1]] for t in tiles], 1)
        for out, (a, b, other) in zip(outs, blocks):
            r = ((z + a * s + 2 * b) & 3) * 2 + (1 - core if other else core)
            out[...] = acc_ref[r] + jnp.dot(f, expand(a_ref, r, where), preferred_element_type=jnp.float32)
        return

    if len(tiles) == group:
        f = jnp.concatenate([f_refs[t[0]][t[1]] for t in tiles], 1)
        for r in range(8):
            got = jnp.dot(f, expand(a_ref, r, where), preferred_element_type=jnp.float32)
            outs[0][r] = got if start else outs[0][r] + got
        return

    out, scr, at = outs
    for n, t in enumerate(tiles):
        scr[n] = f_refs[t[0]][t[1]]
        at[n] = where[n]

    def step(i, carry):
        base = i * group
        f = jnp.concatenate([scr[base + t] for t in range(group)], 1)
        for r in range(8):
            rhs = expand(a_ref, r, [at[base + t] for t in range(group)])
            out[r] = out[r] + jnp.dot(f, rhs, preferred_element_type=jnp.float32)
        return carry

    lax.fori_loop(0, len(tiles) // group, step, 0)


def mm(ab, acc, arrays, tiles, group, blocks=None):
    count = len(tiles)
    if blocks is None:
        out_shape = VM((8, 128, 512), jnp.float32)
        out_specs = FULL
        lanes = 4096
    else:
        out_shape = (VM((128, 512), jnp.float32),) * len(blocks)
        out_specs = (FULL,) * len(blocks)
        lanes = 512 * len(blocks)
    args = [ab] + ([acc] if acc is not None else []) + list(arrays)
    loop = blocks is None and count != group
    return pl.pallas_call(
        functools.partial(
            mm_kernel, tiles=tuple(tiles), arrays=len(arrays), group=group, blocks=blocks, start=acc is None
        ),
        out_shape=out_shape,
        in_specs=[FULL] * len(args),
        out_specs=out_specs,
        scratch_shapes=[pltpu.VMEM((count, 128, TILE), jnp.bfloat16), pltpu.SMEM((count,), jnp.int32)] if loop else [],
        input_output_aliases={1: 0} if blocks is None and acc is not None else {},
        cost_estimate=pl.CostEstimate(flops=2 * 128 * TILE * count * lanes, bytes_accessed=0, transcendentals=0),
        compiler_params=pltpu.CompilerParams(vmem_limit_bytes=32 << 20),
        name="bits_mm",
    )(*args)


def finish_kernel(a_ref, b_ref, c_ref, d_ref, v_ref, p_ref, o_ref):
    reached = a_ref[...] + b_ref[...] + c_ref[...] + d_ref[...]
    shift = lax.broadcasted_iota(jnp.int32, (32, 1), 0)
    rows = []
    words = []
    for w in range(4):
        got = reached[32 * w : 32 * w + 32]
        word = v_ref[w : w + 1]
        unseen = (lax.shift_right_arithmetic(jnp.broadcast_to(word, got.shape), jnp.broadcast_to(shift, got.shape)) & 1) == 0
        rows.append(jnp.where(unseen, got, 0.0))
        fresh = jnp.where(unseen & (got > 0), lax.shift_left(jnp.int32(1), jnp.broadcast_to(shift, got.shape)), 0)
        words.append(word | jnp.sum(fresh, 0, keepdims=True))
    p_ref[...] = jnp.concatenate(rows, 0).T
    o_ref[...] = jnp.concatenate(words, 0)


def finish(parts, visited):
    return pl.pallas_call(
        finish_kernel,
        out_shape=(jax.ShapeDtypeStruct((512, 128), jnp.float32), jax.ShapeDtypeStruct((4, 512), jnp.int32)),
        in_specs=[FULL] * 5,
        out_specs=(FULL, FULL),
        name="finish",
    )(*parts, visited)


O, M, Q, T = (0, 0), (-1, 0), (1, 0), (0, 1)
H0, H1, ALL = (0, 1), (2, 3), (0, 1, 2, 3)


def tiles(array, start, dx, dy, js):
    return [(array, start + n, dx, dy, j) for n, j in enumerate(js)]


def level(adjacency, frontier, visited):
    ft = prep(frontier)
    mine = jnp.concatenate([ft, swap(ft)], 0)
    dx = send(mine, "x")
    dy = send(mine, "y")
    ab, seen = split(adjacency, visited)
    acc = mm(ab, None, [ft], tiles(0, 0, O, O, ALL), 4)

    bx = send(dx[:4], "x")
    by = send(dy[:4], "y")
    px, py = swap(dx), swap(dy)
    cx = send(jnp.concatenate([dy[2:4], py[6:8], dy[6:8], py[2:4]], 0), "x")
    cy = send(jnp.concatenate([dx[0:2], px[4:6], dx[4:6], px[0:2]], 0), "y")
    near_tiles = (
        tiles(0, 0, M, O, ALL) + tiles(1, 4, Q, O, ALL) + tiles(2, 0, O, M, ALL) + tiles(3, 4, O, Q, ALL)
    )
    acc = mm(ab, acc, [dx, px, dy, py], near_tiles, 8)

    pbx, pby = swap(bx[0:2]), swap(by[2:4])
    ex = send(jnp.concatenate([by[2:4], pby, cx[:4]], 0), "x")
    ey = send(jnp.concatenate([bx[0:2], pbx, cy[:4]], 0), "y")
    pcx, pcy = swap(cx[4:8]), swap(cy[4:8])
    far_tiles = (
        tiles(0, 0, T, O, ALL)
        + tiles(1, 0, O, T, ALL)
        + tiles(2, 0, M, M, H1)
        + tiles(2, 2, M, Q, H1)
        + tiles(3, 0, M, M, H0)
        + tiles(3, 2, Q, M, H0)
    )
    acc = mm(ab, acc, [bx, by, cx, cy], far_tiles, 8)

    gx, gy = send(ex[:2], "x"), send(ey[:2], "y")
    pex, pey = swap(ex[2:4]), swap(ey[2:4])
    side_tiles = tiles(0, 0, Q, Q, H1) + tiles(0, 2, Q, M, H1) + tiles(1, 0, Q, Q, H0) + tiles(1, 2, M, Q, H0)
    acc = mm(ab, acc, [pcx, pcy], side_tiles, 8)

    last = [ex, pex, ey, pey, gx, gy]
    last_tiles = (
        tiles(0, 0, M, T, H1)
        + tiles(1, 0, Q, T, H1)
        + tiles(0, 4, T, M, H1)
        + tiles(0, 6, T, Q, H1)
        + tiles(2, 0, T, M, H0)
        + tiles(3, 0, T, Q, H0)
        + tiles(2, 4, M, T, H0)
        + tiles(2, 6, Q, T, H0)
        + tiles(4, 0, T, T, H1)
        + tiles(5, 0, T, T, H0)
    )
    done = lambda *blocks: mm(ab, acc, last, last_tiles, 20, blocks)
    two, two_o = done((0, 1, False), (0, 1, True))
    up_o, down_o = done((-1, 0, True), (1, 0, True))
    up, down = done((1, 0, False), (-1, 0, False))
    own, own_o = done((0, 0, False), (0, 0, True))
    hop = send(two + swap(two_o), "z")
    got0 = send(down + swap(down_o), "z", True)
    got1 = send(up + swap(up_o) + hop, "z")
    return finish([own, swap(own_o), got1, got0], seen)


def solution(mesh):
    placed = (P("col", "row"), P(("row", "col"), None), P(None, ("col", "row")))
    return jax.shard_map(
        level,
        mesh=mesh,
        in_specs=placed,
        out_specs=(P(("col", "row"), None), P(None, ("col", "row"))),
        check_vma=False,
    )
```

time: 84.5 us -> 83 us (0.982)
  the two profiles are of different devices: /device:TPU:1 before, /device:TPU:2 now
where the time goes in v2:
time: 83 us; the launch traced here: 82.6 us
  Pallas kernels  29.6 us (36%)
  waiting for transfers between devices  28.4 us (34%)
  starting transfers between devices  20.9 us (25%)
  local copies, waits for them, and re-layouts  2.25 us (3%)
  between operations  0.97 us (1%)
    ppermute x13, waiting for transfers between devices, send(): return lax.ppermute(value, AXES, pairs(axis, flip))  26.9 us
    pallas_call x8, Pallas kernels, mm(): pl.pallas_call(functools.partial(mm_kernel, tiles=tuple(tiles), arrays=le...  19.3 us
    ppermute x13, starting transfers between devices, send(): return lax.ppermute(value, AXES, pairs(axis, flip))  15.8 us
    pallas_call x1, Pallas kernels, split(): pl.pallas_call(split_kernel, grid=(d // 512,), in_specs=[pl.BlockSpec((51...  6.98 us
    ppermute x13, starting transfers between devices, swap(): return lax.ppermute(value, AXES, pairs('core'))  5.13 us
    pallas_call x1, Pallas kernels, finish(): pl.pallas_call(finish_kernel, out_shape=(jax.ShapeDtypeStruct((512, 128),...  2.07 us
    unnamed x12, local copies, waits for them, and re-layouts  2.01 us
  transfers between devices with their start and end apart: 26, of which 10 were waited for; matrix products, arithmetic and copies ran while one was open for 1% of the time, Pallas kernels for 30%

profile of v2, /device:TPU:2, one launch (start us, length us, event | category | flops | bytes accessed | tf_op | source)
XLA Modules:
  0.0 82.6 jit_solution(9258998644607292521)
XLA Ops:
  2.1 1.5 %collective-permute-done = bf16[4,128,256]{2,1,0:T(8,128)(2,1)S(1)} collective-permute-done((bf16[4,128,256]{2,1,0:T(8,128)(2,1)S(1)}, bf16[4,128,256]{2,1,0:T(8,128)(2,1)S(1)}, u32[]{:S(2)}, u32[]{:S(2)}) %collective-permute-start) | collective-permute-done | bytes 262176 | tf_op jit(solution)/shard_map/ppermute | solution.py:49
  3.6 1.6 %collective-permute-start.1 = (bf16[8,128,256]{2,1,0:T(8,128)(2,1)S(1)}, bf16[8,128,256]{2,1,0:T(8,128)(2,1)S(1)}, u32[]{:S(2)}, u32[]{:S(2)}) collective-permute-start(bf16[8,128,256]{2,1,0:T(8,128)(2,1)S(1)} %pad_maximum_fusion), channel_id=1, source_target_pairs={{0,4},{16,28},{32,36},{48,60},{64,68},{80,92},{96,100},{112,124},{... | collective-permute-start | bytes 1572872 | tf_op jit(solution)/shard_map/ppermute | solution.py:45
  5.2 1.6 %collective-permute-start.3 = (bf16[8,128,256]{2,1,0:T(8,128)(2,1)S(1)}, bf16[8,128,256]{2,1,0:T(8,128)(2,1)S(1)}, u32[]{:S(2)}, u32[]{:S(2)}) collective-permute-start(bf16[8,128,256]{2,1,0:T(8,128)(2,1)S(1)} %pad_maximum_fusion), channel_id=1, source_target_pairs={{0,1},{16,19},{32,33},{48,51},{64,65},{80,83},{96,97},{112,115},{1... | collective-permute-start | bytes 1572872 | tf_op jit(solution)/shard_map/ppermute | solution.py:45
  7.5 7.0 %split.1 = (s8[8,64,32,512]{3,2,1,0:T(32,128)(4,1)S(1)}, s32[4,512]{1,0:T(4,128)S(1)}) custom-call(s32[4096,512]{1,0:T(8,128)} %a_ref.1, s32[4,512]{1,0:T(4,128)S(1)} %copy-done.1), custom_call_target="tpu_custom_call" | custom-call | tf_op jit(solution)/shard_map/split/pallas_call | solution.py:86
  16.4 1.6 %collective-permute-start.5 = (bf16[4,128,256]{2,1,0:T(8,128)(2,1)S(1)}, bf16[4,128,256]{2,1,0:T(8,128)(2,1)S(1)}, u32[]{:S(2)}, u32[]{:S(2)}) collective-permute-start(bf16[4,128,256]{2,1,0:T(8,128)(2,1)S(1)} %slice.82), channel_id=1, source_target_pairs={{0,4},{16,28},{32,36},{48,60},{64,68},{80,92},{96,100},{112,124},{... | collective-permute-start | bytes 786440 | tf_op jit(solution)/shard_map/ppermute | solution.py:45
  19.6 6.1 %collective-permute-done.6.refs_3_ = bf16[4,128,256]{2,1,0:T(8,128)(2,1)S(1)} collective-permute-done((bf16[4,128,256]{2,1,0:T(8,128)(2,1)S(1)}, bf16[4,128,256]{2,1,0:T(8,128)(2,1)S(1)}, u32[]{:S(2)}, u32[]{:S(2)}) %collective-permute-start.6) | collective-permute-done | bytes 262176 | tf_op jit(solution)/shard_map/ppermute | solution.py:45
  26.7 1.6 %collective-permute-start.7 = (bf16[8,128,256]{2,1,0:T(8,128)(2,1)S(1)}, bf16[8,128,256]{2,1,0:T(8,128)(2,1)S(1)}, u32[]{:S(2)}, u32[]{:S(2)}) collective-permute-start(bf16[8,128,256]{2,1,0:T(8,128)(2,1)S(1)} %pad_maximum_fusion.1), channel_id=1, source_target_pairs={{0,4},{16,28},{32,36},{48,60},{64,68},{80,92},{96,100},{112,124},{... | collective-permute-start | bytes 1572872 | tf_op jit(solution)/shard_map/ppermute | solution.py:45
  28.2 4.8 %bits_mm.9.refs_1_ = f32[8,128,512]{2,1,0:T(8,128)S(1)} custom-call(s8[8,64,32,512]{3,2,1,0:T(32,128)(4,1)S(1)} %get-tuple-element.12.refs_0_, f32[8,128,512]{2,1,0:T(8,128)S(1)} %bits_mm.8.refs_1_, bf16[8,128,256]{2,1,0:T(8,128)(2,1)S(1)} %collective-permute-done.1.refs_2_, ...), custom_call_target="tpu_custom_call", output_to_operand_aliasing={{}: (1, {})} | custom-call | flops 4294967296 | tf_op jit(solution)/shard_map/bits_mm/pallas_call | solution.py:168
  33.0 3.9 %collective-permute-done.8.refs_5_ = bf16[8,128,256]{2,1,0:T(8,128)(2,1)S(1)} collective-permute-done((bf16[8,128,256]{2,1,0:T(8,128)(2,1)S(1)}, bf16[8,128,256]{2,1,0:T(8,128)(2,1)S(1)}, u32[]{:S(2)}, u32[]{:S(2)}) %collective-permute-start.8) | collective-permute-done | bytes 524320 | tf_op jit(solution)/shard_map/ppermute | solution.py:45
  37.7 1.6 %collective-permute-start.12 = (bf16[8,128,256]{2,1,0:T(8,128)(2,1)S(1)}, bf16[8,128,256]{2,1,0:T(8,128)(2,1)S(1)}, u32[]{:S(2)}, u32[]{:S(2)}) collective-permute-start(bf16[8,128,256]{2,1,0:T(8,128)(2,1)S(1)} %pad_maximum_fusion.3), channel_id=1, source_target_pairs={{0,4},{16,28},{32,36},{48,60},{64,68},{80,92},{96,100},{112,124},{... | collective-permute-start | bytes 1572872 | tf_op jit(solution)/shard_map/ppermute | solution.py:45
  39.6 4.8 %bits_mm.10.refs_1_ = f32[8,128,512]{2,1,0:T(8,128)S(1)} custom-call(s8[8,64,32,512]{3,2,1,0:T(32,128)(4,1)S(1)} %get-tuple-element.12.refs_0_, f32[8,128,512]{2,1,0:T(8,128)S(1)} %bits_mm.9.refs_1_, bf16[4,128,256]{2,1,0:T(8,128)(2,1)S(1)} %collective-permute-done.5.refs_2_, ...), custom_call_target="tpu_custom_call", output_to_operand_aliasing={{}: (1, {})} | custom-call | flops 4294967296 | tf_op jit(solution)/shard_map/bits_mm/pallas_call | solution.py:168
  44.4 2.6 %collective-permute-done.12.refs_2_ = bf16[8,128,256]{2,1,0:T(8,128)(2,1)S(1)} collective-permute-done((bf16[8,128,256]{2,1,0:T(8,128)(2,1)S(1)}, bf16[8,128,256]{2,1,0:T(8,128)(2,1)S(1)}, u32[]{:S(2)}, u32[]{:S(2)}) %collective-permute-start.12) | collective-permute-done | bytes 524320 | tf_op jit(solution)/shard_map/ppermute | solution.py:45
  47.1 2.9 %collective-permute-done.15.refs_4_ = bf16[8,128,256]{2,1,0:T(8,128)(2,1)S(1)} collective-permute-done((bf16[8,128,256]{2,1,0:T(8,128)(2,1)S(1)}, bf16[8,128,256]{2,1,0:T(8,128)(2,1)S(1)}, u32[]{:S(2)}, u32[]{:S(2)}) %collective-permute-start.15) | collective-permute-done | bytes 524320 | tf_op jit(solution)/shard_map/ppermute | solution.py:45
  50.1 2.5 %collective-permute-start.17 = (bf16[2,128,256]{2,1,0:T(8,128)(2,1)S(1)}, bf16[2,128,256]{2,1,0:T(8,128)(2,1)S(1)}, u32[]{:S(2)}, u32[]{:S(2)}) collective-permute-start(bf16[2,128,256]{2,1,0:T(8,128)(2,1)S(1)} %get-tuple-element.24), channel_id=1, source_target_pairs={{0,4},{16,28},{32,36},{48,60},{64,68},{80,92},{96,100},{112,124},{... | collective-permute-start | bytes 393224 | tf_op jit(solution)/shard_map/ppermute | solution.py:45
  52.6 2.4 %bits_mm.11.refs_1_ = f32[8,128,512]{2,1,0:T(8,128)S(1)} custom-call(s8[8,64,32,512]{3,2,1,0:T(32,128)(4,1)S(1)} %get-tuple-element.12.refs_0_, f32[8,128,512]{2,1,0:T(8,128)S(1)} %bits_mm.10.refs_1_, bf16[4,128,256]{2,1,0:T(8,128)(2,1)S(1)} %collective-permute-done.9.refs_2_, ...), custom_call_target="tpu_custom_call", output_to_operand_aliasing={{}: (1, {})} | custom-call | flops 2147483648 | tf_op jit(solution)/shard_map/bits_mm/pallas_call | solution.py:168
  55.2 3.6 %collective-permute-done.18.refs_7_ = bf16[2,128,256]{2,1,0:T(8,128)(2,1)S(1)} collective-permute-done((bf16[2,128,256]{2,1,0:T(8,128)(2,1)S(1)}, bf16[2,128,256]{2,1,0:T(8,128)(2,1)S(1)}, u32[]{:S(2)}, u32[]{:S(2)}) %collective-permute-start.18) | collective-permute-done | bytes 131104 | tf_op jit(solution)/shard_map/ppermute | solution.py:45
  58.8 1.5 %bits_mm.15 = (f32[128,512]{1,0:T(8,128)S(1)}, f32[128,512]{1,0:T(8,128)S(1)}) custom-call(s8[8,64,32,512]{3,2,1,0:T(32,128)(4,1)S(1)} %get-tuple-element.12.refs_0_, f32[8,128,512]{2,1,0:T(8,128)S(1)} %bits_mm.11.refs_1_, bf16[8,128,256]{2,1,0:T(8,128)(2,1)S(1)} %collective-permute-done.12.refs_2_, ...), custom_call_target="tpu_custom_call" | custom-call | flops 1342177280 | tf_op jit(solution)/shard_map/bits_mm/pallas_call | solution.py:168
  60.4 1.5 %bits_mm.14 = (f32[128,512]{1,0:T(8,128)S(1)}, f32[128,512]{1,0:T(8,128)S(1)}) custom-call(s8[8,64,32,512]{3,2,1,0:T(32,128)(4,1)S(1)} %get-tuple-element.12.refs_0_, f32[8,128,512]{2,1,0:T(8,128)S(1)} %bits_mm.11.refs_1_, bf16[8,128,256]{2,1,0:T(8,128)(2,1)S(1)} %collective-permute-done.12.refs_2_, ...), custom_call_target="tpu_custom_call" | custom-call | flops 1342177280 | tf_op jit(solution)/shard_map/bits_mm/pallas_call | solution.py:168
  62.6 2.0 %collective-permute-start.22 = (f32[128,512]{1,0:T(8,128)S(1)}, f32[128,512]{1,0:T(8,128)S(1)}, u32[]{:S(2)}, u32[]{:S(2)}) collective-permute-start(f32[128,512]{1,0:T(8,128)S(1)} %add.13), channel_id=1, source_target_pairs={{0,32},{16,112},{32,64},{48,16},{64,96},{80,48},{96,0},{112,80},{1... | collective-permute-start | bytes 786440 | tf_op jit(solution)/shard_map/ppermute | solution.py:45
  64.6 1.5 %bits_mm.12 = (f32[128,512]{1,0:T(8,128)S(1)}, f32[128,512]{1,0:T(8,128)S(1)}) custom-call(s8[8,64,32,512]{3,2,1,0:T(32,128)(4,1)S(1)} %get-tuple-element.12.refs_0_, f32[8,128,512]{2,1,0:T(8,128)S(1)} %bits_mm.11.refs_1_, bf16[8,128,256]{2,1,0:T(8,128)(2,1)S(1)} %collective-permute-done.12.refs_2_, ...), custom_call_target="tpu_custom_call" | custom-call | flops 1342177280 | tf_op jit(solution)/shard_map/bits_mm/pallas_call | solution.py:168
  66.2 2.6 %collective-permute-start.19 = (f32[128,512]{1,0:T(8,128)S(1)}, f32[128,512]{1,0:T(8,128)S(1)}, u32[]{:S(2)}, u32[]{:S(2)}) collective-permute-start(f32[128,512]{1,0:T(8,128)S(1)} %get-tuple-element.14), channel_id=1, source_target_pairs={{0,16},{16,0},{32,48},{48,32},{64,80},{80,64},{96,112},{112,96},{1... | collective-permute-start | bytes 786440 | tf_op jit(solution)/shard_map/ppermute | solution.py:49
  68.7 1.5 %bits_mm.13 = (f32[128,512]{1,0:T(8,128)S(1)}, f32[128,512]{1,0:T(8,128)S(1)}) custom-call(s8[8,64,32,512]{3,2,1,0:T(32,128)(4,1)S(1)} %get-tuple-element.12.refs_0_, f32[8,128,512]{2,1,0:T(8,128)S(1)} %bits_mm.11.refs_1_, bf16[8,128,256]{2,1,0:T(8,128)(2,1)S(1)} %collective-permute-done.12.refs_2_, ...), custom_call_target="tpu_custom_call" | custom-call | flops 1342177280 | tf_op jit(solution)/shard_map/bits_mm/pallas_call | solution.py:168
  72.6 6.2 %collective-permute-done.25.d_ref = f32[128,512]{1,0:T(8,128)S(1)} collective-permute-done((f32[128,512]{1,0:T(8,128)S(1)}, f32[128,512]{1,0:T(8,128)S(1)}, u32[]{:S(2)}, u32[]{:S(2)}) %collective-permute-start.25) | collective-permute-done | bytes 262176 | tf_op jit(solution)/shard_map/ppermute | solution.py:45
  80.6 2.1 %finish.1 = (f32[512,128]{1,0:T(8,128)}, s32[4,512]{1,0:T(4,128)}) custom-call(f32[128,512]{1,0:T(8,128)} %copy-done, f32[128,512]{1,0:T(8,128)} %copy-done.3, f32[128,512]{1,0:T(8,128)} %copy-done.5, f32[128,512]{1,0:T(8,128)} %copy-done.4, s32[4,512]{1,0:T(4,128)} %copy-done.2), custom_call_target="tpu_custom_call" | custom-call | tf_op jit(solution)/shard_map/finish/pallas_call | solution.py:200
  (71 shorter events, 12.9 us)
Async XLA Ops:
  3.6 11.4 %collective-permute-start.1 = (bf16[8,128,256]{2,1,0:T(8,128)(2,1)S(1)}, bf16[8,128,256]{2,1,0:T(8,128)(2,1)S(1)}, u32[]{:S(2)}, u32[]{:S(2)}) collective-permute-start(bf16[8,128,256]{2,1,0:T(8,128)(2,1)S(1)} %pad_maximum_fusion), channel_id=1, source_target_pairs={{0,4},{16,28},{32,36},{48,60},{64,68},{80,92},{96,100},{112,124},{... | collective-permute-start | bytes 1572872 | tf_op jit(solution)/shard_map/ppermute | solution.py:45
  5.2 12.8 %collective-permute-start.3 = (bf16[8,128,256]{2,1,0:T(8,128)(2,1)S(1)}, bf16[8,128,256]{2,1,0:T(8,128)(2,1)S(1)}, u32[]{:S(2)}, u32[]{:S(2)}) collective-permute-start(bf16[8,128,256]{2,1,0:T(8,128)(2,1)S(1)} %pad_maximum_fusion), channel_id=1, source_target_pairs={{0,1},{16,19},{32,33},{48,51},{64,65},{80,83},{96,97},{112,115},{1... | collective-permute-start | bytes 1572872 | tf_op jit(solution)/shard_map/ppermute | solution.py:45
  15.1 11.3 %collective-permute-start.2 = (bf16[8,128,256]{2,1,0:T(8,128)(2,1)S(1)}, bf16[8,128,256]{2,1,0:T(8,128)(2,1)S(1)}, u32[]{:S(2)}, u32[]{:S(2)}) collective-permute-start(bf16[8,128,256]{2,1,0:T(8,128)(2,1)S(1)} %collective-permute-done.1.refs_2_), channel_id=1, source_target_pairs={{0,16},{16,0},{32,48},{48,32},{64,80},{80,64},{96,112},{112,96},{1... | collective-permute-start | bytes 1572872 | tf_op jit(solution)/shard_map/ppermute | solution.py:49
  16.4 9.3 %collective-permute-start.5 = (bf16[4,128,256]{2,1,0:T(8,128)(2,1)S(1)}, bf16[4,128,256]{2,1,0:T(8,128)(2,1)S(1)}, u32[]{:S(2)}, u32[]{:S(2)}) collective-permute-start(bf16[4,128,256]{2,1,0:T(8,128)(2,1)S(1)} %slice.82), channel_id=1, source_target_pairs={{0,4},{16,28},{32,36},{48,60},{64,68},{80,92},{96,100},{112,124},{... | collective-permute-start | bytes 786440 | tf_op jit(solution)/shard_map/ppermute | solution.py:45
  18.0 7.7 %collective-permute-start.6 = (bf16[4,128,256]{2,1,0:T(8,128)(2,1)S(1)}, bf16[4,128,256]{2,1,0:T(8,128)(2,1)S(1)}, u32[]{:S(2)}, u32[]{:S(2)}) collective-permute-start(bf16[4,128,256]{2,1,0:T(8,128)(2,1)S(1)} %slice.83), channel_id=1, source_target_pairs={{0,1},{16,19},{32,33},{48,51},{64,65},{80,83},{96,97},{112,115},{1... | collective-permute-start | bytes 786440 | tf_op jit(solution)/shard_map/ppermute | solution.py:45
  19.3 7.2 %collective-permute-start.4 = (bf16[8,128,256]{2,1,0:T(8,128)(2,1)S(1)}, bf16[8,128,256]{2,1,0:T(8,128)(2,1)S(1)}, u32[]{:S(2)}, u32[]{:S(2)}) collective-permute-start(bf16[8,128,256]{2,1,0:T(8,128)(2,1)S(1)} %collective-permute-done.3.refs_4_), channel_id=1, source_target_pairs={{0,16},{16,0},{32,48},{48,32},{64,80},{80,64},{96,112},{112,96},{1... | collective-permute-start | bytes 1572872 | tf_op jit(solution)/shard_map/ppermute | solution.py:49
  25.7 12.0 %collective-permute-start.11 = (bf16[2,128,256]{2,1,0:T(8,128)(2,1)S(1)}, bf16[2,128,256]{2,1,0:T(8,128)(2,1)S(1)}, u32[]{:S(2)}, u32[]{:S(2)}) collective-permute-start(bf16[2,128,256]{2,1,0:T(8,128)(2,1)S(1)} %slice.94), channel_id=1, source_target_pairs={{0,16},{16,0},{32,48},{48,32},{64,80},{80,64},{96,112},{112,96},{1... | collective-permute-start | bytes 393224 | tf_op jit(solution)/shard_map/ppermute | solution.py:49
  25.8 13.5 %collective-permute-start.14 = (bf16[2,128,256]{2,1,0:T(8,128)(2,1)S(1)}, bf16[2,128,256]{2,1,0:T(8,128)(2,1)S(1)}, u32[]{:S(2)}, u32[]{:S(2)}) collective-permute-start(bf16[2,128,256]{2,1,0:T(8,128)(2,1)S(1)} %slice.97), channel_id=1, source_target_pairs={{0,16},{16,0},{32,48},{48,32},{64,80},{80,64},{96,112},{112,96},{1... | collective-permute-start | bytes 393224 | tf_op jit(solution)/shard_map/ppermute | solution.py:49
  26.5 10.5 %collective-permute-start.8 = (bf16[8,128,256]{2,1,0:T(8,128)(2,1)S(1)}, bf16[8,128,256]{2,1,0:T(8,128)(2,1)S(1)}, u32[]{:S(2)}, u32[]{:S(2)}) collective-permute-start(bf16[8,128,256]{2,1,0:T(8,128)(2,1)S(1)} %pad_maximum_fusion.2), channel_id=1, source_target_pairs={{0,1},{16,19},{32,33},{48,51},{64,65},{80,83},{96,97},{112,115},{1... | collective-permute-start | bytes 1572872 | tf_op jit(solution)/shard_map/ppermute | solution.py:45
  26.7 10.4 %collective-permute-start.7 = (bf16[8,128,256]{2,1,0:T(8,128)(2,1)S(1)}, bf16[8,128,256]{2,1,0:T(8,128)(2,1)S(1)}, u32[]{:S(2)}, u32[]{:S(2)}) collective-permute-start(bf16[8,128,256]{2,1,0:T(8,128)(2,1)S(1)} %pad_maximum_fusion.1), channel_id=1, source_target_pairs={{0,4},{16,28},{32,36},{48,60},{64,68},{80,92},{96,100},{112,124},{... | collective-permute-start | bytes 1572872 | tf_op jit(solution)/shard_map/ppermute | solution.py:45
  37.0 15.6 %collective-permute-start.10 = (bf16[4,128,256]{2,1,0:T(8,128)(2,1)S(1)}, bf16[4,128,256]{2,1,0:T(8,128)(2,1)S(1)}, u32[]{:S(2)}, u32[]{:S(2)}) collective-permute-start(bf16[4,128,256]{2,1,0:T(8,128)(2,1)S(1)} %get-tuple-element.27), channel_id=1, source_target_pairs={{0,16},{16,0},{32,48},{48,32},{64,80},{80,64},{96,112},{112,96},{1... | collective-permute-start | bytes 786440 | tf_op jit(solution)/shard_map/ppermute | solution.py:49
  37.1 15.5 %collective-permute-start.9 = (bf16[4,128,256]{2,1,0:T(8,128)(2,1)S(1)}, bf16[4,128,256]{2,1,0:T(8,128)(2,1)S(1)}, u32[]{:S(2)}, u32[]{:S(2)}) collective-permute-start(bf16[4,128,256]{2,1,0:T(8,128)(2,1)S(1)} %get-tuple-element.29), channel_id=1, source_target_pairs={{0,16},{16,0},{32,48},{48,32},{64,80},{80,64},{96,112},{112,96},{1... | collective-permute-start | bytes 786440 | tf_op jit(solution)/shard_map/ppermute | solution.py:49
  37.7 9.2 %collective-permute-start.12 = (bf16[8,128,256]{2,1,0:T(8,128)(2,1)S(1)}, bf16[8,128,256]{2,1,0:T(8,128)(2,1)S(1)}, u32[]{:S(2)}, u32[]{:S(2)}) collective-permute-start(bf16[8,128,256]{2,1,0:T(8,128)(2,1)S(1)} %pad_maximum_fusion.3), channel_id=1, source_target_pairs={{0,4},{16,28},{32,36},{48,60},{64,68},{80,92},{96,100},{112,124},{... | collective-permute-start | bytes 1572872 | tf_op jit(solution)/shard_map/ppermute | solution.py:45
  39.4 10.6 %collective-permute-start.15 = (bf16[8,128,256]{2,1,0:T(8,128)(2,1)S(1)}, bf16[8,128,256]{2,1,0:T(8,128)(2,1)S(1)}, u32[]{:S(2)}, u32[]{:S(2)}) collective-permute-start(bf16[8,128,256]{2,1,0:T(8,128)(2,1)S(1)} %pad_maximum_fusion.4), channel_id=1, source_target_pairs={{0,1},{16,19},{32,33},{48,51},{64,65},{80,83},{96,97},{112,115},{1... | collective-permute-start | bytes 1572872 | tf_op jit(solution)/shard_map/ppermute | solution.py:45
  47.0 8.0 %collective-permute-start.13 = (bf16[2,128,256]{2,1,0:T(8,128)(2,1)S(1)}, bf16[2,128,256]{2,1,0:T(8,128)(2,1)S(1)}, u32[]{:S(2)}, u32[]{:S(2)}) collective-permute-start(bf16[2,128,256]{2,1,0:T(8,128)(2,1)S(1)} %get-tuple-element.25), channel_id=1, source_target_pairs={{0,16},{16,0},{32,48},{48,32},{64,80},{80,64},{96,112},{112,96},{1... | collective-permute-start | bytes 393224 | tf_op jit(solution)/shard_map/ppermute | solution.py:49
  50.0 5.0 %collective-permute-start.16 = (bf16[2,128,256]{2,1,0:T(8,128)(2,1)S(1)}, bf16[2,128,256]{2,1,0:T(8,128)(2,1)S(1)}, u32[]{:S(2)}, u32[]{:S(2)}) collective-permute-start(bf16[2,128,256]{2,1,0:T(8,128)(2,1)S(1)} %get-tuple-element.23), channel_id=1, source_target_pairs={{0,16},{16,0},{32,48},{48,32},{64,80},{80,64},{96,112},{112,96},{1... | collective-permute-start | bytes 393224 | tf_op jit(solution)/shard_map/ppermute | solution.py:49
  50.1 5.0 %collective-permute-start.17 = (bf16[2,128,256]{2,1,0:T(8,128)(2,1)S(1)}, bf16[2,128,256]{2,1,0:T(8,128)(2,1)S(1)}, u32[]{:S(2)}, u32[]{:S(2)}) collective-permute-start(bf16[2,128,256]{2,1,0:T(8,128)(2,1)S(1)} %get-tuple-element.24), channel_id=1, source_target_pairs={{0,4},{16,28},{32,36},{48,60},{64,68},{80,92},{96,100},{112,124},{... | collective-permute-start | bytes 393224 | tf_op jit(solution)/shard_map/ppermute | solution.py:45
  52.6 6.2 %collective-permute-start.18 = (bf16[2,128,256]{2,1,0:T(8,128)(2,1)S(1)}, bf16[2,128,256]{2,1,0:T(8,128)(2,1)S(1)}, u32[]{:S(2)}, u32[]{:S(2)}) collective-permute-start(bf16[2,128,256]{2,1,0:T(8,128)(2,1)S(1)} %get-tuple-element.22), channel_id=1, source_target_pairs={{0,1},{16,19},{32,33},{48,51},{64,65},{80,83},{96,97},{112,115},{1... | collective-permute-start | bytes 393224 | tf_op jit(solution)/shard_map/ppermute | solution.py:45
  61.9 8.3 %collective-permute-start.24 = (f32[128,512]{1,0:T(8,128)S(1)}, f32[128,512]{1,0:T(8,128)S(1)}, u32[]{:S(2)}, u32[]{:S(2)}) collective-permute-start(f32[128,512]{1,0:T(8,128)S(1)} %get-tuple-element.20), channel_id=1, source_target_pairs={{0,16},{16,0},{32,48},{48,32},{64,80},{80,64},{96,112},{112,96},{1... | collective-permute-start | bytes 786440 | tf_op jit(solution)/shard_map/ppermute | solution.py:49
  62.5 8.3 %collective-permute-start.20 = (f32[128,512]{1,0:T(8,128)S(1)}, f32[128,512]{1,0:T(8,128)S(1)}, u32[]{:S(2)}, u32[]{:S(2)}) collective-permute-start(f32[128,512]{1,0:T(8,128)S(1)} %get-tuple-element.16), channel_id=1, source_target_pairs={{0,16},{16,0},{32,48},{48,32},{64,80},{80,64},{96,112},{112,96},{1... | collective-permute-start | bytes 786440 | tf_op jit(solution)/shard_map/ppermute | solution.py:49
  62.6 8.5 %collective-permute-start.22 = (f32[128,512]{1,0:T(8,128)S(1)}, f32[128,512]{1,0:T(8,128)S(1)}, u32[]{:S(2)}, u32[]{:S(2)}) collective-permute-start(f32[128,512]{1,0:T(8,128)S(1)} %add.13), channel_id=1, source_target_pairs={{0,32},{16,112},{32,64},{48,16},{64,96},{80,48},{96,0},{112,80},{1... | collective-permute-start | bytes 786440 | tf_op jit(solution)/shard_map/ppermute | solution.py:45
  66.2 6.4 %collective-permute-start.19 = (f32[128,512]{1,0:T(8,128)S(1)}, f32[128,512]{1,0:T(8,128)S(1)}, u32[]{:S(2)}, u32[]{:S(2)}) collective-permute-start(f32[128,512]{1,0:T(8,128)S(1)} %get-tuple-element.14), channel_id=1, source_target_pairs={{0,16},{16,0},{32,48},{48,32},{64,80},{80,64},{96,112},{112,96},{1... | collective-permute-start | bytes 786440 | tf_op jit(solution)/shard_map/ppermute | solution.py:49
  70.3 8.5 %collective-permute-start.25 = (f32[128,512]{1,0:T(8,128)S(1)}, f32[128,512]{1,0:T(8,128)S(1)}, u32[]{:S(2)}, u32[]{:S(2)}) collective-permute-start(f32[128,512]{1,0:T(8,128)S(1)} %add.15), channel_id=1, source_target_pairs={{0,96},{16,48},{32,0},{48,80},{64,32},{80,112},{96,64},{112,16},{1... | collective-permute-start | bytes 786440 | tf_op jit(solution)/shard_map/ppermute | solution.py:45
  71.2 8.7 %collective-permute-start.23 = (f32[128,512]{1,0:T(8,128)S(1)}, f32[128,512]{1,0:T(8,128)S(1)}, u32[]{:S(2)}, u32[]{:S(2)}) collective-permute-start(f32[128,512]{1,0:T(8,128)S(1)} %add_add_fusion), channel_id=1, source_target_pairs={{0,32},{16,112},{32,64},{48,16},{64,96},{80,48},{96,0},{112,80},{1... | collective-permute-start | bytes 786440 | tf_op jit(solution)/shard_map/ppermute | solution.py:45
  (8 other events, 18.4 us)

commit v3 on v2

--- a/solution.py
+++ b/solution.py
@@ -6,6 +6,7 @@
 from jax.experimental import pallas as pl
 from jax.experimental.pallas import tpu as pltpu
 from jax.sharding import PartitionSpec as P
+
 
 SIDE = 4
 TILE = 256
@@ -111,10 +112,11 @@
 
 
 def mm_kernel(*refs, tiles, arrays, group, blocks, start):
+    n = len(blocks)
     a_ref, refs = refs[0], refs[1:]
     if not start:
-        acc_ref, refs = refs[0], refs[1:]
-    f_refs, outs = refs[:arrays], refs[arrays:]
+        accs, refs = refs[:n], refs[n:]
+    f_refs, outs, rest = refs[:arrays], refs[arrays : arrays + n], refs[arrays + n :]
     x, y, z, core, s = here()
     home = {}
     for t in tiles:
@@ -122,59 +124,45 @@
             (a, b), (c, d) = t[2:4]
             home[t[2:4]] = (((x + a * s + 2 * b) & 3) * SIDE + ((y + c * s + 2 * d) & 3)) * TILES
     where = [home[t[2:4]] + t[4] for t in tiles]
-
-    if blocks is not None:
-        f = jnp.concatenate([f_refs[t[0]][t[1]] for t in tiles], 1)
-        for out, (a, b, other) in zip(outs, blocks):
-            r = ((z + a * s + 2 * b) & 3) * 2 + (1 - core if other else core)
-            out[...] = acc_ref[r] + jnp.dot(f, expand(a_ref, r, where), preferred_element_type=jnp.float32)
-        return
+    rows = [((z + a * s + 2 * b) & 3) * 2 + (1 - core if other else core) for a, b, other in blocks]
 
     if len(tiles) == group:
         f = jnp.concatenate([f_refs[t[0]][t[1]] for t in tiles], 1)
-        for r in range(8):
-            got = jnp.dot(f, expand(a_ref, r, where), preferred_element_type=jnp.float32)
-            outs[0][r] = got if start else outs[0][r] + got
+        for k in range(n):
+            got = jnp.dot(f, expand(a_ref, rows[k], where), preferred_element_type=jnp.float32)
+            outs[k][...] = got if start else accs[k][...] + got
         return
 
-    out, scr, at = outs
-    for n, t in enumerate(tiles):
-        scr[n] = f_refs[t[0]][t[1]]
-        at[n] = where[n]
+    scr, at = rest
+    for k, t in enumerate(tiles):
+        scr[k] = f_refs[t[0]][t[1]]
+        at[k] = where[k]
 
     def step(i, carry):
         base = i * group
         f = jnp.concatenate([scr[base + t] for t in range(group)], 1)
-        for r in range(8):
-            rhs = expand(a_ref, r, [at[base + t] for t in range(group)])
-            out[r] = out[r] + jnp.dot(f, rhs, preferred_element_type=jnp.float32)
+        for k in range(n):
+            rhs = expand(a_ref, rows[k], [at[base + t] for t in range(group)])
+            outs[k][...] = outs[k][...] + jnp.dot(f, rhs, preferred_element_type=jnp.float32)
         return carry
 
     lax.fori_loop(0, len(tiles) // group, step, 0)
 
 
-def mm(ab, acc, arrays, tiles, group, blocks=None):
-    count = len(tiles)
-    if blocks is None:
-        out_shape = VM((8, 128, 512), jnp.float32)
-        out_specs = FULL
-        lanes = 4096
-    else:
-        out_shape = (VM((128, 512), jnp.float32),) * len(blocks)
-        out_specs = (FULL,) * len(blocks)
-        lanes = 512 * len(blocks)
-    args = [ab] + ([acc] if acc is not None else []) + list(arrays)
-    loop = blocks is None and count != group
+def mm(ab, accs, arrays, tiles, group, blocks):
+    count, n = len(tiles), len(blocks)
+    args = [ab] + list(accs or []) + list(arrays)
+    loop = count != group
     return pl.pallas_call(
         functools.partial(
-            mm_kernel, tiles=tuple(tiles), arrays=len(arrays), group=group, blocks=blocks, start=acc is None
+            mm_kernel, tiles=tuple(tiles), arrays=len(arrays), group=group, blocks=tuple(blocks), start=not accs
         ),
-        out_shape=out_shape,
+        out_shape=(VM((128, 512), jnp.float32),) * n,
         in_specs=[FULL] * len(args),
-        out_specs=out_specs,
+        out_specs=(FULL,) * n,
         scratch_shapes=[pltpu.VMEM((count, 128, TILE), jnp.bfloat16), pltpu.SMEM((count,), jnp.int32)] if loop else [],
-        input_output_aliases={1: 0} if blocks is None and acc is not None else {},
-        cost_estimate=pl.CostEstimate(flops=2 * 128 * TILE * count * lanes, bytes_accessed=0, transcendentals=0),
+        input_output_aliases={1 + k: k for k in range(n)} if accs else {},
+        cost_estimate=pl.CostEstimate(flops=2 * 128 * TILE * count * 512 * n, bytes_accessed=0, transcendentals=0),
         compiler_params=pltpu.CompilerParams(vmem_limit_bytes=32 << 20),
         name="bits_mm",
     )(*args)
@@ -203,7 +191,7 @@
         in_specs=[FULL] * 5,
         out_specs=(FULL, FULL),
         name="finish",
-    )(*parts, visited)
+    )(*[pltpu.with_memory_space_constraint(v, VM) for v in (*parts, visited)])
 
 
 O, M, Q, T = (0, 0), (-1, 0), (1, 0), (0, 1)
@@ -214,65 +202,68 @@
     return [(array, start + n, dx, dy, j) for n, j in enumerate(js)]
 
 
+TWO, TWO_O, UP_O, DOWN_O = (0, 1, False), (0, 1, True), (-1, 0, True), (1, 0, True)
+UP, DOWN, OWN, OWN_O = (1, 0, False), (-1, 0, False), (0, 0, False), (0, 0, True)
+EVERY = (TWO, TWO_O, UP_O, DOWN_O, UP, DOWN, OWN, OWN_O)
+
+
 def level(adjacency, frontier, visited):
+    totals = {}
+
+    def work(arrays, tiles, blocks, group):
+        accs = [totals[b] for b in blocks if b in totals]
+        got = mm(ab, accs, arrays, tiles, group, blocks)
+        totals.update(zip(blocks, got))
+
     ft = prep(frontier)
     mine = jnp.concatenate([ft, swap(ft)], 0)
     dx = send(mine, "x")
     dy = send(mine, "y")
     ab, seen = split(adjacency, visited)
-    acc = mm(ab, None, [ft], tiles(0, 0, O, O, ALL), 4)
-
+
+    px, py = swap(dx), swap(dy)
     bx = send(dx[:4], "x")
     by = send(dy[:4], "y")
-    px, py = swap(dx), swap(dy)
+    work([ft], tiles(0, 0, O, O, ALL), EVERY, 4)
     cx = send(jnp.concatenate([dy[2:4], py[6:8], dy[6:8], py[2:4]], 0), "x")
     cy = send(jnp.concatenate([dx[0:2], px[4:6], dx[4:6], px[0:2]], 0), "y")
-    near_tiles = (
-        tiles(0, 0, M, O, ALL) + tiles(1, 4, Q, O, ALL) + tiles(2, 0, O, M, ALL) + tiles(3, 4, O, Q, ALL)
-    )
-    acc = mm(ab, acc, [dx, px, dy, py], near_tiles, 8)
+    work([dx, dy], tiles(0, 0, M, O, ALL) + tiles(1, 0, O, M, ALL), EVERY, 8)
 
     pbx, pby = swap(bx[0:2]), swap(by[2:4])
-    ex = send(jnp.concatenate([by[2:4], pby, cx[:4]], 0), "x")
-    ey = send(jnp.concatenate([bx[0:2], pbx, cy[:4]], 0), "y")
+    work([px, py], tiles(0, 4, Q, O, ALL) + tiles(1, 4, O, Q, ALL), EVERY, 8)
+    ex = send(jnp.concatenate([by[2:4], pby], 0), "x")
+    ey = send(jnp.concatenate([bx[0:2], pbx], 0), "y")
+    hx, hy = send(cx[:4], "x"), send(cy[:4], "y")
     pcx, pcy = swap(cx[4:8]), swap(cy[4:8])
-    far_tiles = (
-        tiles(0, 0, T, O, ALL)
-        + tiles(1, 0, O, T, ALL)
-        + tiles(2, 0, M, M, H1)
-        + tiles(2, 2, M, Q, H1)
-        + tiles(3, 0, M, M, H0)
-        + tiles(3, 2, Q, M, H0)
-    )
-    acc = mm(ab, acc, [bx, by, cx, cy], far_tiles, 8)
+    work([bx, by], tiles(0, 0, T, O, ALL) + tiles(1, 0, O, T, ALL), EVERY, 8)
 
     gx, gy = send(ex[:2], "x"), send(ey[:2], "y")
     pex, pey = swap(ex[2:4]), swap(ey[2:4])
-    side_tiles = tiles(0, 0, Q, Q, H1) + tiles(0, 2, Q, M, H1) + tiles(1, 0, Q, Q, H0) + tiles(1, 2, M, Q, H0)
-    acc = mm(ab, acc, [pcx, pcy], side_tiles, 8)
-
-    last = [ex, pex, ey, pey, gx, gy]
-    last_tiles = (
-        tiles(0, 0, M, T, H1)
-        + tiles(1, 0, Q, T, H1)
-        + tiles(0, 4, T, M, H1)
-        + tiles(0, 6, T, Q, H1)
-        + tiles(2, 0, T, M, H0)
-        + tiles(3, 0, T, Q, H0)
-        + tiles(2, 4, M, T, H0)
-        + tiles(2, 6, Q, T, H0)
-        + tiles(4, 0, T, T, H1)
-        + tiles(5, 0, T, T, H0)
-    )
-    done = lambda *blocks: mm(ab, acc, last, last_tiles, 20, blocks)
-    two, two_o = done((0, 1, False), (0, 1, True))
-    up_o, down_o = done((-1, 0, True), (1, 0, True))
-    up, down = done((1, 0, False), (-1, 0, False))
-    own, own_o = done((0, 0, False), (0, 0, True))
-    hop = send(two + swap(two_o), "z")
-    got0 = send(down + swap(down_o), "z", True)
-    got1 = send(up + swap(up_o) + hop, "z")
-    return finish([own, swap(own_o), got1, got0], seen)
+
+    late = [cx, cy, pcx, pcy, ex, ey, pex, pey, hx, hy, gx, gy]
+    fb = tiles(0, 0, M, M, H1) + tiles(0, 2, M, Q, H1) + tiles(1, 0, M, M, H0) + tiles(1, 2, Q, M, H0)
+    sd = tiles(2, 0, Q, Q, H1) + tiles(2, 2, Q, M, H1) + tiles(3, 0, Q, Q, H0) + tiles(3, 2, M, Q, H0)
+    sd = sd + tiles(4, 0, M, T, H1) + tiles(5, 0, T, M, H0) + tiles(6, 0, Q, T, H1) + tiles(7, 0, T, Q, H0)
+    la = tiles(8, 0, T, M, H1) + tiles(8, 2, T, Q, H1) + tiles(9, 0, M, T, H0) + tiles(9, 2, Q, T, H0)
+    la = la + tiles(10, 0, T, T, H1) + tiles(11, 0, T, T, H0)
+
+    def late_work(tiles, blocks, group):
+        used = sorted({t[0] for t in tiles})
+        work([late[n] for n in used], [(used.index(t[0]),) + t[1:] for t in tiles], blocks, group)
+
+    first = EVERY[:4]
+    late_work(fb, first, 8)
+    late_work(sd, first, 8)
+    late_work(la, (TWO, TWO_O), 12)
+    late_work(la, (UP_O, DOWN_O), 12)
+    late_work(fb + sd + la, (UP, DOWN), 36)
+    late_work(fb + sd + la, (OWN, OWN_O), 36)
+
+    hop = send(totals[TWO] + swap(totals[TWO_O]), "z")
+    got0 = send(totals[DOWN] + swap(totals[DOWN_O]), "z", True)
+    got1 = send(totals[UP] + swap(totals[UP_O]) + hop, "z")
+    rest = swap(totals[OWN_O])
+    return finish([totals[OWN], rest, got1, got0], seen)
 
 
 def solution(mesh):

time: 83 us -> 79.4 us (0.957)
  the two profiles are of different devices: /device:TPU:2 before, /device:TPU:1 now
where the time goes in v3:
time: 79.4 us; the launch traced here: 78.6 us
  starting transfers between devices  31 us (39%)
  Pallas kernels  29.4 us (37%)
  waiting for transfers between devices  16 us (20%)
  local copies, waits for them, and re-layouts  0.93 us (1%)
  between operations  0.93 us (1%)
    pallas_call x10, Pallas kernels, mm(): pl.pallas_call(functools.partial(mm_kernel, tiles=tuple(tiles), arrays=le...  20.2 us
    ppermute x15, starting transfers between devices, send(): return lax.ppermute(value, AXES, pairs(axis, flip))  20 us
    ppermute x15, waiting for transfers between devices, send(): return lax.ppermute(value, AXES, pairs(axis, flip))  14.8 us
    ppermute x13, starting transfers between devices, swap(): return lax.ppermute(value, AXES, pairs('core'))  11 us
    pallas_call x1, Pallas kernels, split(): pl.pallas_call(split_kernel, grid=(d // 512,), in_specs=[pl.BlockSpec((51...  6.98 us
  transfers between devices with their start and end apart: 28, of which 6 were waited for; matrix products, arithmetic and copies ran while one was open for 1% of the time, Pallas kernels for 33%

profile of v3, /device:TPU:1, one launch (start us, length us, event | category | flops | bytes accessed | tf_op | source)
XLA Modules:
  0.0 78.6 jit_solution(2683435346238931907)
XLA Ops:
  0.6 1.3 %prep.1.refs_1_ = bf16[4,128,256]{2,1,0:T(8,128)(2,1)S(1)} custom-call(bf16[1024,128]{1,0:T(8,128)(2,1)} %f_ref.1), custom_call_target="tpu_custom_call" | custom-call | tf_op jit(solution)/shard_map/prep/pallas_call | solution.py:64
  2.0 1.5 %collective-permute-start = (bf16[4,128,256]{2,1,0:T(8,128)(2,1)S(1)}, bf16[4,128,256]{2,1,0:T(8,128)(2,1)S(1)}, u32[]{:S(2)}, u32[]{:S(2)}) collective-permute-start(bf16[4,128,256]{2,1,0:T(8,128)(2,1)S(1)} %prep.1.refs_1_), channel_id=1, source_target_pairs={{0,16},{16,0},{32,48},{48,32},{64,80},{80,64},{96,112},{112,96},{1... | collective-permute-start | bytes 786440 | tf_op jit(solution)/shard_map/ppermute | solution.py:50
  4.7 2.7 %collective-permute-start.1 = (bf16[8,128,256]{2,1,0:T(8,128)(2,1)S(1)}, bf16[8,128,256]{2,1,0:T(8,128)(2,1)S(1)}, u32[]{:S(2)}, u32[]{:S(2)}) collective-permute-start(bf16[8,128,256]{2,1,0:T(8,128)(2,1)S(1)} %pad_maximum_fusion), channel_id=1, source_target_pairs={{0,4},{16,28},{32,36},{48,60},{64,68},{80,92},{96,100},{112,124},{... | collective-permute-start | bytes 1572872 | tf_op jit(solution)/shard_map/ppermute | solution.py:46
  7.3 2.7 %collective-permute-start.2 = (bf16[8,128,256]{2,1,0:T(8,128)(2,1)S(1)}, bf16[8,128,256]{2,1,0:T(8,128)(2,1)S(1)}, u32[]{:S(2)}, u32[]{:S(2)}) collective-permute-start(bf16[8,128,256]{2,1,0:T(8,128)(2,1)S(1)} %pad_maximum_fusion), channel_id=1, source_target_pairs={{0,1},{16,19},{32,33},{48,51},{64,65},{80,83},{96,97},{112,115},{1... | collective-permute-start | bytes 1572872 | tf_op jit(solution)/shard_map/ppermute | solution.py:46
  10.7 7.0 %split.1 = (s8[8,64,32,512]{3,2,1,0:T(32,128)(4,1)S(1)}, s32[4,512]{1,0:T(4,128)S(1)}) custom-call(s32[4096,512]{1,0:T(8,128)} %a_ref.1, s32[4,512]{1,0:T(4,128)S(1)} %copy-done), custom_call_target="tpu_custom_call" | custom-call | tf_op jit(solution)/shard_map/split/pallas_call | solution.py:87
  20.8 4.5 %collective-permute-done.6.refs_10_ = bf16[4,128,256]{2,1,0:T(8,128)(2,1)S(1)} collective-permute-done((bf16[4,128,256]{2,1,0:T(8,128)(2,1)S(1)}, bf16[4,128,256]{2,1,0:T(8,128)(2,1)S(1)}, u32[]{:S(2)}, u32[]{:S(2)}) %collective-permute-start.6) | collective-permute-done | bytes 262176 | tf_op jit(solution)/shard_map/ppermute | solution.py:46
  25.3 1.3 %collective-permute-start.11 = (bf16[2,128,256]{2,1,0:T(8,128)(2,1)S(1)}, bf16[2,128,256]{2,1,0:T(8,128)(2,1)S(1)}, u32[]{:S(2)}, u32[]{:S(2)}) collective-permute-start(bf16[2,128,256]{2,1,0:T(8,128)(2,1)S(1)} %slice.94), channel_id=1, source_target_pairs={{0,16},{16,0},{32,48},{48,32},{64,80},{80,64},{96,112},{112,96},{1... | collective-permute-start | bytes 393224 | tf_op jit(solution)/shard_map/ppermute | solution.py:50
  26.7 2.5 %bits_mm.11 = (f32[128,512]{1,0:T(8,128)S(1)}, f32[128,512]{1,0:T(8,128)S(1)}, f32[128,512]{1,0:T(8,128)S(1)}, f32[128,512]{1,0:T(8,128)S(1)}, f32[128,512]{1,0:...) custom-call(s8[8,64,32,512]{3,2,1,0:T(32,128)(4,1)S(1)} %get-tuple-e, ...), custom_call_target="tpu_custom_call", output_to_operand_aliasing={{0}: (1, {}), {1}: (2, {}), {2}: (3, {}), {3}: (4, {}), {4}... | custom-call | flops 2147483648 | tf_op jit(solution)/shard_map/bits_mm/pallas_call | solution.py:156
  29.3 1.5 %collective-permute-start.12 = (bf16[4,128,256]{2,1,0:T(8,128)(2,1)S(1)}, bf16[4,128,256]{2,1,0:T(8,128)(2,1)S(1)}, u32[]{:S(2)}, u32[]{:S(2)}) collective-permute-start(bf16[4,128,256]{2,1,0:T(8,128)(2,1)S(1)} %pad_maximum_fusion.3), channel_id=1, source_target_pairs={{0,4},{16,28},{32,36},{48,60},{64,68},{80,92},{96,100},{112,124},{... | collective-permute-start | bytes 786440 | tf_op jit(solution)/shard_map/ppermute | solution.py:46
  31.6 1.7 %collective-permute-start.8 = (bf16[8,128,256]{2,1,0:T(8,128)(2,1)S(1)}, bf16[8,128,256]{2,1,0:T(8,128)(2,1)S(1)}, u32[]{:S(2)}, u32[]{:S(2)}) collective-permute-start(bf16[8,128,256]{2,1,0:T(8,128)(2,1)S(1)} %pad_maximum_fusion.2), channel_id=1, source_target_pairs={{0,1},{16,19},{32,33},{48,51},{64,65},{80,83},{96,97},{112,115},{1... | collective-permute-start | bytes 1572872 | tf_op jit(solution)/shard_map/ppermute | solution.py:46
  33.3 2.5 %bits_mm.12 = (f32[128,512]{1,0:T(8,128)S(1)}, f32[128,512]{1,0:T(8,128)S(1)}, f32[128,512]{1,0:T(8,128)S(1)}, f32[128,512]{1,0:T(8,128)S(1)}, f32[128,512]{1,0:...) custom-call(s8[8,64,32,512]{3,2,1,0:T(32,128)(4,1)S(1)} %get-tuple-e, ...), custom_call_target="tpu_custom_call", output_to_operand_aliasing={{0}: (1, {}), {1}: (2, {}), {2}: (3, {}), {3}: (4, {}), {4}... | custom-call | flops 2147483648 | tf_op jit(solution)/shard_map/bits_mm/pallas_call | solution.py:156
  35.8 1.9 %collective-permute-start.15 = (bf16[2,128,256]{2,1,0:T(8,128)(2,1)S(1)}, bf16[2,128,256]{2,1,0:T(8,128)(2,1)S(1)}, u32[]{:S(2)}, u32[]{:S(2)}) collective-permute-start(bf16[2,128,256]{2,1,0:T(8,128)(2,1)S(1)} %get-tuple-element.117), channel_id=1, source_target_pairs={{0,16},{16,0},{32,48},{48,32},{64,80},{80,64},{96,112},{112,96},{1... | collective-permute-start | bytes 393224 | tf_op jit(solution)/shard_map/ppermute | solution.py:50
  38.9 3.2 %collective-permute-done.8.refs_4_.refs_6_ = bf16[8,128,256]{2,1,0:T(8,128)(2,1)S(1)} collective-permute-done((bf16[8,128,256]{2,1,0:T(8,128)(2,1)S(1)}, bf16[8,128,256]{2,1,0:T(8,128)(2,1)S(1)}, u32[]{:S(2)}, u32[]{:S(2)}) %collective-permute-start.8) | collective-permute-done | bytes 524320 | tf_op jit(solution)/shard_map/ppermute | solution.py:46
  42.1 2.4 %collective-permute-start.10 = (bf16[4,128,256]{2,1,0:T(8,128)(2,1)S(1)}, bf16[4,128,256]{2,1,0:T(8,128)(2,1)S(1)}, u32[]{:S(2)}, u32[]{:S(2)}) collective-permute-start(bf16[4,128,256]{2,1,0:T(8,128)(2,1)S(1)} %get-tuple-element.103), channel_id=1, source_target_pairs={{0,16},{16,0},{32,48},{48,32},{64,80},{80,64},{96,112},{112,96},{1... | collective-permute-start | bytes 786440 | tf_op jit(solution)/shard_map/ppermute | solution.py:50
  44.6 2.5 %bits_mm.13 = (f32[128,512]{1,0:T(8,128)S(1)}, f32[128,512]{1,0:T(8,128)S(1)}, f32[128,512]{1,0:T(8,128)S(1)}, f32[128,512]{1,0:T(8,128)S(1)}, f32[128,512]{1,0:...) custom-call(s8[8,64,32,512]{3,2,1,0:T(32,128)(4,1)S(1)} %get-tuple-e, ...), custom_call_target="tpu_custom_call", output_to_operand_aliasing={{0}: (1, {}), {1}: (2, {}), {2}: (3, {}), {3}: (4, {}), {4}... | custom-call | flops 2147483648 | tf_op jit(solution)/shard_map/bits_mm/pallas_call | solution.py:156
  47.2 1.8 %collective-permute-start.17 = (bf16[4,128,256]{2,1,0:T(8,128)(2,1)S(1)}, bf16[4,128,256]{2,1,0:T(8,128)(2,1)S(1)}, u32[]{:S(2)}, u32[]{:S(2)}) collective-permute-start(bf16[4,128,256]{2,1,0:T(8,128)(2,1)S(1)} %get-tuple-element.104), channel_id=1, source_target_pairs={{0,4},{16,28},{32,36},{48,60},{64,68},{80,92},{96,100},{112,124},{... | collective-permute-start | bytes 786440 | tf_op jit(solution)/shard_map/ppermute | solution.py:46
  49.5 1.3 %bits_mm.16 = (f32[128,512]{1,0:T(8,128)S(1)}, f32[128,512]{1,0:T(8,128)S(1)}, f32[128,512]{1,0:T(8,128)S(1)}, f32[128,512]{1,0:T(8,128)S(1)}) custom-call(s8[8,64,32,512]{3,2,1,0:T(32,128)(4,1)S(1)} %get-tuple-element.52.refs_0_, f32[128,512]{1,0:T(8,128)S(1)} %get-tuple-element.84.refs_1_, ...), custom_call_target="tpu_custom_call", output_to_operand_aliasing={{0}: (1, {}), {1}: (2, {}), {2}: (3, {}), {3}: (4, {})} | custom-call | flops 1073741824 | tf_op jit(solution)/shard_map/bits_mm/pallas_call | solution.py:156
  51.5 2.6 %bits_mm.17 = (f32[128,512]{1,0:T(8,128)S(1)}, f32[128,512]{1,0:T(8,128)S(1)}, f32[128,512]{1,0:T(8,128)S(1)}, f32[128,512]{1,0:T(8,128)S(1)}) custom-call(s8[8,64,32,512]{3,2,1,0:T(32,128)(4,1)S(1)} %get-tuple-element.52.refs_0_, f32[128,512]{1,0:T(8,128)S(1)} %get-tuple-element.88.refs_1_, ...), custom_call_target="tpu_custom_call", output_to_operand_aliasing={{0}: (1, {}), {1}: (2, {}), {2}: (3, {}), {3}: (4, {})} | custom-call | flops 2147483648 | tf_op jit(solution)/shard_map/bits_mm/pallas_call | solution.py:156
  57.0 1.5 %collective-permute-start.23 = (f32[128,512]{1,0:T(8,128)S(1)}, f32[128,512]{1,0:T(8,128)S(1)}, u32[]{:S(2)}, u32[]{:S(2)}) collective-permute-start(f32[128,512]{1,0:T(8,128)S(1)} %get-tuple-element.98), channel_id=1, source_target_pairs={{0,16},{16,0},{32,48},{48,32},{64,80},{80,64},{96,112},{112,96},{1... | collective-permute-start | bytes 786440 | tf_op jit(solution)/shard_map/ppermute | solution.py:50
  60.1 4.1 %collective-permute-start.24 = (f32[128,512]{1,0:T(8,128)S(1)}, f32[128,512]{1,0:T(8,128)S(1)}, u32[]{:S(2)}, u32[]{:S(2)}) collective-permute-start(f32[128,512]{1,0:T(8,128)S(1)} %add.13), channel_id=1, source_target_pairs={{0,32},{16,112},{32,64},{48,16},{64,96},{80,48},{96,0},{112,80},{1... | collective-permute-start | bytes 786440 | tf_op jit(solution)/shard_map/ppermute | solution.py:46
  64.2 2.6 %bits_mm.14 = (f32[128,512]{1,0:T(8,128)S(1)}, f32[128,512]{1,0:T(8,128)S(1)}) custom-call(s8[8,64,32,512]{3,2,1,0:T(32,128)(4,1)S(1)} %get-tuple-element.52.refs_0_, f32[128,512]{1,0:T(8,128)S(1)} %get-tuple-element.77.refs_1_, f32[128,512]{1,0:T(8,128)S(1)} %get-tuple-element.78.refs_2_, ...), custom_call_target="tpu_custom_call", output_to_operand_aliasing={{0}: (1, {}), {1}: (2, {})} | custom-call | flops 2415919104 | tf_op jit(solution)/shard_map/bits_mm/pallas_call | solution.py:156
  66.9 2.7 %bits_mm.15 = (f32[128,512]{1,0:T(8,128)S(1)}, f32[128,512]{1,0:T(8,128)S(1)}) custom-call(s8[8,64,32,512]{3,2,1,0:T(32,128)(4,1)S(1)} %get-tuple-element.52.refs_0_, f32[128,512]{1,0:T(8,128)S(1)} %get-tuple-element.81.refs_1_, f32[128,512]{1,0:T(8,128)S(1)} %get-tuple-element.82.refs_2_, ...), custom_call_target="tpu_custom_call", output_to_operand_aliasing={{0}: (1, {}), {1}: (2, {})} | custom-call | flops 2415919104 | tf_op jit(solution)/shard_map/bits_mm/pallas_call | solution.py:156
  69.8 2.7 %collective-permute-start.25 = (f32[128,512]{1,0:T(8,128)S(1)}, f32[128,512]{1,0:T(8,128)S(1)}, u32[]{:S(2)}, u32[]{:S(2)}) collective-permute-start(f32[128,512]{1,0:T(8,128)S(1)} %add_add_fusion), channel_id=1, source_target_pairs={{0,32},{16,112},{32,64},{48,16},{64,96},{80,48},{96,0},{112,80},{1... | collective-permute-start | bytes 786440 | tf_op jit(solution)/shard_map/ppermute | solution.py:46
  72.5 5.2 %collective-permute-done.27.d_ref = f32[128,512]{1,0:T(8,128)S(1)} collective-permute-done((f32[128,512]{1,0:T(8,128)S(1)}, f32[128,512]{1,0:T(8,128)S(1)}, u32[]{:S(2)}, u32[]{:S(2)}) %collective-permute-start.27) | collective-permute-done | bytes 262176 | tf_op jit(solution)/shard_map/ppermute | solution.py:46
  (67 shorter events, 13.8 us)
Async XLA Ops:
  4.7 14.4 %collective-permute-start.1 = (bf16[8,128,256]{2,1,0:T(8,128)(2,1)S(1)}, bf16[8,128,256]{2,1,0:T(8,128)(2,1)S(1)}, u32[]{:S(2)}, u32[]{:S(2)}) collective-permute-start(bf16[8,128,256]{2,1,0:T(8,128)(2,1)S(1)} %pad_maximum_fusion), channel_id=1, source_target_pairs={{0,4},{16,28},{32,36},{48,60},{64,68},{80,92},{96,100},{112,124},{... | collective-permute-start | bytes 1572872 | tf_op jit(solution)/shard_map/ppermute | solution.py:46
  7.3 12.4 %collective-permute-start.2 = (bf16[8,128,256]{2,1,0:T(8,128)(2,1)S(1)}, bf16[8,128,256]{2,1,0:T(8,128)(2,1)S(1)}, u32[]{:S(2)}, u32[]{:S(2)}) collective-permute-start(bf16[8,128,256]{2,1,0:T(8,128)(2,1)S(1)} %pad_maximum_fusion), channel_id=1, source_target_pairs={{0,1},{16,19},{32,33},{48,51},{64,65},{80,83},{96,97},{112,115},{1... | collective-permute-start | bytes 1572872 | tf_op jit(solution)/shard_map/ppermute | solution.py:46
  19.1 7.6 %collective-permute-start.5 = (bf16[4,128,256]{2,1,0:T(8,128)(2,1)S(1)}, bf16[4,128,256]{2,1,0:T(8,128)(2,1)S(1)}, u32[]{:S(2)}, u32[]{:S(2)}) collective-permute-start(bf16[4,128,256]{2,1,0:T(8,128)(2,1)S(1)} %slice.82), channel_id=1, source_target_pairs={{0,4},{16,28},{32,36},{48,60},{64,68},{80,92},{96,100},{112,124},{... | collective-permute-start | bytes 786440 | tf_op jit(solution)/shard_map/ppermute | solution.py:46
  19.7 5.6 %collective-permute-start.6 = (bf16[4,128,256]{2,1,0:T(8,128)(2,1)S(1)}, bf16[4,128,256]{2,1,0:T(8,128)(2,1)S(1)}, u32[]{:S(2)}, u32[]{:S(2)}) collective-permute-start(bf16[4,128,256]{2,1,0:T(8,128)(2,1)S(1)} %slice.83), channel_id=1, source_target_pairs={{0,1},{16,19},{32,33},{48,51},{64,65},{80,83},{96,97},{112,115},{1... | collective-permute-start | bytes 786440 | tf_op jit(solution)/shard_map/ppermute | solution.py:46
  20.2 11.2 %collective-permute-start.3 = (bf16[8,128,256]{2,1,0:T(8,128)(2,1)S(1)}, bf16[8,128,256]{2,1,0:T(8,128)(2,1)S(1)}, u32[]{:S(2)}, u32[]{:S(2)}) collective-permute-start(bf16[8,128,256]{2,1,0:T(8,128)(2,1)S(1)} %collective-permute-done.1.refs_9_), channel_id=1, source_target_pairs={{0,16},{16,0},{32,48},{48,32},{64,80},{80,64},{96,112},{112,96},{1... | collective-permute-start | bytes 1572872 | tf_op jit(solution)/shard_map/ppermute | solution.py:50
  20.5 10.6 %collective-permute-start.4 = (bf16[8,128,256]{2,1,0:T(8,128)(2,1)S(1)}, bf16[8,128,256]{2,1,0:T(8,128)(2,1)S(1)}, u32[]{:S(2)}, u32[]{:S(2)}) collective-permute-start(bf16[8,128,256]{2,1,0:T(8,128)(2,1)S(1)} %collective-permute-done.2.refs_10_), channel_id=1, source_target_pairs={{0,16},{16,0},{32,48},{48,32},{64,80},{80,64},{96,112},{112,96},{1... | collective-permute-start | bytes 1572872 | tf_op jit(solution)/shard_map/ppermute | solution.py:50
  26.6 4.2 %collective-permute-start.13 = (bf16[2,128,256]{2,1,0:T(8,128)(2,1)S(1)}, bf16[2,128,256]{2,1,0:T(8,128)(2,1)S(1)}, u32[]{:S(2)}, u32[]{:S(2)}) collective-permute-start(bf16[2,128,256]{2,1,0:T(8,128)(2,1)S(1)} %slice.95), channel_id=1, source_target_pairs={{0,16},{16,0},{32,48},{48,32},{64,80},{80,64},{96,112},{112,96},{1... | collective-permute-start | bytes 393224 | tf_op jit(solution)/shard_map/ppermute | solution.py:50
  29.3 6.5 %collective-permute-start.12 = (bf16[4,128,256]{2,1,0:T(8,128)(2,1)S(1)}, bf16[4,128,256]{2,1,0:T(8,128)(2,1)S(1)}, u32[]{:S(2)}, u32[]{:S(2)}) collective-permute-start(bf16[4,128,256]{2,1,0:T(8,128)(2,1)S(1)} %pad_maximum_fusion.3), channel_id=1, source_target_pairs={{0,4},{16,28},{32,36},{48,60},{64,68},{80,92},{96,100},{112,124},{... | collective-permute-start | bytes 786440 | tf_op jit(solution)/shard_map/ppermute | solution.py:46
  30.9 6.8 %collective-permute-start.14 = (bf16[4,128,256]{2,1,0:T(8,128)(2,1)S(1)}, bf16[4,128,256]{2,1,0:T(8,128)(2,1)S(1)}, u32[]{:S(2)}, u32[]{:S(2)}) collective-permute-start(bf16[4,128,256]{2,1,0:T(8,128)(2,1)S(1)} %pad_maximum_fusion.4), channel_id=1, source_target_pairs={{0,1},{16,19},{32,33},{48,51},{64,65},{80,83},{96,97},{112,115},{1... | collective-permute-start | bytes 786440 | tf_op jit(solution)/shard_map/ppermute | solution.py:46
  31.2 13.3 %collective-permute-start.7 = (bf16[8,128,256]{2,1,0:T(8,128)(2,1)S(1)}, bf16[8,128,256]{2,1,0:T(8,128)(2,1)S(1)}, u32[]{:S(2)}, u32[]{:S(2)}) collective-permute-start(bf16[8,128,256]{2,1,0:T(8,128)(2,1)S(1)} %pad_maximum_fusion.1), channel_id=1, source_target_pairs={{0,4},{16,28},{32,36},{48,60},{64,68},{80,92},{96,100},{112,124},{... | collective-permute-start | bytes 1572872 | tf_op jit(solution)/shard_map/ppermute | solution.py:46
  31.6 10.5 %collective-permute-start.8 = (bf16[8,128,256]{2,1,0:T(8,128)(2,1)S(1)}, bf16[8,128,256]{2,1,0:T(8,128)(2,1)S(1)}, u32[]{:S(2)}, u32[]{:S(2)}) collective-permute-start(bf16[8,128,256]{2,1,0:T(8,128)(2,1)S(1)} %pad_maximum_fusion.2), channel_id=1, source_target_pairs={{0,1},{16,19},{32,33},{48,51},{64,65},{80,83},{96,97},{112,115},{1... | collective-permute-start | bytes 1572872 | tf_op jit(solution)/shard_map/ppermute | solution.py:46
  35.8 13.2 %collective-permute-start.15 = (bf16[2,128,256]{2,1,0:T(8,128)(2,1)S(1)}, bf16[2,128,256]{2,1,0:T(8,128)(2,1)S(1)}, u32[]{:S(2)}, u32[]{:S(2)}) collective-permute-start(bf16[2,128,256]{2,1,0:T(8,128)(2,1)S(1)} %get-tuple-element.117), channel_id=1, source_target_pairs={{0,16},{16,0},{32,48},{48,32},{64,80},{80,64},{96,112},{112,96},{1... | collective-permute-start | bytes 393224 | tf_op jit(solution)/shard_map/ppermute | solution.py:50
  37.8 13.1 %collective-permute-start.16 = (bf16[2,128,256]{2,1,0:T(8,128)(2,1)S(1)}, bf16[2,128,256]{2,1,0:T(8,128)(2,1)S(1)}, u32[]{:S(2)}, u32[]{:S(2)}) collective-permute-start(bf16[2,128,256]{2,1,0:T(8,128)(2,1)S(1)} %get-tuple-element.115), channel_id=1, source_target_pairs={{0,16},{16,0},{32,48},{48,32},{64,80},{80,64},{96,112},{112,96},{1... | collective-permute-start | bytes 393224 | tf_op jit(solution)/shard_map/ppermute | solution.py:50
  42.1 9.3 %collective-permute-start.10 = (bf16[4,128,256]{2,1,0:T(8,128)(2,1)S(1)}, bf16[4,128,256]{2,1,0:T(8,128)(2,1)S(1)}, u32[]{:S(2)}, u32[]{:S(2)}) collective-permute-start(bf16[4,128,256]{2,1,0:T(8,128)(2,1)S(1)} %get-tuple-element.103), channel_id=1, source_target_pairs={{0,16},{16,0},{32,48},{48,32},{64,80},{80,64},{96,112},{112,96},{1... | collective-permute-start | bytes 786440 | tf_op jit(solution)/shard_map/ppermute | solution.py:50
  44.5 7.0 %collective-permute-start.9 = (bf16[4,128,256]{2,1,0:T(8,128)(2,1)S(1)}, bf16[4,128,256]{2,1,0:T(8,128)(2,1)S(1)}, u32[]{:S(2)}, u32[]{:S(2)}) collective-permute-start(bf16[4,128,256]{2,1,0:T(8,128)(2,1)S(1)} %get-tuple-element.105), channel_id=1, source_target_pairs={{0,16},{16,0},{32,48},{48,32},{64,80},{80,64},{96,112},{112,96},{1... | collective-permute-start | bytes 786440 | tf_op jit(solution)/shard_map/ppermute | solution.py:50
  47.2 8.8 %collective-permute-start.17 = (bf16[4,128,256]{2,1,0:T(8,128)(2,1)S(1)}, bf16[4,128,256]{2,1,0:T(8,128)(2,1)S(1)}, u32[]{:S(2)}, u32[]{:S(2)}) collective-permute-start(bf16[4,128,256]{2,1,0:T(8,128)(2,1)S(1)} %get-tuple-element.104), channel_id=1, source_target_pairs={{0,4},{16,28},{32,36},{48,60},{64,68},{80,92},{96,100},{112,124},{... | collective-permute-start | bytes 786440 | tf_op jit(solution)/shard_map/ppermute | solution.py:46
  49.0 6.9 %collective-permute-start.18 = (bf16[4,128,256]{2,1,0:T(8,128)(2,1)S(1)}, bf16[4,128,256]{2,1,0:T(8,128)(2,1)S(1)}, u32[]{:S(2)}, u32[]{:S(2)}) collective-permute-start(bf16[4,128,256]{2,1,0:T(8,128)(2,1)S(1)} %get-tuple-element.102), channel_id=1, source_target_pairs={{0,1},{16,19},{32,33},{48,51},{64,65},{80,83},{96,97},{112,115},{1... | collective-permute-start | bytes 786440 | tf_op jit(solution)/shard_map/ppermute | solution.py:46
  51.5 4.5 %collective-permute-start.20 = (bf16[2,128,256]{2,1,0:T(8,128)(2,1)S(1)}, bf16[2,128,256]{2,1,0:T(8,128)(2,1)S(1)}, u32[]{:S(2)}, u32[]{:S(2)}) collective-permute-start(bf16[2,128,256]{2,1,0:T(8,128)(2,1)S(1)} %get-tuple-element.114), channel_id=1, source_target_pairs={{0,1},{16,19},{32,33},{48,51},{64,65},{80,83},{96,97},{112,115},{1... | collective-permute-start | bytes 393224 | tf_op jit(solution)/shard_map/ppermute | solution.py:46
  59.5 10.1 %collective-permute-start.26 = (f32[128,512]{1,0:T(8,128)S(1)}, f32[128,512]{1,0:T(8,128)S(1)}, u32[]{:S(2)}, u32[]{:S(2)}) collective-permute-start(f32[128,512]{1,0:T(8,128)S(1)} %get-tuple-element.100), channel_id=1, source_target_pairs={{0,16},{16,0},{32,48},{48,32},{64,80},{80,64},{96,112},{112,96},{1... | collective-permute-start | bytes 786440 | tf_op jit(solution)/shard_map/ppermute | solution.py:50
  59.6 10.1 %collective-permute-start.22 = (f32[128,512]{1,0:T(8,128)S(1)}, f32[128,512]{1,0:T(8,128)S(1)}, u32[]{:S(2)}, u32[]{:S(2)}) collective-permute-start(f32[128,512]{1,0:T(8,128)S(1)} %get-tuple-element.94), channel_id=1, source_target_pairs={{0,16},{16,0},{32,48},{48,32},{64,80},{80,64},{96,112},{112,96},{1... | collective-permute-start | bytes 786440 | tf_op jit(solution)/shard_map/ppermute | solution.py:50
  60.1 9.6 %collective-permute-start.24 = (f32[128,512]{1,0:T(8,128)S(1)}, f32[128,512]{1,0:T(8,128)S(1)}, u32[]{:S(2)}, u32[]{:S(2)}) collective-permute-start(f32[128,512]{1,0:T(8,128)S(1)} %add.13), channel_id=1, source_target_pairs={{0,32},{16,112},{32,64},{48,16},{64,96},{80,48},{96,0},{112,80},{1... | collective-permute-start | bytes 786440 | tf_op jit(solution)/shard_map/ppermute | solution.py:46
  66.8 5.7 %collective-permute-start.21 = (f32[128,512]{1,0:T(8,128)S(1)}, f32[128,512]{1,0:T(8,128)S(1)}, u32[]{:S(2)}, u32[]{:S(2)}) collective-permute-start(f32[128,512]{1,0:T(8,128)S(1)} %get-tuple-element.80), channel_id=1, source_target_pairs={{0,16},{16,0},{32,48},{48,32},{64,80},{80,64},{96,112},{112,96},{1... | collective-permute-start | bytes 786440 | tf_op jit(solution)/shard_map/ppermute | solution.py:50
  69.6 8.1 %collective-permute-start.27 = (f32[128,512]{1,0:T(8,128)S(1)}, f32[128,512]{1,0:T(8,128)S(1)}, u32[]{:S(2)}, u32[]{:S(2)}) collective-permute-start(f32[128,512]{1,0:T(8,128)S(1)} %add.15), channel_id=1, source_target_pairs={{0,96},{16,48},{32,0},{48,80},{64,32},{80,112},{96,64},{112,16},{1... | collective-permute-start | bytes 786440 | tf_op jit(solution)/shard_map/ppermute | solution.py:46
  69.8 8.0 %collective-permute-start.25 = (f32[128,512]{1,0:T(8,128)S(1)}, f32[128,512]{1,0:T(8,128)S(1)}, u32[]{:S(2)}, u32[]{:S(2)}) collective-permute-start(f32[128,512]{1,0:T(8,128)S(1)} %add_add_fusion), channel_id=1, source_target_pairs={{0,32},{16,112},{32,64},{48,16},{64,96},{80,48},{96,0},{112,80},{1... | collective-permute-start | bytes 786440 | tf_op jit(solution)/shard_map/ppermute | solution.py:46
  (5 other events, 14.6 us)

commit v4 on v3

--- a/solution.py
+++ b/solution.py
@@ -87,12 +87,12 @@
     return pl.pallas_call(
         split_kernel,
         grid=(d // 512,),
-        in_specs=[pl.BlockSpec((512, w), lambda k: (k, 0)), FULL],
+        in_specs=[pl.BlockSpec((512, w), lambda k: (k, 0)), pl.BlockSpec(visited.shape, lambda k: (0, 0))],
         out_specs=(FULL, FULL),
         out_shape=(VM((d // 512, w // 8, 32, 512), jnp.int8), VM(visited.shape, jnp.int32)),
         compiler_params=pltpu.CompilerParams(vmem_limit_bytes=24 << 20),
         name="split",
-    )(pltpu.with_memory_space_constraint(adj, pltpu.HBM), visited)
+    )(*[pltpu.with_memory_space_constraint(v, pltpu.HBM) for v in (adj, visited)])
 
 
 def here():
@@ -138,6 +138,10 @@
         scr[k] = f_refs[t[0]][t[1]]
         at[k] = where[k]
 
+    if start:
+        for k in range(n):
+            outs[k][...] = jnp.zeros_like(outs[k])
+
     def step(i, carry):
         base = i * group
         f = jnp.concatenate([scr[base + t] for t in range(group)], 1)
@@ -204,7 +208,7 @@
 
 TWO, TWO_O, UP_O, DOWN_O = (0, 1, False), (0, 1, True), (-1, 0, True), (1, 0, True)
 UP, DOWN, OWN, OWN_O = (1, 0, False), (-1, 0, False), (0, 0, False), (0, 0, True)
-EVERY = (TWO, TWO_O, UP_O, DOWN_O, UP, DOWN, OWN, OWN_O)
+SOON = (TWO, TWO_O, DOWN_O, UP_O, DOWN)
 
 
 def level(adjacency, frontier, visited):
@@ -224,40 +228,45 @@
     px, py = swap(dx), swap(dy)
     bx = send(dx[:4], "x")
     by = send(dy[:4], "y")
-    work([ft], tiles(0, 0, O, O, ALL), EVERY, 4)
+    work([ft], tiles(0, 0, O, O, ALL), SOON, 4)
     cx = send(jnp.concatenate([dy[2:4], py[6:8], dy[6:8], py[2:4]], 0), "x")
     cy = send(jnp.concatenate([dx[0:2], px[4:6], dx[4:6], px[0:2]], 0), "y")
-    work([dx, dy], tiles(0, 0, M, O, ALL) + tiles(1, 0, O, M, ALL), EVERY, 8)
-
-    pbx, pby = swap(bx[0:2]), swap(by[2:4])
-    work([px, py], tiles(0, 4, Q, O, ALL) + tiles(1, 4, O, Q, ALL), EVERY, 8)
-    ex = send(jnp.concatenate([by[2:4], pby], 0), "x")
-    ey = send(jnp.concatenate([bx[0:2], pbx], 0), "y")
+    work([dx], tiles(0, 0, M, O, ALL), SOON, 4)
+
+    pb = swap(jnp.concatenate([bx[0:2], by[2:4]], 0))
+    work([dy], tiles(0, 0, O, M, ALL), SOON, 4)
+    ex = send(jnp.concatenate([by[2:4], pb[2:4]], 0), "x")
+    ey = send(jnp.concatenate([bx[0:2], pb[0:2]], 0), "y")
+    work([px, py], tiles(0, 4, Q, O, ALL) + tiles(1, 4, O, Q, ALL), SOON, 8)
+
+    pc = swap(jnp.concatenate([cx[4:8], cy[4:8]], 0))
     hx, hy = send(cx[:4], "x"), send(cy[:4], "y")
-    pcx, pcy = swap(cx[4:8]), swap(cy[4:8])
-    work([bx, by], tiles(0, 0, T, O, ALL) + tiles(1, 0, O, T, ALL), EVERY, 8)
-
     gx, gy = send(ex[:2], "x"), send(ey[:2], "y")
-    pex, pey = swap(ex[2:4]), swap(ey[2:4])
-
-    late = [cx, cy, pcx, pcy, ex, ey, pex, pey, hx, hy, gx, gy]
-    fb = tiles(0, 0, M, M, H1) + tiles(0, 2, M, Q, H1) + tiles(1, 0, M, M, H0) + tiles(1, 2, Q, M, H0)
-    sd = tiles(2, 0, Q, Q, H1) + tiles(2, 2, Q, M, H1) + tiles(3, 0, Q, Q, H0) + tiles(3, 2, M, Q, H0)
-    sd = sd + tiles(4, 0, M, T, H1) + tiles(5, 0, T, M, H0) + tiles(6, 0, Q, T, H1) + tiles(7, 0, T, Q, H0)
-    la = tiles(8, 0, T, M, H1) + tiles(8, 2, T, Q, H1) + tiles(9, 0, M, T, H0) + tiles(9, 2, Q, T, H0)
-    la = la + tiles(10, 0, T, T, H1) + tiles(11, 0, T, T, H0)
+    pe = swap(jnp.concatenate([ex[2:4], ey[2:4]], 0))
+    work([bx, by], tiles(0, 0, T, O, ALL) + tiles(1, 0, O, T, ALL), SOON, 8)
+
+    arrays = [ft, dx, px, dy, py, bx, by, cx, cy, pc, ex, ey, pe, hx, hy, gx, gy]
+    ea = tiles(0, 0, O, O, ALL) + tiles(1, 0, M, O, ALL) + tiles(2, 4, Q, O, ALL) + tiles(3, 0, O, M, ALL)
+    ea = ea + tiles(4, 4, O, Q, ALL) + tiles(5, 0, T, O, ALL) + tiles(6, 0, O, T, ALL)
+    fb = tiles(7, 0, M, M, H1) + tiles(7, 2, M, Q, H1) + tiles(8, 0, M, M, H0) + tiles(8, 2, Q, M, H0)
+    sd = tiles(9, 0, Q, Q, H1) + tiles(9, 2, Q, M, H1) + tiles(9, 4, Q, Q, H0) + tiles(9, 6, M, Q, H0)
+    sd = sd + tiles(10, 0, M, T, H1) + tiles(11, 0, T, M, H0) + tiles(12, 0, Q, T, H1) + tiles(12, 2, T, Q, H0)
+    la = tiles(13, 0, T, M, H1) + tiles(13, 2, T, Q, H1) + tiles(14, 0, M, T, H0) + tiles(14, 2, Q, T, H0)
+    la = la + tiles(15, 0, T, T, H1) + tiles(16, 0, T, T, H0)
 
     def late_work(tiles, blocks, group):
         used = sorted({t[0] for t in tiles})
-        work([late[n] for n in used], [(used.index(t[0]),) + t[1:] for t in tiles], blocks, group)
-
-    first = EVERY[:4]
-    late_work(fb, first, 8)
-    late_work(sd, first, 8)
+        work([arrays[n] for n in used], [(used.index(t[0]),) + t[1:] for t in tiles], blocks, group)
+
+    late_work(fb, SOON, 8)
+    late_work(sd, (TWO, TWO_O), 16)
     late_work(la, (TWO, TWO_O), 12)
-    late_work(la, (UP_O, DOWN_O), 12)
-    late_work(fb + sd + la, (UP, DOWN), 36)
-    late_work(fb + sd + la, (OWN, OWN_O), 36)
+    late_work(sd + la, (DOWN_O,), 28)
+    late_work(sd + la, (DOWN,), 28)
+    late_work(sd + la, (UP_O,), 28)
+    late_work(ea + fb + sd + la, (UP,), 64)
+    late_work(ea + fb + sd + la, (OWN_O,), 64)
+    late_work(ea + fb + sd + la, (OWN,), 64)
 
     hop = send(totals[TWO] + swap(totals[TWO_O]), "z")
     got0 = send(totals[DOWN] + swap(totals[DOWN_O]), "z", True)

time: 79.4 us -> 75.9 us (0.956)
  the two profiles are of different devices: /device:TPU:1 before, /device:TPU:6 now
where the time goes in v4:
time: 75.9 us; the launch traced here: 75.6 us
  Pallas kernels  29.7 us (39%)
  starting transfers between devices  23.6 us (31%)
  waiting for transfers between devices  20.6 us (27%)
  between operations  1 us (1%)
    ppermute x15, starting transfers between devices, send(): return lax.ppermute(value, AXES, pairs(axis, flip))  20.9 us
    pallas_call x14, Pallas kernels, mm(): pl.pallas_call(functools.partial(mm_kernel, tiles=tuple(tiles), arrays=le...  20.5 us
    ppermute x15, waiting for transfers between devices, send(): return lax.ppermute(value, AXES, pairs(axis, flip))  18.1 us
    pallas_call x1, Pallas kernels, split(): pl.pallas_call(split_kernel, grid=(d // 512,), in_specs=[pl.BlockSpec((51...  6.98 us
    ppermute x10, starting transfers between devices, swap(): return lax.ppermute(value, AXES, pairs('core'))  2.66 us
    ppermute x10, waiting for transfers between devices, swap(): return lax.ppermute(value, AXES, pairs('core'))  2.51 us
  transfers between devices with their start and end apart: 25, of which 9 were waited for; matrix products, arithmetic and copies ran while one was open for 1% of the time, Pallas kernels for 35%

profile of v4, /device:TPU:6, one launch (start us, length us, event | category | flops | bytes accessed | tf_op | source)
XLA Modules:
  0.0 75.6 jit_solution(12080289469877957335)
XLA Ops:
  0.6 1.3 %prep.1.refs_1_ = bf16[4,128,256]{2,1,0:T(8,128)(2,1)S(1)} custom-call(bf16[1024,128]{1,0:T(8,128)(2,1)} %f_ref.1), custom_call_target="tpu_custom_call" | custom-call | tf_op jit(solution)/shard_map/prep/pallas_call | solution.py:64
  2.1 1.5 %collective-permute-done = bf16[4,128,256]{2,1,0:T(8,128)(2,1)S(1)} collective-permute-done((bf16[4,128,256]{2,1,0:T(8,128)(2,1)S(1)}, bf16[4,128,256]{2,1,0:T(8,128)(2,1)S(1)}, u32[]{:S(2)}, u32[]{:S(2)}) %collective-permute-start) | collective-permute-done | bytes 262176 | tf_op jit(solution)/shard_map/ppermute | solution.py:50
  4.1 1.7 %collective-permute-start.3 = (bf16[8,128,256]{2,1,0:T(8,128)(2,1)S(1)}, bf16[8,128,256]{2,1,0:T(8,128)(2,1)S(1)}, u32[]{:S(2)}, u32[]{:S(2)}) collective-permute-start(bf16[8,128,256]{2,1,0:T(8,128)(2,1)S(1)} %pad_maximum_fusion), channel_id=1, source_target_pairs={{0,1},{16,19},{32,33},{48,51},{64,65},{80,83},{96,97},{112,115},{1... | collective-permute-start | bytes 1572872 | tf_op jit(solution)/shard_map/ppermute | solution.py:46
  5.8 7.0 %split.1 = (s8[8,64,32,512]{3,2,1,0:T(32,128)(4,1)S(1)}, s32[4,512]{1,0:T(4,128)S(1)}) custom-call(s32[4096,512]{1,0:T(8,128)} %a_ref.1, s32[4,512]{1,0:T(4,128)} %v_ref.1), custom_call_target="tpu_custom_call" | custom-call | tf_op jit(solution)/shard_map/split/pallas_call | solution.py:87
  13.7 1.6 %collective-permute-start.5 = (bf16[4,128,256]{2,1,0:T(8,128)(2,1)S(1)}, bf16[4,128,256]{2,1,0:T(8,128)(2,1)S(1)}, u32[]{:S(2)}, u32[]{:S(2)}) collective-permute-start(bf16[4,128,256]{2,1,0:T(8,128)(2,1)S(1)} %slice.90), channel_id=1, source_target_pairs={{0,4},{16,28},{32,36},{48,60},{64,68},{80,92},{96,100},{112,124},{... | collective-permute-start | bytes 786440 | tf_op jit(solution)/shard_map/ppermute | solution.py:46
  15.3 1.6 %collective-permute-start.6 = (bf16[4,128,256]{2,1,0:T(8,128)(2,1)S(1)}, bf16[4,128,256]{2,1,0:T(8,128)(2,1)S(1)}, u32[]{:S(2)}, u32[]{:S(2)}) collective-permute-start(bf16[4,128,256]{2,1,0:T(8,128)(2,1)S(1)} %slice.91), channel_id=1, source_target_pairs={{0,1},{16,19},{32,33},{48,51},{64,65},{80,83},{96,97},{112,115},{1... | collective-permute-start | bytes 786440 | tf_op jit(solution)/shard_map/ppermute | solution.py:46
  19.4 3.5 %collective-permute-done.6.refs_7_ = bf16[4,128,256]{2,1,0:T(8,128)(2,1)S(1)} collective-permute-done((bf16[4,128,256]{2,1,0:T(8,128)(2,1)S(1)}, bf16[4,128,256]{2,1,0:T(8,128)(2,1)S(1)}, u32[]{:S(2)}, u32[]{:S(2)}) %collective-permute-start.6) | collective-permute-done | bytes 262176 | tf_op jit(solution)/shard_map/ppermute | solution.py:46
  24.7 1.6 %collective-permute-start.11 = (bf16[4,128,256]{2,1,0:T(8,128)(2,1)S(1)}, bf16[4,128,256]{2,1,0:T(8,128)(2,1)S(1)}, u32[]{:S(2)}, u32[]{:S(2)}) collective-permute-start(bf16[4,128,256]{2,1,0:T(8,128)(2,1)S(1)} %pad_maximum_fusion.6), channel_id=1, source_target_pairs={{0,4},{16,28},{32,36},{48,60},{64,68},{80,92},{96,100},{112,124},{... | collective-permute-start | bytes 786440 | tf_op jit(solution)/shard_map/ppermute | solution.py:46
  28.1 3.0 %collective-permute-done.11.refs_11_.refs_3_.refs_4_ = bf16[4,128,256]{2,1,0:T(8,128)(2,1)S(1)} collective-permute-done((bf16[4,128,256]{2,1,0:T(8,128)(2,1)S(1)}, bf16[4,128,256]{2,1,0:T(8,128)(2,1)S(1)}, u32[]{:S(2)}, u32[]{:S(2)}) %collective-permute-start.11) | collective-permute-done | bytes 262176 | tf_op jit(solution)/shard_map/ppermute | solution.py:46
  31.1 2.8 %collective-permute-start.16 = (bf16[2,128,256]{2,1,0:T(8,128)(2,1)S(1)}, bf16[2,128,256]{2,1,0:T(8,128)(2,1)S(1)}, u32[]{:S(2)}, u32[]{:S(2)}) collective-permute-start(bf16[2,128,256]{2,1,0:T(8,128)(2,1)S(1)} %get-tuple-element.88), channel_id=1, source_target_pairs={{0,4},{16,28},{32,36},{48,60},{64,68},{80,92},{96,100},{112,124},{... | collective-permute-start | bytes 393224 | tf_op jit(solution)/shard_map/ppermute | solution.py:46
  33.9 2.8 %collective-permute-done.7.refs_8_.refs_6_ = bf16[8,128,256]{2,1,0:T(8,128)(2,1)S(1)} collective-permute-done((bf16[8,128,256]{2,1,0:T(8,128)(2,1)S(1)}, bf16[8,128,256]{2,1,0:T(8,128)(2,1)S(1)}, u32[]{:S(2)}, u32[]{:S(2)}) %collective-permute-start.7) | collective-permute-done | bytes 524320 | tf_op jit(solution)/shard_map/ppermute | solution.py:46
  37.5 2.7 %collective-permute-start.14 = (bf16[4,128,256]{2,1,0:T(8,128)(2,1)S(1)}, bf16[4,128,256]{2,1,0:T(8,128)(2,1)S(1)}, u32[]{:S(2)}, u32[]{:S(2)}) collective-permute-start(bf16[4,128,256]{2,1,0:T(8,128)(2,1)S(1)} %get-tuple-element.76), channel_id=1, source_target_pairs={{0,4},{16,28},{32,36},{48,60},{64,68},{80,92},{96,100},{112,124},{... | collective-permute-start | bytes 786440 | tf_op jit(solution)/shard_map/ppermute | solution.py:46
  40.6 1.6 %bits_mm.20 = (f32[128,512]{1,0:T(8,128)S(1)}, f32[128,512]{1,0:T(8,128)S(1)}, f32[128,512]{1,0:T(8,128)S(1)}, f32[128,512]{1,0:T(8,128)S(1)}, f32[128,512]{1,0:T(8,128)S(1)}) custom-call(s8[8,64,32,512]{3,2,1,0:T(32,128)(4,1)S(1)} %get-tuple-element.38.refs_0_, ...), custom_call_target="tpu_custom_call", output_to_operand_aliasing={{0}: (1, {}), {1}: (2, {}), {2}: (3, {}), {3}: (4, {}), {4}... | custom-call | flops 1342177280 | tf_op jit(solution)/shard_map/bits_mm/pallas_call | solution.py:160
  42.3 1.5 %collective-permute-start.17 = (bf16[2,128,256]{2,1,0:T(8,128)(2,1)S(1)}, bf16[2,128,256]{2,1,0:T(8,128)(2,1)S(1)}, u32[]{:S(2)}, u32[]{:S(2)}) collective-permute-start(bf16[2,128,256]{2,1,0:T(8,128)(2,1)S(1)} %get-tuple-element.86), channel_id=1, source_target_pairs={{0,1},{16,19},{32,33},{48,51},{64,65},{80,83},{96,97},{112,115},{1... | collective-permute-start | bytes 393224 | tf_op jit(solution)/shard_map/ppermute | solution.py:46
  43.8 1.6 %bits_mm.21 = (f32[128,512]{1,0:T(8,128)S(1)}, f32[128,512]{1,0:T(8,128)S(1)}, f32[128,512]{1,0:T(8,128)S(1)}, f32[128,512]{1,0:T(8,128)S(1)}, f32[128,512]{1,0:T(8,128)S(1)}) custom-call(s8[8,64,32,512]{3,2,1,0:T(32,128)(4,1)S(1)} %get-tuple-element.38.refs_0_, ...), custom_call_target="tpu_custom_call", output_to_operand_aliasing={{0}: (1, {}), {1}: (2, {}), {2}: (3, {}), {3}: (4, {}), {4}... | custom-call | flops 1342177280 | tf_op jit(solution)/shard_map/bits_mm/pallas_call | solution.py:160
  45.5 1.7 %bits_mm.22 = (f32[128,512]{1,0:T(8,128)S(1)}, f32[128,512]{1,0:T(8,128)S(1)}, f32[128,512]{1,0:T(8,128)S(1)}, f32[128,512]{1,0:T(8,128)S(1)}, f32[128,512]{1,0:T(8,128)S(1)}) custom-call(s8[8,64,32,512]{3,2,1,0:T(32,128)(4,1)S(1)} %get-tuple-element.38.refs_0_, ...), custom_call_target="tpu_custom_call", output_to_operand_aliasing={{0}: (1, {}), {1}: (2, {}), {2}: (3, {}), {3}: (4, {}), {4}... | custom-call | flops 1342177280 | tf_op jit(solution)/shard_map/bits_mm/pallas_call | solution.py:160
  47.1 2.1 %collective-permute-done.17.refs_17_.refs_9_.refs_6_ = bf16[2,128,256]{2,1,0:T(8,128)(2,1)S(1)} collective-permute-done((bf16[2,128,256]{2,1,0:T(8,128)(2,1)S(1)}, bf16[2,128,256]{2,1,0:T(8,128)(2,1)S(1)}, u32[]{:S(2)}, u32[]{:S(2)}) %collective-permute-start.17) | collective-permute-done | bytes 131104 | tf_op jit(solution)/shard_map/ppermute | solution.py:46
  54.7 2.3 %bits_mm.15 = f32[128,512]{1,0:T(8,128)S(1)} custom-call(s8[8,64,32,512]{3,2,1,0:T(32,128)(4,1)S(1)} %get-tuple-element.38.refs_0_, bf16[4,128,256]{2,1,0:T(8,128)(2,1)S(1)} %prep.1.refs_1_, bf16[8,128,256]{2,1,0:T(8,128)(2,1)S(1)} %collective-permute-done.1.refs_2_.refs_6_, bf16[8,128,256]{2,1,0:T(8,128)(2,1)S(1)} %collective-permute-done.2.refs_3_.refs_6_, ...), custom_call_target="tpu_custom_call" | custom-call | flops 2147483648 | tf_op jit(solution)/shard_map/bits_mm/pallas_call | solution.py:160
  57.6 2.2 %collective-permute-start.21 = (f32[128,512]{1,0:T(8,128)S(1)}, f32[128,512]{1,0:T(8,128)S(1)}, u32[]{:S(2)}, u32[]{:S(2)}) collective-permute-start(f32[128,512]{1,0:T(8,128)S(1)} %add.13), channel_id=1, source_target_pairs={{0,32},{16,112},{32,64},{48,16},{64,96},{80,48},{96,0},{112,80},{1... | collective-permute-start | bytes 786440 | tf_op jit(solution)/shard_map/ppermute | solution.py:46
  61.0 2.3 %bits_mm.16 = f32[128,512]{1,0:T(8,128)S(1)} custom-call(s8[8,64,32,512]{3,2,1,0:T(32,128)(4,1)S(1)} %get-tuple-element.38.refs_0_, bf16[4,128,256]{2,1,0:T(8,128)(2,1)S(1)} %prep.1.refs_1_, bf16[8,128,256]{2,1,0:T(8,128)(2,1)S(1)} %collective-permute-done.1.refs_2_.refs_6_, bf16[8,128,256]{2,1,0:T(8,128)(2,1)S(1)} %collective-permute-done.2.refs_3_.refs_6_, ...), custom_call_target="tpu_custom_call" | custom-call | flops 2147483648 | tf_op jit(solution)/shard_map/bits_mm/pallas_call | solution.py:160
  63.4 2.2 %collective-permute-start.24 = (f32[128,512]{1,0:T(8,128)S(1)}, f32[128,512]{1,0:T(8,128)S(1)}, u32[]{:S(2)}, u32[]{:S(2)}) collective-permute-start(f32[128,512]{1,0:T(8,128)S(1)} %add.15), channel_id=1, source_target_pairs={{0,96},{16,48},{32,0},{48,80},{64,32},{80,112},{96,64},{112,16},{1... | collective-permute-start | bytes 786440 | tf_op jit(solution)/shard_map/ppermute | solution.py:46
  66.4 2.3 %bits_mm.14.a_ref = f32[128,512]{1,0:T(8,128)S(1)} custom-call(s8[8,64,32,512]{3,2,1,0:T(32,128)(4,1)S(1)} %get-tuple-element.38.refs_0_, bf16[4,128,256]{2,1,0:T(8,128)(2,1)S(1)} %prep.1.refs_1_, bf16[8,128,256]{2,1,0:T(8,128)(2,1)S(1)} %collective-permute-done.1.refs_2_.refs_6_, bf16[8,128,256]{2,1,0:T(8,128)(2,1)S(1)} %collective-permute-done.2.refs_3_.refs_6_, ...), custom_call_target="tpu_custom_call" | custom-call | flops 2147483648 | tf_op jit(solution)/shard_map/bits_mm/pallas_call | solution.py:160
  68.8 2.8 %collective-permute-done.24.d_ref = f32[128,512]{1,0:T(8,128)S(1)} collective-permute-done((f32[128,512]{1,0:T(8,128)S(1)}, f32[128,512]{1,0:T(8,128)S(1)}, u32[]{:S(2)}, u32[]{:S(2)}) %collective-permute-start.24) | collective-permute-done | bytes 262176 | tf_op jit(solution)/shard_map/ppermute | solution.py:46
  71.6 3.2 %collective-permute-done.22.c_ref = f32[128,512]{1,0:T(8,128)S(1)} collective-permute-done((f32[128,512]{1,0:T(8,128)S(1)}, f32[128,512]{1,0:T(8,128)S(1)}, u32[]{:S(2)}, u32[]{:S(2)}) %collective-permute-start.22) | collective-permute-done | bytes 262176 | tf_op jit(solution)/shard_map/ppermute | solution.py:46
  (67 shorter events, 17.5 us)
Async XLA Ops:
  2.0 1.6 %collective-permute-start = (bf16[4,128,256]{2,1,0:T(8,128)(2,1)S(1)}, bf16[4,128,256]{2,1,0:T(8,128)(2,1)S(1)}, u32[]{:S(2)}, u32[]{:S(2)}) collective-permute-start(bf16[4,128,256]{2,1,0:T(8,128)(2,1)S(1)} %prep.1.refs_1_), channel_id=1, source_target_pairs={{0,16},{16,0},{32,48},{48,32},{64,80},{80,64},{96,112},{112,96},{1... | collective-permute-start | bytes 786440 | tf_op jit(solution)/shard_map/ppermute | solution.py:50
  3.6 10.0 %collective-permute-start.1 = (bf16[8,128,256]{2,1,0:T(8,128)(2,1)S(1)}, bf16[8,128,256]{2,1,0:T(8,128)(2,1)S(1)}, u32[]{:S(2)}, u32[]{:S(2)}) collective-permute-start(bf16[8,128,256]{2,1,0:T(8,128)(2,1)S(1)} %pad_maximum_fusion), channel_id=1, source_target_pairs={{0,4},{16,28},{32,36},{48,60},{64,68},{80,92},{96,100},{112,124},{... | collective-permute-start | bytes 1572872 | tf_op jit(solution)/shard_map/ppermute | solution.py:46
  4.1 11.2 %collective-permute-start.3 = (bf16[8,128,256]{2,1,0:T(8,128)(2,1)S(1)}, bf16[8,128,256]{2,1,0:T(8,128)(2,1)S(1)}, u32[]{:S(2)}, u32[]{:S(2)}) collective-permute-start(bf16[8,128,256]{2,1,0:T(8,128)(2,1)S(1)} %pad_maximum_fusion), channel_id=1, source_target_pairs={{0,1},{16,19},{32,33},{48,51},{64,65},{80,83},{96,97},{112,115},{1... | collective-permute-start | bytes 1572872 | tf_op jit(solution)/shard_map/ppermute | solution.py:46
  13.7 9.3 %collective-permute-start.5 = (bf16[4,128,256]{2,1,0:T(8,128)(2,1)S(1)}, bf16[4,128,256]{2,1,0:T(8,128)(2,1)S(1)}, u32[]{:S(2)}, u32[]{:S(2)}) collective-permute-start(bf16[4,128,256]{2,1,0:T(8,128)(2,1)S(1)} %slice.90), channel_id=1, source_target_pairs={{0,4},{16,28},{32,36},{48,60},{64,68},{80,92},{96,100},{112,124},{... | collective-permute-start | bytes 786440 | tf_op jit(solution)/shard_map/ppermute | solution.py:46
  15.3 7.7 %collective-permute-start.6 = (bf16[4,128,256]{2,1,0:T(8,128)(2,1)S(1)}, bf16[4,128,256]{2,1,0:T(8,128)(2,1)S(1)}, u32[]{:S(2)}, u32[]{:S(2)}) collective-permute-start(bf16[4,128,256]{2,1,0:T(8,128)(2,1)S(1)} %slice.91), channel_id=1, source_target_pairs={{0,1},{16,19},{32,33},{48,51},{64,65},{80,83},{96,97},{112,115},{1... | collective-permute-start | bytes 786440 | tf_op jit(solution)/shard_map/ppermute | solution.py:46
  16.9 6.2 %collective-permute-start.2 = (bf16[8,128,256]{2,1,0:T(8,128)(2,1)S(1)}, bf16[8,128,256]{2,1,0:T(8,128)(2,1)S(1)}, u32[]{:S(2)}, u32[]{:S(2)}) collective-permute-start(bf16[8,128,256]{2,1,0:T(8,128)(2,1)S(1)} %collective-permute-done.1.refs_2_.refs_6_), channel_id=1, source_target_pairs={{0,16},{16,0},{32,48},{48,32},{64,80},{80,64},{96,112},{112,96},{1... | collective-permute-start | bytes 1572872 | tf_op jit(solution)/shard_map/ppermute | solution.py:50
  16.9 9.3 %collective-permute-start.4 = (bf16[8,128,256]{2,1,0:T(8,128)(2,1)S(1)}, bf16[8,128,256]{2,1,0:T(8,128)(2,1)S(1)}, u32[]{:S(2)}, u32[]{:S(2)}) collective-permute-start(bf16[8,128,256]{2,1,0:T(8,128)(2,1)S(1)} %collective-permute-done.3.refs_4_.refs_6_), channel_id=1, source_target_pairs={{0,16},{16,0},{32,48},{48,32},{64,80},{80,64},{96,112},{112,96},{1... | collective-permute-start | bytes 1572872 | tf_op jit(solution)/shard_map/ppermute | solution.py:50
  23.2 10.7 %collective-permute-start.8 = (bf16[8,128,256]{2,1,0:T(8,128)(2,1)S(1)}, bf16[8,128,256]{2,1,0:T(8,128)(2,1)S(1)}, u32[]{:S(2)}, u32[]{:S(2)}) collective-permute-start(bf16[8,128,256]{2,1,0:T(8,128)(2,1)S(1)} %pad_maximum_fusion.2), channel_id=1, source_target_pairs={{0,1},{16,19},{32,33},{48,51},{64,65},{80,83},{96,97},{112,115},{1... | collective-permute-start | bytes 1572872 | tf_op jit(solution)/shard_map/ppermute | solution.py:46
  24.7 6.4 %collective-permute-start.11 = (bf16[4,128,256]{2,1,0:T(8,128)(2,1)S(1)}, bf16[4,128,256]{2,1,0:T(8,128)(2,1)S(1)}, u32[]{:S(2)}, u32[]{:S(2)}) collective-permute-start(bf16[4,128,256]{2,1,0:T(8,128)(2,1)S(1)} %pad_maximum_fusion.6), channel_id=1, source_target_pairs={{0,4},{16,28},{32,36},{48,60},{64,68},{80,92},{96,100},{112,124},{... | collective-permute-start | bytes 786440 | tf_op jit(solution)/shard_map/ppermute | solution.py:46
  26.3 10.4 %collective-permute-start.7 = (bf16[8,128,256]{2,1,0:T(8,128)(2,1)S(1)}, bf16[8,128,256]{2,1,0:T(8,128)(2,1)S(1)}, u32[]{:S(2)}, u32[]{:S(2)}) collective-permute-start(bf16[8,128,256]{2,1,0:T(8,128)(2,1)S(1)} %pad_maximum_fusion.1), channel_id=1, source_target_pairs={{0,4},{16,28},{32,36},{48,60},{64,68},{80,92},{96,100},{112,124},{... | collective-permute-start | bytes 1572872 | tf_op jit(solution)/shard_map/ppermute | solution.py:46
  27.6 9.5 %collective-permute-start.12 = (bf16[4,128,256]{2,1,0:T(8,128)(2,1)S(1)}, bf16[4,128,256]{2,1,0:T(8,128)(2,1)S(1)}, u32[]{:S(2)}, u32[]{:S(2)}) collective-permute-start(bf16[4,128,256]{2,1,0:T(8,128)(2,1)S(1)} %pad_maximum_fusion.4), channel_id=1, source_target_pairs={{0,1},{16,19},{32,33},{48,51},{64,65},{80,83},{96,97},{112,115},{1... | collective-permute-start | bytes 786440 | tf_op jit(solution)/shard_map/ppermute | solution.py:46
  31.1 11.1 %collective-permute-start.16 = (bf16[2,128,256]{2,1,0:T(8,128)(2,1)S(1)}, bf16[2,128,256]{2,1,0:T(8,128)(2,1)S(1)}, u32[]{:S(2)}, u32[]{:S(2)}) collective-permute-start(bf16[2,128,256]{2,1,0:T(8,128)(2,1)S(1)} %get-tuple-element.88), channel_id=1, source_target_pairs={{0,4},{16,28},{32,36},{48,60},{64,68},{80,92},{96,100},{112,124},{... | collective-permute-start | bytes 393224 | tf_op jit(solution)/shard_map/ppermute | solution.py:46
  36.8 12.4 %collective-permute-start.9 = (bf16[8,128,256]{2,1,0:T(8,128)(2,1)S(1)}, bf16[8,128,256]{2,1,0:T(8,128)(2,1)S(1)}, u32[]{:S(2)}, u32[]{:S(2)}) collective-permute-start(bf16[8,128,256]{2,1,0:T(8,128)(2,1)S(1)} %pad_maximum_fusion.3), channel_id=1, source_target_pairs={{0,16},{16,0},{32,48},{48,32},{64,80},{80,64},{96,112},{112,96},{1... | collective-permute-start | bytes 1572872 | tf_op jit(solution)/shard_map/ppermute | solution.py:50
  37.2 12.1 %collective-permute-start.13 = (bf16[4,128,256]{2,1,0:T(8,128)(2,1)S(1)}, bf16[4,128,256]{2,1,0:T(8,128)(2,1)S(1)}, u32[]{:S(2)}, u32[]{:S(2)}) collective-permute-start(bf16[4,128,256]{2,1,0:T(8,128)(2,1)S(1)} %pad_maximum_fusion.7), channel_id=1, source_target_pairs={{0,16},{16,0},{32,48},{48,32},{64,80},{80,64},{96,112},{112,96},{1... | collective-permute-start | bytes 786440 | tf_op jit(solution)/shard_map/ppermute | solution.py:50
  37.5 11.7 %collective-permute-start.14 = (bf16[4,128,256]{2,1,0:T(8,128)(2,1)S(1)}, bf16[4,128,256]{2,1,0:T(8,128)(2,1)S(1)}, u32[]{:S(2)}, u32[]{:S(2)}) collective-permute-start(bf16[4,128,256]{2,1,0:T(8,128)(2,1)S(1)} %get-tuple-element.76), channel_id=1, source_target_pairs={{0,4},{16,28},{32,36},{48,60},{64,68},{80,92},{96,100},{112,124},{... | collective-permute-start | bytes 786440 | tf_op jit(solution)/shard_map/ppermute | solution.py:46
  40.2 9.0 %collective-permute-start.15 = (bf16[4,128,256]{2,1,0:T(8,128)(2,1)S(1)}, bf16[4,128,256]{2,1,0:T(8,128)(2,1)S(1)}, u32[]{:S(2)}, u32[]{:S(2)}) collective-permute-start(bf16[4,128,256]{2,1,0:T(8,128)(2,1)S(1)} %get-tuple-element.74), channel_id=1, source_target_pairs={{0,1},{16,19},{32,33},{48,51},{64,65},{80,83},{96,97},{112,115},{1... | collective-permute-start | bytes 786440 | tf_op jit(solution)/shard_map/ppermute | solution.py:46
  42.3 7.0 %collective-permute-start.17 = (bf16[2,128,256]{2,1,0:T(8,128)(2,1)S(1)}, bf16[2,128,256]{2,1,0:T(8,128)(2,1)S(1)}, u32[]{:S(2)}, u32[]{:S(2)}) collective-permute-start(bf16[2,128,256]{2,1,0:T(8,128)(2,1)S(1)} %get-tuple-element.86), channel_id=1, source_target_pairs={{0,1},{16,19},{32,33},{48,51},{64,65},{80,83},{96,97},{112,115},{1... | collective-permute-start | bytes 393224 | tf_op jit(solution)/shard_map/ppermute | solution.py:46
  50.4 12.9 %collective-permute-start.23 = (f32[128,512]{1,0:T(8,128)S(1)}, f32[128,512]{1,0:T(8,128)S(1)}, u32[]{:S(2)}, u32[]{:S(2)}) collective-permute-start(f32[128,512]{1,0:T(8,128)S(1)} %bits_mm.27), channel_id=1, source_target_pairs={{0,16},{16,0},{32,48},{48,32},{64,80},{80,64},{96,112},{112,96},{1... | collective-permute-start | bytes 786440 | tf_op jit(solution)/shard_map/ppermute | solution.py:50
  52.9 4.7 %collective-permute-start.20 = (f32[128,512]{1,0:T(8,128)S(1)}, f32[128,512]{1,0:T(8,128)S(1)}, u32[]{:S(2)}, u32[]{:S(2)}) collective-permute-start(f32[128,512]{1,0:T(8,128)S(1)} %get-tuple-element.70), channel_id=1, source_target_pairs={{0,16},{16,0},{32,48},{48,32},{64,80},{80,64},{96,112},{112,96},{1... | collective-permute-start | bytes 786440 | tf_op jit(solution)/shard_map/ppermute | solution.py:50
  54.6 11.0 %collective-permute-start.19 = (f32[128,512]{1,0:T(8,128)S(1)}, f32[128,512]{1,0:T(8,128)S(1)}, u32[]{:S(2)}, u32[]{:S(2)}) collective-permute-start(f32[128,512]{1,0:T(8,128)S(1)} %bits_mm.23), channel_id=1, source_target_pairs={{0,16},{16,0},{32,48},{48,32},{64,80},{80,64},{96,112},{112,96},{1... | collective-permute-start | bytes 786440 | tf_op jit(solution)/shard_map/ppermute | solution.py:50
  57.0 11.8 %collective-permute-start.18 = (f32[128,512]{1,0:T(8,128)S(1)}, f32[128,512]{1,0:T(8,128)S(1)}, u32[]{:S(2)}, u32[]{:S(2)}) collective-permute-start(f32[128,512]{1,0:T(8,128)S(1)} %bits_mm.15), channel_id=1, source_target_pairs={{0,16},{16,0},{32,48},{48,32},{64,80},{80,64},{96,112},{112,96},{1... | collective-permute-start | bytes 786440 | tf_op jit(solution)/shard_map/ppermute | solution.py:50
  57.6 8.7 %collective-permute-start.21 = (f32[128,512]{1,0:T(8,128)S(1)}, f32[128,512]{1,0:T(8,128)S(1)}, u32[]{:S(2)}, u32[]{:S(2)}) collective-permute-start(f32[128,512]{1,0:T(8,128)S(1)} %add.13), channel_id=1, source_target_pairs={{0,32},{16,112},{32,64},{48,16},{64,96},{80,48},{96,0},{112,80},{1... | collective-permute-start | bytes 786440 | tf_op jit(solution)/shard_map/ppermute | solution.py:46
  63.4 8.2 %collective-permute-start.24 = (f32[128,512]{1,0:T(8,128)S(1)}, f32[128,512]{1,0:T(8,128)S(1)}, u32[]{:S(2)}, u32[]{:S(2)}) collective-permute-start(f32[128,512]{1,0:T(8,128)S(1)} %add.15), channel_id=1, source_target_pairs={{0,96},{16,48},{32,0},{48,80},{64,32},{80,112},{96,64},{112,16},{1... | collective-permute-start | bytes 786440 | tf_op jit(solution)/shard_map/ppermute | solution.py:46
  66.4 8.4 %collective-permute-start.22 = (f32[128,512]{1,0:T(8,128)S(1)}, f32[128,512]{1,0:T(8,128)S(1)}, u32[]{:S(2)}, u32[]{:S(2)}) collective-permute-start(f32[128,512]{1,0:T(8,128)S(1)} %add_add_fusion), channel_id=1, source_target_pairs={{0,32},{16,112},{32,64},{48,16},{64,96},{80,48},{96,0},{112,80},{1... | collective-permute-start | bytes 786440 | tf_op jit(solution)/shard_map/ppermute | solution.py:46
  (1 other events, 1.6 us)

commit v5 on v4

v5 whole, which is shorter than its diff:
```python
import functools

import jax
import jax.numpy as jnp
from jax import lax
from jax.experimental import pallas as pl
from jax.experimental.pallas import tpu as pltpu
from jax.sharding import PartitionSpec as P


SIDE = 4
TILE = 256
CHUNK = 1024
TILES = CHUNK // TILE
BITS = 8

VM = pltpu.VMEM
FULL = pl.BlockSpec(memory_space=VM)

AXES = ("row", "col")


def place(x, y, z, core):
    return (z * 2 + core) * (SIDE * SIDE) + x * SIDE + y


def pairs(axis, flip=False):
    out = []
    for x in range(SIDE):
        for y in range(SIDE):
            for z in range(SIDE):
                for core in range(2):
                    at = [x, y, z]
                    if axis == "core":
                        out.append((place(*at, core), place(*at, 1 - core)))
                        continue
                    n = "xyz".index(axis)
                    step = 1 if (core == 0) != flip else -1
                    to = list(at)
                    to[n] = (to[n] + step) % SIDE
                    out.append((place(*at, core), place(*to, core)))
    return out


def send(value, axis, flip=False):
    return lax.ppermute(value, AXES, pairs(axis, flip))


def swap(value):
    return lax.ppermute(value, AXES, pairs("core"))


def prep_kernel(f_ref, o_ref, s_ref):
    s_ref[...] = f_ref[...].astype(jnp.float32)
    for j in range(TILES):
        rows = []
        for b in range(BITS):
            scale = 2.0**-b if b < 7 else -(2.0**-7)
            rows.append(s_ref[pl.ds(8 * j + b, 32, stride=32), :] * scale)
        o_ref[j] = jnp.concatenate(rows, 0).T.astype(jnp.bfloat16)


def prep(f):
    return pl.pallas_call(
        prep_kernel,
        out_shape=VM((TILES, 128, TILE), jnp.bfloat16),
        in_specs=[FULL],
        out_specs=FULL,
        scratch_shapes=[pltpu.VMEM((CHUNK, 128), jnp.float32)],
        name="prep",
    )(f)


def split_kernel(a_hbm, v_hbm, o_ref, w_ref, buf, sem):
    rows = a_hbm.shape[0] // 512

    def fetch(r):
        return pltpu.make_async_copy(a_hbm.at[pl.ds(pl.multiple_of(512 * r, 512), 512)], buf.at[r], sem.at[r])

    for r in range(rows):
        fetch(r).start()
    seen = pltpu.make_async_copy(v_hbm, w_ref, sem.at[rows])
    seen.start()

    def step(r, carry):
        fetch(r).wait()
        for i in range(buf.shape[2] // 128):
            a = buf[r, :, 128 * i : 128 * i + 128]
            for j in range(4):
                part = (lax.shift_right_logical(a, 8 * j) if j else a).astype(jnp.int8).T
                for c in range(4):
                    o_ref[r, 16 * i + 4 * c + j] = part[32 * c : 32 * c + 32]
        return carry

    lax.fori_loop(0, rows, step, 0)
    seen.wait()


def split(adj, visited):
    d, w = adj.shape
    return pl.pallas_call(
        split_kernel,
        in_specs=[pl.BlockSpec(memory_space=pltpu.HBM)] * 2,
        out_specs=(FULL, FULL),
        out_shape=(VM((d // 512, w // 8, 32, 512), jnp.int8), VM(visited.shape, jnp.int32)),
        scratch_shapes=[pltpu.VMEM((d // 512, 512, w), jnp.int32), pltpu.SemaphoreType.DMA((d // 512 + 1,))],
        compiler_params=pltpu.CompilerParams(vmem_limit_bytes=32 << 20),
        name="split",
    )(*[pltpu.with_memory_space_constraint(v, pltpu.HBM) for v in (adj, visited)])


def here():
    row, col = lax.axis_index("row"), lax.axis_index("col")
    core = row & 1
    return col >> 2, col & 3, row >> 1, core, 1 - 2 * core


def expand(a_ref, r, where):
    parts = []
    for at in where:
        x = a_ref[r, at]
        for b in range(BITS):
            m = 1 << b if b < 7 else -128
            parts.append((x & jnp.int8(m)).astype(jnp.bfloat16))
    return jnp.concatenate(parts, 0)


def mm_kernel(*refs, jobs, arrays, started):
    a_ref, refs = refs[0], refs[1:]
    count = sum(started)
    accs, f_refs, outs = iter(refs[:count]), refs[count : count + arrays], refs[count + arrays :]
    x, y, z, core, s = here()
    where, left = {}, {}
    for _, tiles in jobs:
        for t in tiles:
            if t[2:4] not in where:
                (a, b), (c, d) = t[2:4]
                where[t[2:4]] = (((x + a * s + 2 * b) & 3) * SIDE + ((y + c * s + 2 * d) & 3)) * TILES
    for ((a, b, other), tiles), out, has in zip(jobs, outs, started):
        r = ((z + a * s + 2 * b) & 3) * 2 + (1 - core if other else core)
        if tiles not in left:
            left[tiles] = jnp.concatenate([f_refs[t[0]][t[1]] for t in tiles], 1)
        right = expand(a_ref, r, [where[t[2:4]] + t[4] for t in tiles])
        got = jnp.dot(left[tiles], right, preferred_element_type=jnp.float32)
        out[...] = next(accs)[...] + got if has else got


def mm(ab, accs, arrays, jobs):
    started = tuple(a is not None for a in accs)
    olds = [a for a in accs if a is not None]
    count = sum(len(t) for _, t in jobs)
    alias, k = {}, 0
    for n, has in enumerate(started):
        if has:
            k += 1
            alias[k] = n
    args = [ab] + olds + list(arrays)
    return pl.pallas_call(
        functools.partial(mm_kernel, jobs=jobs, arrays=len(arrays), started=started),
        out_shape=(VM((128, 512), jnp.float32),) * len(jobs),
        in_specs=[FULL] * len(args),
        out_specs=(FULL,) * len(jobs),
        input_output_aliases=alias,
        cost_estimate=pl.CostEstimate(flops=2 * 128 * TILE * count * 512, bytes_accessed=0, transcendentals=0),
        compiler_params=pltpu.CompilerParams(vmem_limit_bytes=32 << 20),
        name="bits_mm",
    )(*args)


def finish_kernel(a_ref, b_ref, c_ref, d_ref, v_ref, p_ref, o_ref):
    reached = a_ref[...] + b_ref[...] + c_ref[...] + d_ref[...]
    shift = lax.broadcasted_iota(jnp.int32, (32, 1), 0)
    rows = []
    words = []
    for w in range(4):
        got = reached[32 * w : 32 * w + 32]
        word = v_ref[w : w + 1]
        unseen = (lax.shift_right_arithmetic(jnp.broadcast_to(word, got.shape), jnp.broadcast_to(shift, got.shape)) & 1) == 0
        rows.append(jnp.where(unseen, got, 0.0))
        fresh = jnp.where(unseen & (got > 0), lax.shift_left(jnp.int32(1), jnp.broadcast_to(shift, got.shape)), 0)
        words.append(word | jnp.sum(fresh, 0, keepdims=True))
    p_ref[...] = jnp.concatenate(rows, 0).T
    o_ref[...] = jnp.concatenate(words, 0)


def finish(parts, visited):
    return pl.pallas_call(
        finish_kernel,
        out_shape=(jax.ShapeDtypeStruct((512, 128), jnp.float32), jax.ShapeDtypeStruct((4, 512), jnp.int32)),
        in_specs=[FULL] * 5,
        out_specs=(FULL, FULL),
        name="finish",
    )(*[pltpu.with_memory_space_constraint(v, VM) for v in (*parts, visited)])


O, M, Q, T = (0, 0), (-1, 0), (1, 0), (0, 1)
H0, H1, ALL = (0, 1), (2, 3), (0, 1, 2, 3)


def tiles(array, start, dx, dy, js):
    return tuple((array, start + n, dx, dy, j) for n, j in enumerate(js))


TWO, TWO_O, UP_O, DOWN_O = (0, 1, False), (0, 1, True), (-1, 0, True), (1, 0, True)
UP, DOWN, OWN, OWN_O = (1, 0, False), (-1, 0, False), (0, 0, False), (0, 0, True)
SOON = (TWO, TWO_O, DOWN_O, UP_O, DOWN)


def level(adjacency, frontier, visited):
    totals = {}

    def work(*jobs):
        used = sorted({t[0] for ts, _ in jobs for t in ts})
        each = tuple(
            (b, tuple((used.index(t[0]),) + t[1:] for t in ts)) for ts, blocks in jobs for b in blocks
        )
        got = mm(ab, [totals.get(b) for b, _ in each], [arrays[n] for n in used], each)
        totals.update(zip([b for b, _ in each], got))

    ft = prep(frontier)
    theirs = swap(ft)
    dx, dy = send(ft, "x"), send(ft, "y")
    ox, oy = send(theirs, "x"), send(theirs, "y")
    ab, seen = split(adjacency, visited)

    bx, by = send(dx, "x"), send(dy, "y")
    po = swap(jnp.concatenate([dx[0:2], dy[2:4]], 0))
    pn = swap(jnp.concatenate([ox, oy], 0))
    cx = send(jnp.concatenate([dy[2:4], pn[6:8], oy[2:4], po[2:4]], 0), "x")
    cy = send(jnp.concatenate([dx[0:2], pn[0:2], ox[0:2], po[0:2]], 0), "y")
    pb = swap(jnp.concatenate([bx[0:2], by[2:4]], 0))
    ex = send(jnp.concatenate([by[2:4], pb[2:4]], 0), "x")
    ey = send(jnp.concatenate([bx[0:2], pb[0:2]], 0), "y")
    hx, hy = send(cx[:4], "x"), send(cy[:4], "y")
    pc = swap(jnp.concatenate([cx[4:8], cy[4:8]], 0))
    gx, gy = send(ex[:2], "x"), send(ey[:2], "y")
    pe = swap(jnp.concatenate([ex[2:4], ey[2:4]], 0))
    arrays = [ft, dx, pn, dy, bx, by, cx, cy, pc, ex, ey, pe, hx, hy, gx, gy]

    own = tiles(0, 0, O, O, ALL)
    n1, n2 = tiles(1, 0, M, O, ALL), tiles(3, 0, O, M, ALL)
    n3, n4 = tiles(2, 0, Q, O, ALL), tiles(2, 4, O, Q, ALL)
    fa = tiles(4, 0, T, O, ALL) + tiles(5, 0, O, T, ALL)
    fb = tiles(6, 0, M, M, H1) + tiles(6, 2, M, Q, H1) + tiles(7, 0, M, M, H0) + tiles(7, 2, Q, M, H0)
    sd = tiles(8, 0, Q, Q, H1) + tiles(8, 2, Q, M, H1) + tiles(8, 4, Q, Q, H0) + tiles(8, 6, M, Q, H0)
    sd = sd + tiles(9, 0, M, T, H1) + tiles(10, 0, T, M, H0) + tiles(11, 0, Q, T, H1) + tiles(11, 2, T, Q, H0)
    la = tiles(12, 0, T, M, H1) + tiles(12, 2, T, Q, H1) + tiles(13, 0, M, T, H0) + tiles(13, 2, Q, T, H0)
    la = la + tiles(14, 0, T, T, H1) + tiles(15, 0, T, T, H0)
    rest = n1 + n2 + n3 + n4 + fa + fb + sd + la

    work((own, SOON))
    work((n1, SOON))
    work((n2, SOON))
    work((n3, SOON))
    work((n4, SOON))
    work((fa, SOON))
    work((fb, SOON))
    work((sd, (TWO, TWO_O)))
    work((la, (TWO_O, TWO)))
    work((sd + la, (DOWN_O,)))
    work((sd + la, (DOWN,)))
    work((sd + la, (UP_O,)))
    work((own + rest, (UP,)))
    work((own + rest, (OWN_O,)))
    work((own + rest, (OWN,)))

    hop = send(totals[TWO] + swap(totals[TWO_O]), "z")
    got0 = send(totals[DOWN] + swap(totals[DOWN_O]), "z", True)
    got1 = send(totals[UP] + swap(totals[UP_O]) + hop, "z")
    last = swap(totals[OWN_O])
    return finish([totals[OWN], last, got1, got0], seen)


def solution(mesh):
    placed = (P("col", "row"), P(("row", "col"), None), P(None, ("col", "row")))
    return jax.shard_map(
        level,
        mesh=mesh,
        in_specs=placed,
        out_specs=(P(("col", "row"), None), P(None, ("col", "row"))),
        check_vma=False,
    )
```

time: 75.9 us -> 79.2 us (1.043)
  the two profiles are of different devices: /device:TPU:6 before, /device:TPU:1 now
where the time goes in v5:
time: 79.2 us; the launch traced here: 77.9 us
  starting transfers between devices  36.5 us (46%)
  Pallas kernels  27.1 us (34%)
  waiting for transfers between devices  12.5 us (16%)
  between operations  1.04 us (1%)
    ppermute x17, starting transfers between devices, send(): return lax.ppermute(value, AXES, pairs(axis, flip))  28.5 us
    pallas_call x15, Pallas kernels, mm(): pl.pallas_call(functools.partial(mm_kernel, jobs=jobs, arrays=len(arrays)...  20.7 us
    ppermute x17, waiting for transfers between devices, send(): return lax.ppermute(value, AXES, pairs(axis, flip))  12.5 us
    ppermute x10, starting transfers between devices, swap(): return lax.ppermute(value, AXES, pairs('core'))  8.01 us
    pallas_call x1, Pallas kernels, split(): pl.pallas_call(split_kernel, in_specs=[pl.BlockSpec(memory_space=pltpu.HB...  4.18 us
  transfers between devices with their start and end apart: 27, of which 7 were waited for; matrix products, arithmetic and copies ran while one was open for 1% of the time, Pallas kernels for 30%

profile of v5, /device:TPU:1, one launch (start us, length us, event | category | flops | bytes accessed | tf_op | source)
XLA Modules:
  0.0 77.9 jit_solution(5590302611196620981)
XLA Ops:
  2.0 3.6 %collective-permute-start.5 = (bf16[4,128,256]{2,1,0:T(8,128)(2,1)S(1)}, bf16[4,128,256]{2,1,0:T(8,128)(2,1)S(1)}, u32[]{:S(2)}, u32[]{:S(2)}) collective-permute-start(bf16[4,128,256]{2,1,0:T(8,128)(2,1)S(1)} %prep.1.refs_1_), channel_id=1, source_target_pairs={{0,1},{16,19},{32,33},{48,51},{64,65},{80,83},{96,97},{112,115},{1... | collective-permute-start | bytes 786440 | tf_op jit(solution)/shard_map/ppermute | solution.py:46
  5.6 2.5 %collective-permute-start = (bf16[4,128,256]{2,1,0:T(8,128)(2,1)S(1)}, bf16[4,128,256]{2,1,0:T(8,128)(2,1)S(1)}, u32[]{:S(2)}, u32[]{:S(2)}) collective-permute-start(bf16[4,128,256]{2,1,0:T(8,128)(2,1)S(1)} %prep.1.refs_1_), channel_id=1, source_target_pairs={{0,4},{16,28},{32,36},{48,60},{64,68},{80,92},{96,100},{112,124},{... | collective-permute-start | bytes 786440 | tf_op jit(solution)/shard_map/ppermute | solution.py:46
  8.9 3.4 %collective-permute-start.7 = (bf16[4,128,256]{2,1,0:T(8,128)(2,1)S(1)}, bf16[4,128,256]{2,1,0:T(8,128)(2,1)S(1)}, u32[]{:S(2)}, u32[]{:S(2)}) collective-permute-start(bf16[4,128,256]{2,1,0:T(8,128)(2,1)S(1)} %collective-permute-done.5.refs_4_.refs_6_), channel_id=1, source_target_pairs={{0,1},{16,19},{32,33},{48,51},{64,65},{80,83},{96,97},{112,115},{1... | collective-permute-start | bytes 786440 | tf_op jit(solution)/shard_map/ppermute | solution.py:46
  12.3 2.2 %collective-permute-start.6 = (bf16[4,128,256]{2,1,0:T(8,128)(2,1)S(1)}, bf16[4,128,256]{2,1,0:T(8,128)(2,1)S(1)}, u32[]{:S(2)}, u32[]{:S(2)}) collective-permute-start(bf16[4,128,256]{2,1,0:T(8,128)(2,1)S(1)} %collective-permute-done.refs_2_.refs_6_), channel_id=1, source_target_pairs={{0,4},{16,28},{32,36},{48,60},{64,68},{80,92},{96,100},{112,124},{... | collective-permute-start | bytes 786440 | tf_op jit(solution)/shard_map/ppermute | solution.py:46
  14.5 4.2 %split.1 = (s8[8,64,32,512]{3,2,1,0:T(32,128)(4,1)S(1)}, s32[4,512]{1,0:T(4,128)S(1)}) custom-call(s32[4096,512]{1,0:T(8,128)} %a_hbm.1, s32[4,512]{1,0:T(4,128)} %v_hbm.1), custom_call_target="tpu_custom_call" | custom-call | tf_op jit(solution)/shard_map/split/pallas_call | solution.py:101
  22.5 2.7 %collective-permute-done.2 = bf16[4,128,256]{2,1,0:T(8,128)(2,1)S(1)} collective-permute-done((bf16[4,128,256]{2,1,0:T(8,128)(2,1)S(1)}, bf16[4,128,256]{2,1,0:T(8,128)(2,1)S(1)}, u32[]{:S(2)}, u32[]{:S(2)}) %collective-permute-start.2) | collective-permute-done | bytes 262176 | tf_op jit(solution)/shard_map/ppermute | solution.py:46
  25.8 1.6 %collective-permute-start.4 = (bf16[8,128,256]{2,1,0:T(8,128)(2,1)S(1)}, bf16[8,128,256]{2,1,0:T(8,128)(2,1)S(1)}, u32[]{:S(2)}, u32[]{:S(2)}) collective-permute-start(bf16[8,128,256]{2,1,0:T(8,128)(2,1)S(1)} %pad_maximum_fusion), channel_id=1, source_target_pairs={{0,16},{16,0},{32,48},{48,32},{64,80},{80,64},{96,112},{112,96},{1... | collective-permute-start | bytes 1572872 | tf_op jit(solution)/shard_map/ppermute | solution.py:50
  27.5 1.5 %collective-permute-start.13 = (bf16[4,128,256]{2,1,0:T(8,128)(2,1)S(1)}, bf16[4,128,256]{2,1,0:T(8,128)(2,1)S(1)}, u32[]{:S(2)}, u32[]{:S(2)}) collective-permute-start(bf16[4,128,256]{2,1,0:T(8,128)(2,1)S(1)} %pad_maximum_fusion.7), channel_id=1, source_target_pairs={{0,4},{16,28},{32,36},{48,60},{64,68},{80,92},{96,100},{112,124},{... | collective-permute-start | bytes 786440 | tf_op jit(solution)/shard_map/ppermute | solution.py:46
  29.1 1.5 %collective-permute-start.10 = (bf16[8,128,256]{2,1,0:T(8,128)(2,1)S(1)}, bf16[8,128,256]{2,1,0:T(8,128)(2,1)S(1)}, u32[]{:S(2)}, u32[]{:S(2)}) collective-permute-start(bf16[8,128,256]{2,1,0:T(8,128)(2,1)S(1)} %pad_maximum_fusion.2), channel_id=1, source_target_pairs={{0,1},{16,19},{32,33},{48,51},{64,65},{80,83},{96,97},{112,115},{1... | collective-permute-start | bytes 1572872 | tf_op jit(solution)/shard_map/ppermute | solution.py:46
  31.6 1.4 %collective-permute-start.9 = (bf16[8,128,256]{2,1,0:T(8,128)(2,1)S(1)}, bf16[8,128,256]{2,1,0:T(8,128)(2,1)S(1)}, u32[]{:S(2)}, u32[]{:S(2)}) collective-permute-start(bf16[8,128,256]{2,1,0:T(8,128)(2,1)S(1)} %pad_maximum_fusion.1), channel_id=1, source_target_pairs={{0,4},{16,28},{32,36},{48,60},{64,68},{80,92},{96,100},{112,124},{... | collective-permute-start | bytes 1572872 | tf_op jit(solution)/shard_map/ppermute | solution.py:46
  33.6 2.2 %collective-permute-start.18 = (bf16[2,128,256]{2,1,0:T(8,128)(2,1)S(1)}, bf16[2,128,256]{2,1,0:T(8,128)(2,1)S(1)}, u32[]{:S(2)}, u32[]{:S(2)}) collective-permute-start(bf16[2,128,256]{2,1,0:T(8,128)(2,1)S(1)} %get-tuple-element.92), channel_id=1, source_target_pairs={{0,4},{16,28},{32,36},{48,60},{64,68},{80,92},{96,100},{112,124},{... | collective-permute-start | bytes 393224 | tf_op jit(solution)/shard_map/ppermute | solution.py:46
  35.8 1.7 %collective-permute-done.10.refs_8_.refs_7_ = bf16[8,128,256]{2,1,0:T(8,128)(2,1)S(1)} collective-permute-done((bf16[8,128,256]{2,1,0:T(8,128)(2,1)S(1)}, bf16[8,128,256]{2,1,0:T(8,128)(2,1)S(1)}, u32[]{:S(2)}, u32[]{:S(2)}) %collective-permute-start.10) | collective-permute-done | bytes 524320 | tf_op jit(solution)/shard_map/ppermute | solution.py:46
  37.5 2.5 %collective-permute-done.9.refs_7_.refs_6_ = bf16[8,128,256]{2,1,0:T(8,128)(2,1)S(1)} collective-permute-done((bf16[8,128,256]{2,1,0:T(8,128)(2,1)S(1)}, bf16[8,128,256]{2,1,0:T(8,128)(2,1)S(1)}, u32[]{:S(2)}, u32[]{:S(2)}) %collective-permute-start.9) | collective-permute-done | bytes 524320 | tf_op jit(solution)/shard_map/ppermute | solution.py:46
  43.7 1.5 %collective-permute-start.16 = (bf16[4,128,256]{2,1,0:T(8,128)(2,1)S(1)}, bf16[4,128,256]{2,1,0:T(8,128)(2,1)S(1)}, u32[]{:S(2)}, u32[]{:S(2)}) collective-permute-start(bf16[4,128,256]{2,1,0:T(8,128)(2,1)S(1)} %get-tuple-element.86), channel_id=1, source_target_pairs={{0,4},{16,28},{32,36},{48,60},{64,68},{80,92},{96,100},{112,124},{... | collective-permute-start | bytes 786440 | tf_op jit(solution)/shard_map/ppermute | solution.py:46
  46.7 1.6 %bits_mm.23 = (f32[128,512]{1,0:T(8,128)S(1)}, f32[128,512]{1,0:T(8,128)S(1)}, f32[128,512]{1,0:T(8,128)S(1)}, f32[128,512]{1,0:T(8,128)S(1)}, f32[128,512]{1,0:T(8,128)S(1)}) custom-call(s8[8,64,32,512]{3,2,1,0:T(32,128)(4,1)S(1)} %get-tuple-element.43.refs_0_, ...), custom_call_target="tpu_custom_call", output_to_operand_aliasing={{0}: (1, {}), {1}: (2, {}), {2}: (3, {}), {3}: (4, {}), {4}... | custom-call | flops 1342177280 | tf_op jit(solution)/shard_map/bits_mm/pallas_call | solution.py:158
  48.4 1.7 %bits_mm.24 = (f32[128,512]{1,0:T(8,128)S(1)}, f32[128,512]{1,0:T(8,128)S(1)}, f32[128,512]{1,0:T(8,128)S(1)}, f32[128,512]{1,0:T(8,128)S(1)}, f32[128,512]{1,0:T(8,128)S(1)}) custom-call(s8[8,64,32,512]{3,2,1,0:T(32,128)(4,1)S(1)} %get-tuple-element.43.refs_0_, ...), custom_call_target="tpu_custom_call", output_to_operand_aliasing={{0}: (1, {}), {1}: (2, {}), {2}: (3, {}), {3}: (4, {}), {4}... | custom-call | flops 1342177280 | tf_op jit(solution)/shard_map/bits_mm/pallas_call | solution.py:158
  50.1 2.1 %collective-permute-done.19.refs_16_.refs_9_.refs_6_ = bf16[2,128,256]{2,1,0:T(8,128)(2,1)S(1)} collective-permute-done((bf16[2,128,256]{2,1,0:T(8,128)(2,1)S(1)}, bf16[2,128,256]{2,1,0:T(8,128)(2,1)S(1)}, u32[]{:S(2)}, u32[]{:S(2)}) %collective-permute-start.19) | collective-permute-done | bytes 131104 | tf_op jit(solution)/shard_map/ppermute | solution.py:46
  53.3 1.9 %collective-permute-start.25 = (f32[128,512]{1,0:T(8,128)S(1)}, f32[128,512]{1,0:T(8,128)S(1)}, u32[]{:S(2)}, u32[]{:S(2)}) collective-permute-start(f32[128,512]{1,0:T(8,128)S(1)} %bits_mm.29), channel_id=1, source_target_pairs={{0,16},{16,0},{32,48},{48,32},{64,80},{80,64},{96,112},{112,96},{1... | collective-permute-start | bytes 786440 | tf_op jit(solution)/shard_map/ppermute | solution.py:50
  59.4 2.3 %bits_mm.16 = f32[128,512]{1,0:T(8,128)S(1)} custom-call(s8[8,64,32,512]{3,2,1,0:T(32,128)(4,1)S(1)} %get-tuple-element.43.refs_0_, bf16[4,128,256]{2,1,0:T(8,128)(2,1)S(1)} %prep.1.refs_1_, bf16[4,128,256]{2,1,0:T(8,128)(2,1)S(1)} %collective-permute-done.refs_2_.refs_6_, bf16[8,128,256]{2,1,0:T(8,128)(2,1)S(1)} %collective-permute-done.4.refs_3_.refs_6_, ...), custom_call_target="tpu_custom_call" | custom-call | flops 2147483648 | tf_op jit(solution)/shard_map/bits_mm/pallas_call | solution.py:158
  61.9 4.1 %collective-permute-start.23 = (f32[128,512]{1,0:T(8,128)S(1)}, f32[128,512]{1,0:T(8,128)S(1)}, u32[]{:S(2)}, u32[]{:S(2)}) collective-permute-start(f32[128,512]{1,0:T(8,128)S(1)} %add.13), channel_id=1, source_target_pairs={{0,32},{16,112},{32,64},{48,16},{64,96},{80,48},{96,0},{112,80},{1... | collective-permute-start | bytes 786440 | tf_op jit(solution)/shard_map/ppermute | solution.py:46
  67.0 2.3 %bits_mm.17 = f32[128,512]{1,0:T(8,128)S(1)} custom-call(s8[8,64,32,512]{3,2,1,0:T(32,128)(4,1)S(1)} %get-tuple-element.43.refs_0_, bf16[4,128,256]{2,1,0:T(8,128)(2,1)S(1)} %prep.1.refs_1_, bf16[4,128,256]{2,1,0:T(8,128)(2,1)S(1)} %collective-permute-done.refs_2_.refs_6_, bf16[8,128,256]{2,1,0:T(8,128)(2,1)S(1)} %collective-permute-done.4.refs_3_.refs_6_, ...), custom_call_target="tpu_custom_call" | custom-call | flops 2147483648 | tf_op jit(solution)/shard_map/bits_mm/pallas_call | solution.py:158
  69.6 2.8 %collective-permute-start.24 = (f32[128,512]{1,0:T(8,128)S(1)}, f32[128,512]{1,0:T(8,128)S(1)}, u32[]{:S(2)}, u32[]{:S(2)}) collective-permute-start(f32[128,512]{1,0:T(8,128)S(1)} %add_add_fusion), channel_id=1, source_target_pairs={{0,32},{16,112},{32,64},{48,16},{64,96},{80,48},{96,0},{112,80},{1... | collective-permute-start | bytes 786440 | tf_op jit(solution)/shard_map/ppermute | solution.py:46
  72.5 2.3 %bits_mm.15.a_ref = f32[128,512]{1,0:T(8,128)S(1)} custom-call(s8[8,64,32,512]{3,2,1,0:T(32,128)(4,1)S(1)} %get-tuple-element.43.refs_0_, bf16[4,128,256]{2,1,0:T(8,128)(2,1)S(1)} %prep.1.refs_1_, bf16[4,128,256]{2,1,0:T(8,128)(2,1)S(1)} %collective-permute-done.refs_2_.refs_6_, bf16[8,128,256]{2,1,0:T(8,128)(2,1)S(1)} %collective-permute-done.4.refs_3_.refs_6_, ...), custom_call_target="tpu_custom_call" | custom-call | flops 2147483648 | tf_op jit(solution)/shard_map/bits_mm/pallas_call | solution.py:158
  74.8 2.2 %collective-permute-done.26.d_ref = f32[128,512]{1,0:T(8,128)S(1)} collective-permute-done((f32[128,512]{1,0:T(8,128)S(1)}, f32[128,512]{1,0:T(8,128)S(1)}, u32[]{:S(2)}, u32[]{:S(2)}) %collective-permute-start.26) | collective-permute-done | bytes 262176 | tf_op jit(solution)/shard_map/ppermute | solution.py:46
  (73 shorter events, 21.0 us)
Async XLA Ops:
  2.0 6.9 %collective-permute-start.5 = (bf16[4,128,256]{2,1,0:T(8,128)(2,1)S(1)}, bf16[4,128,256]{2,1,0:T(8,128)(2,1)S(1)}, u32[]{:S(2)}, u32[]{:S(2)}) collective-permute-start(bf16[4,128,256]{2,1,0:T(8,128)(2,1)S(1)} %prep.1.refs_1_), channel_id=1, source_target_pairs={{0,1},{16,19},{32,33},{48,51},{64,65},{80,83},{96,97},{112,115},{1... | collective-permute-start | bytes 786440 | tf_op jit(solution)/shard_map/ppermute | solution.py:46
  5.6 6.7 %collective-permute-start = (bf16[4,128,256]{2,1,0:T(8,128)(2,1)S(1)}, bf16[4,128,256]{2,1,0:T(8,128)(2,1)S(1)}, u32[]{:S(2)}, u32[]{:S(2)}) collective-permute-start(bf16[4,128,256]{2,1,0:T(8,128)(2,1)S(1)} %prep.1.refs_1_), channel_id=1, source_target_pairs={{0,4},{16,28},{32,36},{48,60},{64,68},{80,92},{96,100},{112,124},{... | collective-permute-start | bytes 786440 | tf_op jit(solution)/shard_map/ppermute | solution.py:46
  8.1 11.5 %collective-permute-start.1 = (bf16[4,128,256]{2,1,0:T(8,128)(2,1)S(1)}, bf16[4,128,256]{2,1,0:T(8,128)(2,1)S(1)}, u32[]{:S(2)}, u32[]{:S(2)}) collective-permute-start(bf16[4,128,256]{2,1,0:T(8,128)(2,1)S(1)} %prep.1.refs_1_), channel_id=1, source_target_pairs={{0,16},{16,0},{32,48},{48,32},{64,80},{80,64},{96,112},{112,96},{1... | collective-permute-start | bytes 786440 | tf_op jit(solution)/shard_map/ppermute | solution.py:50
  8.9 13.4 %collective-permute-start.7 = (bf16[4,128,256]{2,1,0:T(8,128)(2,1)S(1)}, bf16[4,128,256]{2,1,0:T(8,128)(2,1)S(1)}, u32[]{:S(2)}, u32[]{:S(2)}) collective-permute-start(bf16[4,128,256]{2,1,0:T(8,128)(2,1)S(1)} %collective-permute-done.5.refs_4_.refs_6_), channel_id=1, source_target_pairs={{0,1},{16,19},{32,33},{48,51},{64,65},{80,83},{96,97},{112,115},{1... | collective-permute-start | bytes 786440 | tf_op jit(solution)/shard_map/ppermute | solution.py:46
  12.3 10.0 %collective-permute-start.6 = (bf16[4,128,256]{2,1,0:T(8,128)(2,1)S(1)}, bf16[4,128,256]{2,1,0:T(8,128)(2,1)S(1)}, u32[]{:S(2)}, u32[]{:S(2)}) collective-permute-start(bf16[4,128,256]{2,1,0:T(8,128)(2,1)S(1)} %collective-permute-done.refs_2_.refs_6_), channel_id=1, source_target_pairs={{0,4},{16,28},{32,36},{48,60},{64,68},{80,92},{96,100},{112,124},{... | collective-permute-start | bytes 786440 | tf_op jit(solution)/shard_map/ppermute | solution.py:46
  19.6 5.6 %collective-permute-start.2 = (bf16[4,128,256]{2,1,0:T(8,128)(2,1)S(1)}, bf16[4,128,256]{2,1,0:T(8,128)(2,1)S(1)}, u32[]{:S(2)}, u32[]{:S(2)}) collective-permute-start(bf16[4,128,256]{2,1,0:T(8,128)(2,1)S(1)} %collective-permute-done.1), channel_id=1, source_target_pairs={{0,4},{16,28},{32,36},{48,60},{64,68},{80,92},{96,100},{112,124},{... | collective-permute-start | bytes 786440 | tf_op jit(solution)/shard_map/ppermute | solution.py:46
  20.2 5.5 %collective-permute-start.3 = (bf16[4,128,256]{2,1,0:T(8,128)(2,1)S(1)}, bf16[4,128,256]{2,1,0:T(8,128)(2,1)S(1)}, u32[]{:S(2)}, u32[]{:S(2)}) collective-permute-start(bf16[4,128,256]{2,1,0:T(8,128)(2,1)S(1)} %collective-permute-done.1), channel_id=1, source_target_pairs={{0,1},{16,19},{32,33},{48,51},{64,65},{80,83},{96,97},{112,115},{1... | collective-permute-start | bytes 786440 | tf_op jit(solution)/shard_map/ppermute | solution.py:46
  20.3 7.1 %collective-permute-start.8 = (bf16[4,128,256]{2,1,0:T(8,128)(2,1)S(1)}, bf16[4,128,256]{2,1,0:T(8,128)(2,1)S(1)}, u32[]{:S(2)}, u32[]{:S(2)}) collective-permute-start(bf16[4,128,256]{2,1,0:T(8,128)(2,1)S(1)} %pad_maximum_fusion.6), channel_id=1, source_target_pairs={{0,16},{16,0},{32,48},{48,32},{64,80},{80,64},{96,112},{112,96},{1... | collective-permute-start | bytes 786440 | tf_op jit(solution)/shard_map/ppermute | solution.py:50
  27.5 6.1 %collective-permute-start.13 = (bf16[4,128,256]{2,1,0:T(8,128)(2,1)S(1)}, bf16[4,128,256]{2,1,0:T(8,128)(2,1)S(1)}, u32[]{:S(2)}, u32[]{:S(2)}) collective-permute-start(bf16[4,128,256]{2,1,0:T(8,128)(2,1)S(1)} %pad_maximum_fusion.7), channel_id=1, source_target_pairs={{0,4},{16,28},{32,36},{48,60},{64,68},{80,92},{96,100},{112,124},{... | collective-permute-start | bytes 786440 | tf_op jit(solution)/shard_map/ppermute | solution.py:46
  29.1 8.4 %collective-permute-start.10 = (bf16[8,128,256]{2,1,0:T(8,128)(2,1)S(1)}, bf16[8,128,256]{2,1,0:T(8,128)(2,1)S(1)}, u32[]{:S(2)}, u32[]{:S(2)}) collective-permute-start(bf16[8,128,256]{2,1,0:T(8,128)(2,1)S(1)} %pad_maximum_fusion.2), channel_id=1, source_target_pairs={{0,1},{16,19},{32,33},{48,51},{64,65},{80,83},{96,97},{112,115},{1... | collective-permute-start | bytes 1572872 | tf_op jit(solution)/shard_map/ppermute | solution.py:46
  31.6 8.4 %collective-permute-start.9 = (bf16[8,128,256]{2,1,0:T(8,128)(2,1)S(1)}, bf16[8,128,256]{2,1,0:T(8,128)(2,1)S(1)}, u32[]{:S(2)}, u32[]{:S(2)}) collective-permute-start(bf16[8,128,256]{2,1,0:T(8,128)(2,1)S(1)} %pad_maximum_fusion.1), channel_id=1, source_target_pairs={{0,4},{16,28},{32,36},{48,60},{64,68},{80,92},{96,100},{112,124},{... | collective-permute-start | bytes 1572872 | tf_op jit(solution)/shard_map/ppermute | solution.py:46
  33.0 8.4 %collective-permute-start.14 = (bf16[4,128,256]{2,1,0:T(8,128)(2,1)S(1)}, bf16[4,128,256]{2,1,0:T(8,128)(2,1)S(1)}, u32[]{:S(2)}, u32[]{:S(2)}) collective-permute-start(bf16[4,128,256]{2,1,0:T(8,128)(2,1)S(1)} %pad_maximum_fusion.4), channel_id=1, source_target_pairs={{0,1},{16,19},{32,33},{48,51},{64,65},{80,83},{96,97},{112,115},{1... | collective-permute-start | bytes 786440 | tf_op jit(solution)/shard_map/ppermute | solution.py:46
  33.6 12.9 %collective-permute-start.18 = (bf16[2,128,256]{2,1,0:T(8,128)(2,1)S(1)}, bf16[2,128,256]{2,1,0:T(8,128)(2,1)S(1)}, u32[]{:S(2)}, u32[]{:S(2)}) collective-permute-start(bf16[2,128,256]{2,1,0:T(8,128)(2,1)S(1)} %get-tuple-element.92), channel_id=1, source_target_pairs={{0,4},{16,28},{32,36},{48,60},{64,68},{80,92},{96,100},{112,124},{... | collective-permute-start | bytes 393224 | tf_op jit(solution)/shard_map/ppermute | solution.py:46
  40.1 12.1 %collective-permute-start.11 = (bf16[8,128,256]{2,1,0:T(8,128)(2,1)S(1)}, bf16[8,128,256]{2,1,0:T(8,128)(2,1)S(1)}, u32[]{:S(2)}, u32[]{:S(2)}) collective-permute-start(bf16[8,128,256]{2,1,0:T(8,128)(2,1)S(1)} %pad_maximum_fusion.3), channel_id=1, source_target_pairs={{0,16},{16,0},{32,48},{48,32},{64,80},{80,64},{96,112},{112,96},{1... | collective-permute-start | bytes 1572872 | tf_op jit(solution)/shard_map/ppermute | solution.py:50
  41.5 10.6 %collective-permute-start.15 = (bf16[4,128,256]{2,1,0:T(8,128)(2,1)S(1)}, bf16[4,128,256]{2,1,0:T(8,128)(2,1)S(1)}, u32[]{:S(2)}, u32[]{:S(2)}) collective-permute-start(bf16[4,128,256]{2,1,0:T(8,128)(2,1)S(1)} %pad_maximum_fusion.8), channel_id=1, source_target_pairs={{0,16},{16,0},{32,48},{48,32},{64,80},{80,64},{96,112},{112,96},{1... | collective-permute-start | bytes 786440 | tf_op jit(solution)/shard_map/ppermute | solution.py:50
  43.7 8.5 %collective-permute-start.16 = (bf16[4,128,256]{2,1,0:T(8,128)(2,1)S(1)}, bf16[4,128,256]{2,1,0:T(8,128)(2,1)S(1)}, u32[]{:S(2)}, u32[]{:S(2)}) collective-permute-start(bf16[4,128,256]{2,1,0:T(8,128)(2,1)S(1)} %get-tuple-element.86), channel_id=1, source_target_pairs={{0,4},{16,28},{32,36},{48,60},{64,68},{80,92},{96,100},{112,124},{... | collective-permute-start | bytes 786440 | tf_op jit(solution)/shard_map/ppermute | solution.py:46
  45.2 6.9 %collective-permute-start.17 = (bf16[4,128,256]{2,1,0:T(8,128)(2,1)S(1)}, bf16[4,128,256]{2,1,0:T(8,128)(2,1)S(1)}, u32[]{:S(2)}, u32[]{:S(2)}) collective-permute-start(bf16[4,128,256]{2,1,0:T(8,128)(2,1)S(1)} %get-tuple-element.84), channel_id=1, source_target_pairs={{0,1},{16,19},{32,33},{48,51},{64,65},{80,83},{96,97},{112,115},{1... | collective-permute-start | bytes 786440 | tf_op jit(solution)/shard_map/ppermute | solution.py:46
  46.5 5.7 %collective-permute-start.19 = (bf16[2,128,256]{2,1,0:T(8,128)(2,1)S(1)}, bf16[2,128,256]{2,1,0:T(8,128)(2,1)S(1)}, u32[]{:S(2)}, u32[]{:S(2)}) collective-permute-start(bf16[2,128,256]{2,1,0:T(8,128)(2,1)S(1)} %get-tuple-element.90), channel_id=1, source_target_pairs={{0,1},{16,19},{32,33},{48,51},{64,65},{80,83},{96,97},{112,115},{1... | collective-permute-start | bytes 393224 | tf_op jit(solution)/shard_map/ppermute | solution.py:46
  53.3 16.1 %collective-permute-start.25 = (f32[128,512]{1,0:T(8,128)S(1)}, f32[128,512]{1,0:T(8,128)S(1)}, u32[]{:S(2)}, u32[]{:S(2)}) collective-permute-start(f32[128,512]{1,0:T(8,128)S(1)} %bits_mm.29), channel_id=1, source_target_pairs={{0,16},{16,0},{32,48},{48,32},{64,80},{80,64},{96,112},{112,96},{1... | collective-permute-start | bytes 786440 | tf_op jit(solution)/shard_map/ppermute | solution.py:50
  58.8 10.7 %collective-permute-start.21 = (f32[128,512]{1,0:T(8,128)S(1)}, f32[128,512]{1,0:T(8,128)S(1)}, u32[]{:S(2)}, u32[]{:S(2)}) collective-permute-start(f32[128,512]{1,0:T(8,128)S(1)} %bits_mm.25), channel_id=1, source_target_pairs={{0,16},{16,0},{32,48},{48,32},{64,80},{80,64},{96,112},{112,96},{1... | collective-permute-start | bytes 786440 | tf_op jit(solution)/shard_map/ppermute | solution.py:50
  61.7 13.1 %collective-permute-start.20 = (f32[128,512]{1,0:T(8,128)S(1)}, f32[128,512]{1,0:T(8,128)S(1)}, u32[]{:S(2)}, u32[]{:S(2)}) collective-permute-start(f32[128,512]{1,0:T(8,128)S(1)} %bits_mm.16), channel_id=1, source_target_pairs={{0,16},{16,0},{32,48},{48,32},{64,80},{80,64},{96,112},{112,96},{1... | collective-permute-start | bytes 786440 | tf_op jit(solution)/shard_map/ppermute | solution.py:50
  61.9 7.7 %collective-permute-start.23 = (f32[128,512]{1,0:T(8,128)S(1)}, f32[128,512]{1,0:T(8,128)S(1)}, u32[]{:S(2)}, u32[]{:S(2)}) collective-permute-start(f32[128,512]{1,0:T(8,128)S(1)} %add.13), channel_id=1, source_target_pairs={{0,32},{16,112},{32,64},{48,16},{64,96},{80,48},{96,0},{112,80},{1... | collective-permute-start | bytes 786440 | tf_op jit(solution)/shard_map/ppermute | solution.py:46
  69.5 7.5 %collective-permute-start.26 = (f32[128,512]{1,0:T(8,128)S(1)}, f32[128,512]{1,0:T(8,128)S(1)}, u32[]{:S(2)}, u32[]{:S(2)}) collective-permute-start(f32[128,512]{1,0:T(8,128)S(1)} %add.15), channel_id=1, source_target_pairs={{0,96},{16,48},{32,0},{48,80},{64,32},{80,112},{96,64},{112,16},{1... | collective-permute-start | bytes 786440 | tf_op jit(solution)/shard_map/ppermute | solution.py:46
  69.6 7.4 %collective-permute-start.24 = (f32[128,512]{1,0:T(8,128)S(1)}, f32[128,512]{1,0:T(8,128)S(1)}, u32[]{:S(2)}, u32[]{:S(2)}) collective-permute-start(f32[128,512]{1,0:T(8,128)S(1)} %add_add_fusion), channel_id=1, source_target_pairs={{0,32},{16,112},{32,64},{48,16},{64,96},{80,48},{96,0},{112,80},{1... | collective-permute-start | bytes 786440 | tf_op jit(solution)/shard_map/ppermute | solution.py:46
  (3 other events, 12.5 us)

commit v6 on v5

--- a/solution.py
+++ b/solution.py
@@ -224,18 +224,17 @@
     ab, seen = split(adjacency, visited)
 
     bx, by = send(dx, "x"), send(dy, "y")
-    po = swap(jnp.concatenate([dx[0:2], dy[2:4]], 0))
-    pn = swap(jnp.concatenate([ox, oy], 0))
+    pn = swap(jnp.concatenate([ox, oy, dx[0:2], dy[2:4]], 0))
+    po = pn[8:12]
     cx = send(jnp.concatenate([dy[2:4], pn[6:8], oy[2:4], po[2:4]], 0), "x")
     cy = send(jnp.concatenate([dx[0:2], pn[0:2], ox[0:2], po[0:2]], 0), "y")
     pb = swap(jnp.concatenate([bx[0:2], by[2:4]], 0))
     ex = send(jnp.concatenate([by[2:4], pb[2:4]], 0), "x")
     ey = send(jnp.concatenate([bx[0:2], pb[0:2]], 0), "y")
     hx, hy = send(cx[:4], "x"), send(cy[:4], "y")
-    pc = swap(jnp.concatenate([cx[4:8], cy[4:8]], 0))
     gx, gy = send(ex[:2], "x"), send(ey[:2], "y")
-    pe = swap(jnp.concatenate([ex[2:4], ey[2:4]], 0))
-    arrays = [ft, dx, pn, dy, bx, by, cx, cy, pc, ex, ey, pe, hx, hy, gx, gy]
+    pc = swap(jnp.concatenate([cx[4:8], cy[4:8], ex[2:4], ey[2:4]], 0))
+    arrays = [ft, dx, pn, dy, bx, by, cx, cy, pc, ex, ey, hx, hy, gx, gy]
 
     own = tiles(0, 0, O, O, ALL)
     n1, n2 = tiles(1, 0, M, O, ALL), tiles(3, 0, O, M, ALL)
@@ -243,24 +242,23 @@
     fa = tiles(4, 0, T, O, ALL) + tiles(5, 0, O, T, ALL)
     fb = tiles(6, 0, M, M, H1) + tiles(6, 2, M, Q, H1) + tiles(7, 0, M, M, H0) + tiles(7, 2, Q, M, H0)
     sd = tiles(8, 0, Q, Q, H1) + tiles(8, 2, Q, M, H1) + tiles(8, 4, Q, Q, H0) + tiles(8, 6, M, Q, H0)
-    sd = sd + tiles(9, 0, M, T, H1) + tiles(10, 0, T, M, H0) + tiles(11, 0, Q, T, H1) + tiles(11, 2, T, Q, H0)
-    la = tiles(12, 0, T, M, H1) + tiles(12, 2, T, Q, H1) + tiles(13, 0, M, T, H0) + tiles(13, 2, Q, T, H0)
-    la = la + tiles(14, 0, T, T, H1) + tiles(15, 0, T, T, H0)
+    sd = sd + tiles(9, 0, M, T, H1) + tiles(10, 0, T, M, H0) + tiles(8, 8, Q, T, H1) + tiles(8, 10, T, Q, H0)
+    la = tiles(11, 0, T, M, H1) + tiles(11, 2, T, Q, H1) + tiles(12, 0, M, T, H0) + tiles(12, 2, Q, T, H0)
+    la = la + tiles(13, 0, T, T, H1) + tiles(14, 0, T, T, H0)
     rest = n1 + n2 + n3 + n4 + fa + fb + sd + la
 
-    work((own, SOON))
-    work((n1, SOON))
+    work((own + n1, SOON))
     work((n2, SOON))
     work((n3, SOON))
-    work((n4, SOON))
-    work((fa, SOON))
+    work((n4 + fa, SOON))
     work((fb, SOON))
+    work((own + n1 + n2 + n3 + n4 + fa + fb, (UP,)))
     work((sd, (TWO, TWO_O)))
     work((la, (TWO_O, TWO)))
     work((sd + la, (DOWN_O,)))
     work((sd + la, (DOWN,)))
     work((sd + la, (UP_O,)))
-    work((own + rest, (UP,)))
+    work((sd + la, (UP,)))
     work((own + rest, (OWN_O,)))
     work((own + rest, (OWN,)))
 

time: 79.2 us -> 79.5 us (level)
  the two profiles are of different devices: /device:TPU:1 before, /device:TPU:4 now
where the time goes in v6:
time: 79.5 us; the launch traced here: 79.4 us
  starting transfers between devices  27.4 us (34%)
  Pallas kernels  26.8 us (34%)
  waiting for transfers between devices  23.4 us (29%)
  between operations  1 us (1%)
    ppermute x17, starting transfers between devices, send(): return lax.ppermute(value, AXES, pairs(axis, flip))  23.6 us
    ppermute x17, waiting for transfers between devices, send(): return lax.ppermute(value, AXES, pairs(axis, flip))  21.9 us
    pallas_call x14, Pallas kernels, mm(): pl.pallas_call(functools.partial(mm_kernel, jobs=jobs, arrays=len(arrays)...  20.3 us
    pallas_call x1, Pallas kernels, split(): pl.pallas_call(split_kernel, in_specs=[pl.BlockSpec(memory_space=pltpu.HB...  4.18 us
    ppermute x8, starting transfers between devices, swap(): return lax.ppermute(value, AXES, pairs('core'))  3.85 us
  transfers between devices with their start and end apart: 25, of which 10 were waited for; matrix products, arithmetic and copies ran while one was open for 1% of the time, Pallas kernels for 30%

profile of v6, /device:TPU:4, one launch (start us, length us, event | category | flops | bytes accessed | tf_op | source)
XLA Modules:
  0.0 79.4 jit_solution(8823655551709229280)
XLA Ops:
  0.6 1.3 %prep.1.refs_1_ = bf16[4,128,256]{2,1,0:T(8,128)(2,1)S(1)} custom-call(bf16[1024,128]{1,0:T(8,128)(2,1)} %f_ref.1), custom_call_target="tpu_custom_call" | custom-call | tf_op jit(solution)/shard_map/prep/pallas_call | solution.py:64
  2.1 1.6 %collective-permute-start.4 = (bf16[4,128,256]{2,1,0:T(8,128)(2,1)S(1)}, bf16[4,128,256]{2,1,0:T(8,128)(2,1)S(1)}, u32[]{:S(2)}, u32[]{:S(2)}) collective-permute-start(bf16[4,128,256]{2,1,0:T(8,128)(2,1)S(1)} %prep.1.refs_1_), channel_id=1, source_target_pairs={{0,1},{16,19},{32,33},{48,51},{64,65},{80,83},{96,97},{112,115},{1... | collective-permute-start | bytes 786440 | tf_op jit(solution)/shard_map/ppermute | solution.py:46
  5.4 1.6 %collective-permute-start.3 = (bf16[4,128,256]{2,1,0:T(8,128)(2,1)S(1)}, bf16[4,128,256]{2,1,0:T(8,128)(2,1)S(1)}, u32[]{:S(2)}, u32[]{:S(2)}) collective-permute-start(bf16[4,128,256]{2,1,0:T(8,128)(2,1)S(1)} %collective-permute-done.1), channel_id=1, source_target_pairs={{0,1},{16,19},{32,33},{48,51},{64,65},{80,83},{96,97},{112,115},{1... | collective-permute-start | bytes 786440 | tf_op jit(solution)/shard_map/ppermute | solution.py:46
  7.0 2.7 %collective-permute-done.4.refs_4_.refs_6_ = bf16[4,128,256]{2,1,0:T(8,128)(2,1)S(1)} collective-permute-done((bf16[4,128,256]{2,1,0:T(8,128)(2,1)S(1)}, bf16[4,128,256]{2,1,0:T(8,128)(2,1)S(1)}, u32[]{:S(2)}, u32[]{:S(2)}) %collective-permute-start.4) | collective-permute-done | bytes 262176 | tf_op jit(solution)/shard_map/ppermute | solution.py:46
  11.3 1.6 %collective-permute-done.2 = bf16[4,128,256]{2,1,0:T(8,128)(2,1)S(1)} collective-permute-done((bf16[4,128,256]{2,1,0:T(8,128)(2,1)S(1)}, bf16[4,128,256]{2,1,0:T(8,128)(2,1)S(1)}, u32[]{:S(2)}, u32[]{:S(2)}) %collective-permute-start.2) | collective-permute-done | bytes 262176 | tf_op jit(solution)/shard_map/ppermute | solution.py:46
  13.5 3.8 %collective-permute-done.7.refs_6_.refs_8_ = bf16[4,128,256]{2,1,0:T(8,128)(2,1)S(1)} collective-permute-done((bf16[4,128,256]{2,1,0:T(8,128)(2,1)S(1)}, bf16[4,128,256]{2,1,0:T(8,128)(2,1)S(1)}, u32[]{:S(2)}, u32[]{:S(2)}) %collective-permute-start.7) | collective-permute-done | bytes 262176 | tf_op jit(solution)/shard_map/ppermute | solution.py:46
  17.5 1.5 %collective-permute-done.10 = bf16[4,128,256]{2,1,0:T(8,128)(2,1)S(1)} collective-permute-done((bf16[4,128,256]{2,1,0:T(8,128)(2,1)S(1)}, bf16[4,128,256]{2,1,0:T(8,128)(2,1)S(1)}, u32[]{:S(2)}, u32[]{:S(2)}) %collective-permute-start.10) | collective-permute-done | bytes 262176 | tf_op jit(solution)/shard_map/ppermute | solution.py:50
  19.9 1.3 %collective-permute-start.11 = (bf16[4,128,256]{2,1,0:T(8,128)(2,1)S(1)}, bf16[4,128,256]{2,1,0:T(8,128)(2,1)S(1)}, u32[]{:S(2)}, u32[]{:S(2)}) collective-permute-start(bf16[4,128,256]{2,1,0:T(8,128)(2,1)S(1)} %pad_maximum_fusion.6), channel_id=1, source_target_pairs={{0,4},{16,28},{32,36},{48,60},{64,68},{80,92},{96,100},{112,124},{... | collective-permute-start | bytes 786440 | tf_op jit(solution)/shard_map/ppermute | solution.py:46
  22.7 3.0 %collective-permute-start.8 = (bf16[8,128,256]{2,1,0:T(8,128)(2,1)S(1)}, bf16[8,128,256]{2,1,0:T(8,128)(2,1)S(1)}, u32[]{:S(2)}, u32[]{:S(2)}) collective-permute-start(bf16[8,128,256]{2,1,0:T(8,128)(2,1)S(1)} %pad_maximum_fusion.2), channel_id=1, source_target_pairs={{0,4},{16,28},{32,36},{48,60},{64,68},{80,92},{96,100},{112,124},{... | collective-permute-start | bytes 1572872 | tf_op jit(solution)/shard_map/ppermute | solution.py:46
  26.8 5.6 %collective-permute-done.9.refs_8_.refs_7_ = bf16[8,128,256]{2,1,0:T(8,128)(2,1)S(1)} collective-permute-done((bf16[8,128,256]{2,1,0:T(8,128)(2,1)S(1)}, bf16[8,128,256]{2,1,0:T(8,128)(2,1)S(1)}, u32[]{:S(2)}, u32[]{:S(2)}) %collective-permute-start.9) | collective-permute-done | bytes 524320 | tf_op jit(solution)/shard_map/ppermute | solution.py:46
  32.6 4.2 %split.1 = (s8[8,64,32,512]{3,2,1,0:T(32,128)(4,1)S(1)}, s32[4,512]{1,0:T(4,128)S(1)}) custom-call(s32[4096,512]{1,0:T(8,128)} %a_hbm.1, s32[4,512]{1,0:T(4,128)} %v_hbm.1), custom_call_target="tpu_custom_call" | custom-call | tf_op jit(solution)/shard_map/split/pallas_call | solution.py:101
  36.8 1.5 %bits_mm.18 = (f32[128,512]{1,0:T(8,128)S(1)}, f32[128,512]{1,0:T(8,128)S(1)}, f32[128,512]{1,0:T(8,128)S(1)}, f32[128,512]{1,0:T(8,128)S(1)}, f32[128,512]{1,0:T(8,128)S(1)}) custom-call(s8[8,64,32,512]{3,2,1,0:T(32,128)(4,1)S(1)} %get-tuple-element.33.refs_0_, bf16[4,128,256]{2,1,0:T(8,128)(2,1)S(1)} %prep.1.refs_1_, ...), custom_call_target="tpu_custom_call" | custom-call | flops 1342177280 | tf_op jit(solution)/shard_map/bits_mm/pallas_call | solution.py:158
  39.3 2.5 %collective-permute-start.16 = (bf16[2,128,256]{2,1,0:T(8,128)(2,1)S(1)}, bf16[2,128,256]{2,1,0:T(8,128)(2,1)S(1)}, u32[]{:S(2)}, u32[]{:S(2)}) collective-permute-start(bf16[2,128,256]{2,1,0:T(8,128)(2,1)S(1)} %get-tuple-element.74), channel_id=1, source_target_pairs={{0,4},{16,28},{32,36},{48,60},{64,68},{80,92},{96,100},{112,124},{... | collective-permute-start | bytes 393224 | tf_op jit(solution)/shard_map/ppermute | solution.py:46
  43.3 3.2 %collective-permute-start.14 = (bf16[4,128,256]{2,1,0:T(8,128)(2,1)S(1)}, bf16[4,128,256]{2,1,0:T(8,128)(2,1)S(1)}, u32[]{:S(2)}, u32[]{:S(2)}) collective-permute-start(bf16[4,128,256]{2,1,0:T(8,128)(2,1)S(1)} %get-tuple-element.70), channel_id=1, source_target_pairs={{0,4},{16,28},{32,36},{48,60},{64,68},{80,92},{96,100},{112,124},{... | collective-permute-start | bytes 786440 | tf_op jit(solution)/shard_map/ppermute | solution.py:46
  46.7 2.3 %bits_mm.21 = (f32[128,512]{1,0:T(8,128)S(1)}, f32[128,512]{1,0:T(8,128)S(1)}, f32[128,512]{1,0:T(8,128)S(1)}, f32[128,512]{1,0:T(8,128)S(1)}, f32[128,512]{1,0:T(8,128)S(1)}) custom-call(s8[8,64,32,512]{3,2,1,0:T(32,128)(4,1)S(1)} %get-tuple-element.33.refs_0_, ...), custom_call_target="tpu_custom_call", output_to_operand_aliasing={{0}: (1, {}), {1}: (2, {}), {2}: (3, {}), {3}: (4, {}), {4}... | custom-call | flops 2013265920 | tf_op jit(solution)/shard_map/bits_mm/pallas_call | solution.py:158
  49.0 1.7 %bits_mm.22 = (f32[128,512]{1,0:T(8,128)S(1)}, f32[128,512]{1,0:T(8,128)S(1)}, f32[128,512]{1,0:T(8,128)S(1)}, f32[128,512]{1,0:T(8,128)S(1)}, f32[128,512]{1,0:T(8,128)S(1)}) custom-call(s8[8,64,32,512]{3,2,1,0:T(32,128)(4,1)S(1)} %get-tuple-element.33.refs_0_, ...), custom_call_target="tpu_custom_call", output_to_operand_aliasing={{0}: (1, {}), {1}: (2, {}), {2}: (3, {}), {3}: (4, {}), {4}... | custom-call | flops 1342177280 | tf_op jit(solution)/shard_map/bits_mm/pallas_call | solution.py:158
  52.0 2.1 %collective-permute-done.15.refs_13_.refs_6_.refs_4_ = bf16[4,128,256]{2,1,0:T(8,128)(2,1)S(1)} collective-permute-done((bf16[4,128,256]{2,1,0:T(8,128)(2,1)S(1)}, bf16[4,128,256]{2,1,0:T(8,128)(2,1)S(1)}, u32[]{:S(2)}, u32[]{:S(2)}) %collective-permute-start.15) | collective-permute-done | bytes 262176 | tf_op jit(solution)/shard_map/ppermute | solution.py:46
  55.3 1.4 %bits_mm.16.refs_1_ = f32[128,512]{1,0:T(8,128)S(1)} custom-call(s8[8,64,32,512]{3,2,1,0:T(32,128)(4,1)S(1)} %get-tuple-element.33.refs_0_, bf16[4,128,256]{2,1,0:T(8,128)(2,1)S(1)} %prep.1.refs_1_, bf16[4,128,256]{2,1,0:T(8,128)(2,1)S(1)} %collective-permute-done.refs_2_, bf16[12,128,256]{2,1,0:T(8,128)(2,1)S(1)} %collective-permute-done.5.refs_3_.refs_6_, ...), custom_call_target="tpu_custom_call" | custom-call | flops 1207959552 | tf_op jit(solution)/shard_map/bits_mm/pallas_call | solution.py:158
  59.7 2.2 %collective-permute-start.21 = (f32[128,512]{1,0:T(8,128)S(1)}, f32[128,512]{1,0:T(8,128)S(1)}, u32[]{:S(2)}, u32[]{:S(2)}) collective-permute-start(f32[128,512]{1,0:T(8,128)S(1)} %add.13), channel_id=1, source_target_pairs={{0,32},{16,112},{32,64},{48,16},{64,96},{80,48},{96,0},{112,80},{1... | collective-permute-start | bytes 786440 | tf_op jit(solution)/shard_map/ppermute | solution.py:46
  61.9 2.3 %bits_mm.15 = f32[128,512]{1,0:T(8,128)S(1)} custom-call(s8[8,64,32,512]{3,2,1,0:T(32,128)(4,1)S(1)} %get-tuple-element.33.refs_0_, bf16[4,128,256]{2,1,0:T(8,128)(2,1)S(1)} %prep.1.refs_1_, bf16[4,128,256]{2,1,0:T(8,128)(2,1)S(1)} %collective-permute-done.refs_2_, bf16[12,128,256]{2,1,0:T(8,128)(2,1)S(1)} %collective-permute-done.5.refs_3_.refs_6_, ...), custom_call_target="tpu_custom_call" | custom-call | flops 2147483648 | tf_op jit(solution)/shard_map/bits_mm/pallas_call | solution.py:158
  64.2 2.4 %collective-permute-start.18 = (f32[128,512]{1,0:T(8,128)S(1)}, f32[128,512]{1,0:T(8,128)S(1)}, u32[]{:S(2)}, u32[]{:S(2)}) collective-permute-start(f32[128,512]{1,0:T(8,128)S(1)} %bits_mm.15), channel_id=1, source_target_pairs={{0,16},{16,0},{32,48},{48,32},{64,80},{80,64},{96,112},{112,96},{1... | collective-permute-start | bytes 786440 | tf_op jit(solution)/shard_map/ppermute | solution.py:50
  69.5 1.7 %collective-permute-start.22 = (f32[128,512]{1,0:T(8,128)S(1)}, f32[128,512]{1,0:T(8,128)S(1)}, u32[]{:S(2)}, u32[]{:S(2)}) collective-permute-start(f32[128,512]{1,0:T(8,128)S(1)} %add_add_fusion), channel_id=1, source_target_pairs={{0,32},{16,112},{32,64},{48,16},{64,96},{80,48},{96,0},{112,80},{1... | collective-permute-start | bytes 786440 | tf_op jit(solution)/shard_map/ppermute | solution.py:46
  71.2 2.3 %bits_mm.14.a_ref = f32[128,512]{1,0:T(8,128)S(1)} custom-call(s8[8,64,32,512]{3,2,1,0:T(32,128)(4,1)S(1)} %get-tuple-element.33.refs_0_, bf16[4,128,256]{2,1,0:T(8,128)(2,1)S(1)} %prep.1.refs_1_, bf16[4,128,256]{2,1,0:T(8,128)(2,1)S(1)} %collective-permute-done.refs_2_, bf16[12,128,256]{2,1,0:T(8,128)(2,1)S(1)} %collective-permute-done.5.refs_3_.refs_6_, ...), custom_call_target="tpu_custom_call" | custom-call | flops 2147483648 | tf_op jit(solution)/shard_map/bits_mm/pallas_call | solution.py:158
  73.6 3.9 %collective-permute-done.24.d_ref = f32[128,512]{1,0:T(8,128)S(1)} collective-permute-done((f32[128,512]{1,0:T(8,128)S(1)}, f32[128,512]{1,0:T(8,128)S(1)}, u32[]{:S(2)}, u32[]{:S(2)}) %collective-permute-start.24) | collective-permute-done | bytes 262176 | tf_op jit(solution)/shard_map/ppermute | solution.py:46
  (65 shorter events, 20.6 us)
Async XLA Ops:
  2.0 2.9 %collective-permute-start.1 = (bf16[4,128,256]{2,1,0:T(8,128)(2,1)S(1)}, bf16[4,128,256]{2,1,0:T(8,128)(2,1)S(1)}, u32[]{:S(2)}, u32[]{:S(2)}) collective-permute-start(bf16[4,128,256]{2,1,0:T(8,128)(2,1)S(1)} %prep.1.refs_1_), channel_id=1, source_target_pairs={{0,16},{16,0},{32,48},{48,32},{64,80},{80,64},{96,112},{112,96},{1... | collective-permute-start | bytes 786440 | tf_op jit(solution)/shard_map/ppermute | solution.py:50
  2.1 7.7 %collective-permute-start.4 = (bf16[4,128,256]{2,1,0:T(8,128)(2,1)S(1)}, bf16[4,128,256]{2,1,0:T(8,128)(2,1)S(1)}, u32[]{:S(2)}, u32[]{:S(2)}) collective-permute-start(bf16[4,128,256]{2,1,0:T(8,128)(2,1)S(1)} %prep.1.refs_1_), channel_id=1, source_target_pairs={{0,1},{16,19},{32,33},{48,51},{64,65},{80,83},{96,97},{112,115},{1... | collective-permute-start | bytes 786440 | tf_op jit(solution)/shard_map/ppermute | solution.py:46
  3.7 6.4 %collective-permute-start = (bf16[4,128,256]{2,1,0:T(8,128)(2,1)S(1)}, bf16[4,128,256]{2,1,0:T(8,128)(2,1)S(1)}, u32[]{:S(2)}, u32[]{:S(2)}) collective-permute-start(bf16[4,128,256]{2,1,0:T(8,128)(2,1)S(1)} %prep.1.refs_1_), channel_id=1, source_target_pairs={{0,4},{16,28},{32,36},{48,60},{64,68},{80,92},{96,100},{112,124},{... | collective-permute-start | bytes 786440 | tf_op jit(solution)/shard_map/ppermute | solution.py:46
  4.9 8.0 %collective-permute-start.2 = (bf16[4,128,256]{2,1,0:T(8,128)(2,1)S(1)}, bf16[4,128,256]{2,1,0:T(8,128)(2,1)S(1)}, u32[]{:S(2)}, u32[]{:S(2)}) collective-permute-start(bf16[4,128,256]{2,1,0:T(8,128)(2,1)S(1)} %collective-permute-done.1), channel_id=1, source_target_pairs={{0,4},{16,28},{32,36},{48,60},{64,68},{80,92},{96,100},{112,124},{... | collective-permute-start | bytes 786440 | tf_op jit(solution)/shard_map/ppermute | solution.py:46
  5.4 7.6 %collective-permute-start.3 = (bf16[4,128,256]{2,1,0:T(8,128)(2,1)S(1)}, bf16[4,128,256]{2,1,0:T(8,128)(2,1)S(1)}, u32[]{:S(2)}, u32[]{:S(2)}) collective-permute-start(bf16[4,128,256]{2,1,0:T(8,128)(2,1)S(1)} %collective-permute-done.1), channel_id=1, source_target_pairs={{0,1},{16,19},{32,33},{48,51},{64,65},{80,83},{96,97},{112,115},{1... | collective-permute-start | bytes 786440 | tf_op jit(solution)/shard_map/ppermute | solution.py:46
  9.7 7.6 %collective-permute-start.7 = (bf16[4,128,256]{2,1,0:T(8,128)(2,1)S(1)}, bf16[4,128,256]{2,1,0:T(8,128)(2,1)S(1)}, u32[]{:S(2)}, u32[]{:S(2)}) collective-permute-start(bf16[4,128,256]{2,1,0:T(8,128)(2,1)S(1)} %collective-permute-done.4.refs_4_.refs_6_), channel_id=1, source_target_pairs={{0,1},{16,19},{32,33},{48,51},{64,65},{80,83},{96,97},{112,115},{1... | collective-permute-start | bytes 786440 | tf_op jit(solution)/shard_map/ppermute | solution.py:46
  10.1 7.2 %collective-permute-start.6 = (bf16[4,128,256]{2,1,0:T(8,128)(2,1)S(1)}, bf16[4,128,256]{2,1,0:T(8,128)(2,1)S(1)}, u32[]{:S(2)}, u32[]{:S(2)}) collective-permute-start(bf16[4,128,256]{2,1,0:T(8,128)(2,1)S(1)} %collective-permute-done.refs_2_), channel_id=1, source_target_pairs={{0,4},{16,28},{32,36},{48,60},{64,68},{80,92},{96,100},{112,124},{... | collective-permute-start | bytes 786440 | tf_op jit(solution)/shard_map/ppermute | solution.py:46
  13.1 8.1 %collective-permute-start.5 = (bf16[12,128,256]{2,1,0:T(8,128)(2,1)S(1)}, bf16[12,128,256]{2,1,0:T(8,128)(2,1)S(1)}, u32[]{:S(2)}, u32[]{:S(2)}) collective-permute-start(bf16[12,128,256]{2,1,0:T(8,128)(2,1)S(1)} %pad_maximum_fusion), channel_id=1, source_target_pairs={{0,16},{16,0},{32,48},{48,32},{64,80},{80,64},{96,112},{112,96},{1... | collective-permute-start | bytes 2359304 | tf_op jit(solution)/shard_map/ppermute | solution.py:50
  19.1 7.7 %collective-permute-start.12 = (bf16[4,128,256]{2,1,0:T(8,128)(2,1)S(1)}, bf16[4,128,256]{2,1,0:T(8,128)(2,1)S(1)}, u32[]{:S(2)}, u32[]{:S(2)}) collective-permute-start(bf16[4,128,256]{2,1,0:T(8,128)(2,1)S(1)} %pad_maximum_fusion.4), channel_id=1, source_target_pairs={{0,1},{16,19},{32,33},{48,51},{64,65},{80,83},{96,97},{112,115},{1... | collective-permute-start | bytes 786440 | tf_op jit(solution)/shard_map/ppermute | solution.py:46
  19.9 6.9 %collective-permute-start.11 = (bf16[4,128,256]{2,1,0:T(8,128)(2,1)S(1)}, bf16[4,128,256]{2,1,0:T(8,128)(2,1)S(1)}, u32[]{:S(2)}, u32[]{:S(2)}) collective-permute-start(bf16[4,128,256]{2,1,0:T(8,128)(2,1)S(1)} %pad_maximum_fusion.6), channel_id=1, source_target_pairs={{0,4},{16,28},{32,36},{48,60},{64,68},{80,92},{96,100},{112,124},{... | collective-permute-start | bytes 786440 | tf_op jit(solution)/shard_map/ppermute | solution.py:46
  21.3 11.0 %collective-permute-start.9 = (bf16[8,128,256]{2,1,0:T(8,128)(2,1)S(1)}, bf16[8,128,256]{2,1,0:T(8,128)(2,1)S(1)}, u32[]{:S(2)}, u32[]{:S(2)}) collective-permute-start(bf16[8,128,256]{2,1,0:T(8,128)(2,1)S(1)} %pad_maximum_fusion.3), channel_id=1, source_target_pairs={{0,1},{16,19},{32,33},{48,51},{64,65},{80,83},{96,97},{112,115},{1... | collective-permute-start | bytes 1572872 | tf_op jit(solution)/shard_map/ppermute | solution.py:46
  22.7 9.7 %collective-permute-start.8 = (bf16[8,128,256]{2,1,0:T(8,128)(2,1)S(1)}, bf16[8,128,256]{2,1,0:T(8,128)(2,1)S(1)}, u32[]{:S(2)}, u32[]{:S(2)}) collective-permute-start(bf16[8,128,256]{2,1,0:T(8,128)(2,1)S(1)} %pad_maximum_fusion.2), channel_id=1, source_target_pairs={{0,4},{16,28},{32,36},{48,60},{64,68},{80,92},{96,100},{112,124},{... | collective-permute-start | bytes 1572872 | tf_op jit(solution)/shard_map/ppermute | solution.py:46
  32.5 18.1 %collective-permute-start.13 = (bf16[12,128,256]{2,1,0:T(8,128)(2,1)S(1)}, bf16[12,128,256]{2,1,0:T(8,128)(2,1)S(1)}, u32[]{:S(2)}, u32[]{:S(2)}) collective-permute-start(bf16[12,128,256]{2,1,0:T(8,128)(2,1)S(1)} %pad_maximum_fusion.1), channel_id=1, source_target_pairs={{0,16},{16,0},{32,48},{48,32},{64,80},{80,64},{96,112},{112,96},{1... | collective-permute-start | bytes 2359304 | tf_op jit(solution)/shard_map/ppermute | solution.py:50
  39.3 12.6 %collective-permute-start.16 = (bf16[2,128,256]{2,1,0:T(8,128)(2,1)S(1)}, bf16[2,128,256]{2,1,0:T(8,128)(2,1)S(1)}, u32[]{:S(2)}, u32[]{:S(2)}) collective-permute-start(bf16[2,128,256]{2,1,0:T(8,128)(2,1)S(1)} %get-tuple-element.74), channel_id=1, source_target_pairs={{0,4},{16,28},{32,36},{48,60},{64,68},{80,92},{96,100},{112,124},{... | collective-permute-start | bytes 393224 | tf_op jit(solution)/shard_map/ppermute | solution.py:46
  41.8 10.2 %collective-permute-start.17 = (bf16[2,128,256]{2,1,0:T(8,128)(2,1)S(1)}, bf16[2,128,256]{2,1,0:T(8,128)(2,1)S(1)}, u32[]{:S(2)}, u32[]{:S(2)}) collective-permute-start(bf16[2,128,256]{2,1,0:T(8,128)(2,1)S(1)} %get-tuple-element.72), channel_id=1, source_target_pairs={{0,1},{16,19},{32,33},{48,51},{64,65},{80,83},{96,97},{112,115},{1... | collective-permute-start | bytes 393224 | tf_op jit(solution)/shard_map/ppermute | solution.py:46
  43.3 8.7 %collective-permute-start.14 = (bf16[4,128,256]{2,1,0:T(8,128)(2,1)S(1)}, bf16[4,128,256]{2,1,0:T(8,128)(2,1)S(1)}, u32[]{:S(2)}, u32[]{:S(2)}) collective-permute-start(bf16[4,128,256]{2,1,0:T(8,128)(2,1)S(1)} %get-tuple-element.70), channel_id=1, source_target_pairs={{0,4},{16,28},{32,36},{48,60},{64,68},{80,92},{96,100},{112,124},{... | collective-permute-start | bytes 786440 | tf_op jit(solution)/shard_map/ppermute | solution.py:46
  46.6 7.6 %collective-permute-start.15 = (bf16[4,128,256]{2,1,0:T(8,128)(2,1)S(1)}, bf16[4,128,256]{2,1,0:T(8,128)(2,1)S(1)}, u32[]{:S(2)}, u32[]{:S(2)}) collective-permute-start(bf16[4,128,256]{2,1,0:T(8,128)(2,1)S(1)} %get-tuple-element.68), channel_id=1, source_target_pairs={{0,1},{16,19},{32,33},{48,51},{64,65},{80,83},{96,97},{112,115},{1... | collective-permute-start | bytes 786440 | tf_op jit(solution)/shard_map/ppermute | solution.py:46
  55.2 4.5 %collective-permute-start.20 = (f32[128,512]{1,0:T(8,128)S(1)}, f32[128,512]{1,0:T(8,128)S(1)}, u32[]{:S(2)}, u32[]{:S(2)}) collective-permute-start(f32[128,512]{1,0:T(8,128)S(1)} %get-tuple-element.60), channel_id=1, source_target_pairs={{0,16},{16,0},{32,48},{48,32},{64,80},{80,64},{96,112},{112,96},{1... | collective-permute-start | bytes 786440 | tf_op jit(solution)/shard_map/ppermute | solution.py:50
  57.8 11.1 %collective-permute-start.23 = (f32[128,512]{1,0:T(8,128)S(1)}, f32[128,512]{1,0:T(8,128)S(1)}, u32[]{:S(2)}, u32[]{:S(2)}) collective-permute-start(f32[128,512]{1,0:T(8,128)S(1)} %bits_mm.27), channel_id=1, source_target_pairs={{0,16},{16,0},{32,48},{48,32},{64,80},{80,64},{96,112},{112,96},{1... | collective-permute-start | bytes 786440 | tf_op jit(solution)/shard_map/ppermute | solution.py:50
  59.5 9.9 %collective-permute-start.19 = (f32[128,512]{1,0:T(8,128)S(1)}, f32[128,512]{1,0:T(8,128)S(1)}, u32[]{:S(2)}, u32[]{:S(2)}) collective-permute-start(f32[128,512]{1,0:T(8,128)S(1)} %bits_mm.23), channel_id=1, source_target_pairs={{0,16},{16,0},{32,48},{48,32},{64,80},{80,64},{96,112},{112,96},{1... | collective-permute-start | bytes 786440 | tf_op jit(solution)/shard_map/ppermute | solution.py:50
  59.7 9.8 %collective-permute-start.21 = (f32[128,512]{1,0:T(8,128)S(1)}, f32[128,512]{1,0:T(8,128)S(1)}, u32[]{:S(2)}, u32[]{:S(2)}) collective-permute-start(f32[128,512]{1,0:T(8,128)S(1)} %add.13), channel_id=1, source_target_pairs={{0,32},{16,112},{32,64},{48,16},{64,96},{80,48},{96,0},{112,80},{1... | collective-permute-start | bytes 786440 | tf_op jit(solution)/shard_map/ppermute | solution.py:46
  64.2 9.3 %collective-permute-start.18 = (f32[128,512]{1,0:T(8,128)S(1)}, f32[128,512]{1,0:T(8,128)S(1)}, u32[]{:S(2)}, u32[]{:S(2)}) collective-permute-start(f32[128,512]{1,0:T(8,128)S(1)} %bits_mm.15), channel_id=1, source_target_pairs={{0,16},{16,0},{32,48},{48,32},{64,80},{80,64},{96,112},{112,96},{1... | collective-permute-start | bytes 786440 | tf_op jit(solution)/shard_map/ppermute | solution.py:50
  69.0 8.5 %collective-permute-start.24 = (f32[128,512]{1,0:T(8,128)S(1)}, f32[128,512]{1,0:T(8,128)S(1)}, u32[]{:S(2)}, u32[]{:S(2)}) collective-permute-start(f32[128,512]{1,0:T(8,128)S(1)} %add.15), channel_id=1, source_target_pairs={{0,96},{16,48},{32,0},{48,80},{64,32},{80,112},{96,64},{112,16},{1... | collective-permute-start | bytes 786440 | tf_op jit(solution)/shard_map/ppermute | solution.py:46
  69.5 9.0 %collective-permute-start.22 = (f32[128,512]{1,0:T(8,128)S(1)}, f32[128,512]{1,0:T(8,128)S(1)}, u32[]{:S(2)}, u32[]{:S(2)}) collective-permute-start(f32[128,512]{1,0:T(8,128)S(1)} %add_add_fusion), channel_id=1, source_target_pairs={{0,32},{16,112},{32,64},{48,16},{64,96},{80,48},{96,0},{112,80},{1... | collective-permute-start | bytes 786440 | tf_op jit(solution)/shard_map/ppermute | solution.py:46
  (1 other events, 1.6 us)
